TPU v7x, 32 devices: a whole 2x2x4 slice. The times are simulated.
32 devices in a mesh: grp: 4 (over y, x), inner: 8 (over z, core).
Axes of the slice: x: 2, y: 2, z: 4, core: 2. Of those that a mesh axis runs over, the one named last changes fastest.
Arguments:
- tokens: bfloat16 [32, 1024, 512], P(('grp', 'inner')), may hold values from -8 to 8
- cotangent: bfloat16 [32, 1024, 512], P(('grp', 'inner')), may hold values from -6 to 6
- mixer_gain: bfloat16 [512], P(('grp', 'inner')), may hold values from 0.5 to 1.5
- forget_weight: bfloat16 [512, 1024], P('grp', 'inner'), may hold values from -0.25 to 0.25
- input_gate_weight: bfloat16 [512, 1024], P('grp', 'inner'), may hold values from -0.25 to 0.25
- candidate_weight: bfloat16 [512, 1024], P('grp', 'inner'), may hold values from -0.25 to 0.25
- forget_bias: bfloat16 [1024], P(('grp', 'inner')), may hold values from -2 to 6
- input_bias: bfloat16 [1024], P(('grp', 'inner')), may hold values from -6 to 2
- output_weight: bfloat16 [1024, 512], P('grp', 'inner'), may hold values from -0.1875 to 0.1875
- feed_norm_gain: bfloat16 [512], P(('grp', 'inner')), may hold values from 0.5 to 1.5
- up_weight: bfloat16 [512, 2048], P('grp', 'inner'), may hold values from -0.25 to 0.25
- down_weight: bfloat16 [2048, 512], P('grp', 'inner'), may hold values from -0.125 to 0.125
- mixer_second: float32 [512], P(('grp', 'inner')), may hold values from 9830.4 to 39321.6
- forget_rows: float32 [512], P('grp'), may hold values from 3276.8 to 13107.2
- forget_columns: float32 [1024], P('inner'), may hold values from 3276.8 to 13107.2
- input_rows: float32 [512], P('grp'), may hold values from 3276.8 to 13107.2
- input_columns: float32 [1024], P('inner'), may hold values from 3276.8 to 13107.2
- candidate_rows: float32 [512], P('grp'), may hold values from 3276.8 to 13107.2
- candidate_columns: float32 [1024], P('inner'), may hold values from 3276.8 to 13107.2
- forget_second: float32 [1024], P(('grp', 'inner')), may hold values from 6553.6 to 26214.4
- input_second: float32 [1024], P(('grp', 'inner')), may hold values from 6553.6 to 26214.4
- output_rows: float32 [1024], P('grp'), may hold values from 16384 to 65536
- output_columns: float32 [512], P('inner'), may hold values from 16384 to 65536
- feed_second: float32 [512], P(('grp', 'inner')), may hold values from 11468.8 to 45875.2
- up_rows: float32 [512], P('grp'), may hold values from 3276.8 to 13107.2
- up_columns: float32 [2048], P('inner'), may hold values from 3276.8 to 13107.2
- down_rows: float32 [2048], P('grp'), may hold values from 11468.8 to 45875.2
- down_columns: float32 [512], P('inner'), may hold values from 11468.8 to 45875.2
Outputs:
- block_output: bfloat16 [32, 1024, 512], P(('grp', 'inner'))
- tokens_grad: bfloat16 [32, 1024, 512], P(('grp', 'inner'))
- mixer_gain_grad: float32 [512], P(('grp', 'inner'))
- forget_weight_grad: float32 [512, 1024], P('grp', 'inner')
- input_weight_grad: float32 [512, 1024], P('grp', 'inner')
- candidate_weight_grad: float32 [512, 1024], P('grp', 'inner')
- forget_bias_grad: float32 [1024], P(('grp', 'inner'))
- input_bias_grad: float32 [1024], P(('grp', 'inner'))
- output_weight_grad: float32 [1024, 512], P('grp', 'inner')
- feed_gain_grad: float32 [512], P(('grp', 'inner'))
- up_weight_grad: float32 [512, 2048], P('grp', 'inner')
- down_weight_grad: float32 [2048, 512], P('grp', 'inner')
- mixer_gain_new: float32 [512], P(('grp', 'inner'))
- forget_weight_new: float32 [512, 1024], P('grp', 'inner')
- input_weight_new: float32 [512, 1024], P('grp', 'inner')
- candidate_weight_new: float32 [512, 1024], P('grp', 'inner')
- forget_bias_new: float32 [1024], P(('grp', 'inner'))
- next_input_bias: float32 [1024], P(('grp', 'inner'))
- output_weight_new: float32 [1024, 512], P('grp', 'inner')
- feed_gain_new: float32 [512], P(('grp', 'inner'))
- up_weight_new: float32 [512, 2048], P('grp', 'inner')
- down_weight_new: float32 [2048, 512], P('grp', 'inner')
- mixer_second_new: float32 [512], P(('grp', 'inner'))
- forget_rows_new: float32 [512], P('grp')
- forget_columns_new: float32 [1024], P('inner')
- input_rows_new: float32 [512], P('grp')
- input_columns_new: float32 [1024], P('inner')
- candidate_rows_new: float32 [512], P('grp')
- candidate_columns_new: float32 [1024], P('inner')
- forget_second_new: float32 [1024], P(('grp', 'inner'))
- input_second_new: float32 [1024], P(('grp', 'inner'))
- output_rows_new: float32 [1024], P('grp')
- output_columns_new: float32 [512], P('inner')
- feed_second_new: float32 [512], P(('grp', 'inner'))
- up_rows_new: float32 [512], P('grp')
- up_columns_new: float32 [2048], P('inner')
- down_rows_new: float32 [2048], P('grp')
- down_columns_new: float32 [512], P('inner')
- update_norms: float32 [10], replicated
All inputs are finite; a program needn't handle non-finite values.
Results may differ from a plain program's by a relative error of at most 0.0065.
The roundings to bfloat16 on the way count: a program that leaves them out, or rounds other values in their place, can miss the bound.
Values may be sent and summed in bfloat16 or wider, within the bound.
A program may use at most 256 MiB of HBM per device.

v0:
```python
import jax
import jax.numpy as jnp
from jax import lax
from jax.sharding import PartitionSpec as P

EPS = 1e-06
TINY = 1e-30
CLIP = 0.01


def rms_norm(values, gain):
    return values * lax.rsqrt(jnp.mean(values * values, axis=-1, keepdims=True) + EPS) * gain


def log_value(candidate_preact):
    return jnp.where(
        candidate_preact >= 0,
        jnp.log(jnp.maximum(candidate_preact, 0.0) + 0.5),
        -jax.nn.softplus(-candidate_preact),
    )


def linear_combine(first, second):
    return (first[0] * second[0], second[0] * first[1] + second[1])


def mixer(pre_forget, pre_input, candidate_preact):
    gap = jax.nn.softplus(-pre_forget) - jax.nn.softplus(-pre_input)
    log_keep = -jax.nn.softplus(gap)
    log_admit = -jax.nn.softplus(-gap)
    keep = jnp.exp(log_keep)
    inflow = jnp.exp(log_admit + log_value(candidate_preact))
    _, state = lax.associative_scan(linear_combine, (keep, inflow), axis=1)
    return state


def gelu_exact(values):
    return jax.nn.gelu(values, approximate=False)


def matmul(left_operand, right_operand):
    return jnp.dot(left_operand, right_operand, preferred_element_type=jnp.float32)


def over_rows(left_operand, right_operand):
    return lax.dot_general(
        left_operand, right_operand, (((0,), (0,)), ((), ())), preferred_element_type=jnp.float32
    )


def by_transpose(left_operand, right_operand):
    return lax.dot_general(
        left_operand, right_operand, (((1,), (1,)), ((), ())), preferred_element_type=jnp.float32
    )


def body(
    tokens,
    cotangent,
    mixer_gain,
    forget_weight,
    input_gate_weight,
    candidate_weight,
    forget_bias,
    input_bias,
    output_weight,
    feed_norm_gain,
    up_weight,
    down_weight,
    mixer_second,
    forget_rows,
    forget_columns,
    input_rows,
    input_columns,
    candidate_rows,
    candidate_columns,
    forget_second,
    input_second,
    output_rows,
    output_columns,
    feed_second,
    up_rows,
    up_columns,
    down_rows,
    down_columns,
):
    groups = lax.axis_size("grp")
    inners = lax.axis_size("inner")
    seqs, length, width = tokens.shape
    inner_parts = (
        lax.all_gather(mixer_gain.reshape(1, -1), "inner", axis=1, tiled=True),
        lax.all_gather(forget_weight, "inner", axis=1, tiled=True),
        lax.all_gather(input_gate_weight, "inner", axis=1, tiled=True),
        lax.all_gather(candidate_weight, "inner", axis=1, tiled=True),
        lax.all_gather(forget_bias.reshape(1, -1), "inner", axis=1, tiled=True),
        lax.all_gather(input_bias.reshape(1, -1), "inner", axis=1, tiled=True),
        lax.all_gather(output_weight, "inner", axis=1, tiled=True),
        lax.all_gather(feed_norm_gain.reshape(1, -1), "inner", axis=1, tiled=True),
        lax.all_gather(up_weight, "inner", axis=1, tiled=True),
        lax.all_gather(down_weight, "inner", axis=1, tiled=True),
    )
    whole = (
        lax.all_gather(inner_parts[0], "grp", axis=0, tiled=True),
        lax.all_gather(inner_parts[1], "grp", axis=0, tiled=True),
        lax.all_gather(inner_parts[2], "grp", axis=0, tiled=True),
        lax.all_gather(inner_parts[3], "grp", axis=0, tiled=True),
        lax.all_gather(inner_parts[4], "grp", axis=0, tiled=True),
        lax.all_gather(inner_parts[5], "grp", axis=0, tiled=True),
        lax.all_gather(inner_parts[6], "grp", axis=0, tiled=True),
        lax.all_gather(inner_parts[7], "grp", axis=0, tiled=True),
        lax.all_gather(inner_parts[8], "grp", axis=0, tiled=True),
        lax.all_gather(inner_parts[9], "grp", axis=0, tiled=True),
    )
    gain_first = whole[0].reshape(-1).astype(jnp.float32)
    forget_full = whole[1]
    input_full = whole[2]
    cand_full = whole[3]
    fbias_full = whole[4].reshape(-1).astype(jnp.float32)
    ibias_full = whole[5].reshape(-1).astype(jnp.float32)
    output_full = whole[6]
    gain_second = whole[7].reshape(-1).astype(jnp.float32)
    upper_full = whole[8]
    lower_full = whole[9]
    hidden_width = forget_full.shape[1]
    flat = tokens.reshape(seqs * length, width).astype(jnp.float32)
    normed_in, pull_first = jax.vjp(rms_norm, flat, gain_first)
    mixer_in = normed_in.astype(jnp.bfloat16)
    pre_forget = matmul(mixer_in, forget_full) + fbias_full
    pre_input = matmul(mixer_in, input_full) + ibias_full
    candidate_preact = matmul(mixer_in, cand_full)
    state, pull_mixer = jax.vjp(
        mixer,
        pre_forget.reshape(seqs, length, hidden_width),
        pre_input.reshape(seqs, length, hidden_width),
        candidate_preact.reshape(seqs, length, hidden_width),
    )
    state_low = state.reshape(seqs * length, hidden_width).astype(jnp.bfloat16)
    resid = flat + matmul(state_low, output_full)
    normed_feed, pull_second = jax.vjp(rms_norm, resid, gain_second)
    feed_in = normed_feed.astype(jnp.bfloat16)
    up_pre = matmul(feed_in, upper_full)
    act_value, pull_gelu = jax.vjp(gelu_exact, up_pre)
    act = act_value.astype(jnp.bfloat16)
    block_output = (
        (resid + matmul(act, lower_full)).astype(jnp.bfloat16).reshape(seqs, length, width)
    )
    back_parts = (
        lax.all_gather(forget_weight, "inner", axis=1, tiled=True),
        lax.all_gather(input_gate_weight, "inner", axis=1, tiled=True),
        lax.all_gather(candidate_weight, "inner", axis=1, tiled=True),
        lax.all_gather(output_weight, "inner", axis=1, tiled=True),
        lax.all_gather(up_weight, "inner", axis=1, tiled=True),
        lax.all_gather(down_weight, "inner", axis=1, tiled=True),
    )
    back_whole = (
        lax.all_gather(back_parts[0], "grp", axis=0, tiled=True),
        lax.all_gather(back_parts[1], "grp", axis=0, tiled=True),
        lax.all_gather(back_parts[2], "grp", axis=0, tiled=True),
        lax.all_gather(back_parts[3], "grp", axis=0, tiled=True),
        lax.all_gather(back_parts[4], "grp", axis=0, tiled=True),
        lax.all_gather(back_parts[5], "grp", axis=0, tiled=True),
    )
    forget_back = back_whole[0]
    input_back = back_whole[1]
    cand_back = back_whole[2]
    output_back = back_whole[3]
    upper_back = back_whole[4]
    lower_back = back_whole[5]
    grad_flat = cotangent.reshape(seqs * length, width)
    down_term = over_rows(act, grad_flat)
    d_act = by_transpose(grad_flat, lower_back)
    (d_up,) = pull_gelu(d_act)
    d_up_low = d_up.astype(jnp.bfloat16)
    up_term = over_rows(feed_in, d_up_low)
    d_feed = by_transpose(d_up_low, upper_back)
    d_resid_norm, gain_second_term = pull_second(d_feed)
    d_resid = grad_flat.astype(jnp.float32) + d_resid_norm
    d_mixed = d_resid.astype(jnp.bfloat16)
    output_term = over_rows(state_low, d_mixed)
    d_state = by_transpose(d_mixed, output_back)
    d_forget, d_input, d_cand = pull_mixer(d_state.reshape(seqs, length, hidden_width))
    d_forget_low = d_forget.reshape(seqs * length, hidden_width).astype(jnp.bfloat16)
    d_input_low = d_input.reshape(seqs * length, hidden_width).astype(jnp.bfloat16)
    d_cand_low = d_cand.reshape(seqs * length, hidden_width).astype(jnp.bfloat16)
    fbias_term = jnp.sum(d_forget_low, axis=0, dtype=jnp.float32)
    ibias_term = jnp.sum(d_input_low, axis=0, dtype=jnp.float32)
    forget_term = over_rows(mixer_in, d_forget_low)
    input_term = over_rows(mixer_in, d_input_low)
    cand_term = over_rows(mixer_in, d_cand_low)
    d_in = (
        by_transpose(d_forget_low, forget_back)
        + by_transpose(d_input_low, input_back)
        + by_transpose(d_cand_low, cand_back)
    )
    d_flat_norm, gain_first_term = pull_first(d_in)
    tokens_grad = (d_resid + d_flat_norm).astype(jnp.bfloat16).reshape(seqs, length, width)
    part = (
        lax.psum_scatter(
            gain_first_term.reshape(groups, -1), "inner", scatter_dimension=1, tiled=True
        ),
        lax.psum_scatter(forget_term, "inner", scatter_dimension=1, tiled=True),
        lax.psum_scatter(input_term, "inner", scatter_dimension=1, tiled=True),
        lax.psum_scatter(cand_term, "inner", scatter_dimension=1, tiled=True),
        lax.psum_scatter(fbias_term.reshape(groups, -1), "inner", scatter_dimension=1, tiled=True),
        lax.psum_scatter(ibias_term.reshape(groups, -1), "inner", scatter_dimension=1, tiled=True),
        lax.psum_scatter(output_term, "inner", scatter_dimension=1, tiled=True),
        lax.psum_scatter(
            gain_second_term.reshape(groups, -1), "inner", scatter_dimension=1, tiled=True
        ),
        lax.psum_scatter(up_term, "inner", scatter_dimension=1, tiled=True),
        lax.psum_scatter(down_term, "inner", scatter_dimension=1, tiled=True),
    )
    mine = (
        lax.psum_scatter(part[0], "grp", scatter_dimension=0, tiled=True),
        lax.psum_scatter(part[1], "grp", scatter_dimension=0, tiled=True),
        lax.psum_scatter(part[2], "grp", scatter_dimension=0, tiled=True),
        lax.psum_scatter(part[3], "grp", scatter_dimension=0, tiled=True),
        lax.psum_scatter(part[4], "grp", scatter_dimension=0, tiled=True),
        lax.psum_scatter(part[5], "grp", scatter_dimension=0, tiled=True),
        lax.psum_scatter(part[6], "grp", scatter_dimension=0, tiled=True),
        lax.psum_scatter(part[7], "grp", scatter_dimension=0, tiled=True),
        lax.psum_scatter(part[8], "grp", scatter_dimension=0, tiled=True),
        lax.psum_scatter(part[9], "grp", scatter_dimension=0, tiled=True),
    )
    params = [
        mixer_gain,
        forget_weight,
        input_gate_weight,
        candidate_weight,
        forget_bias,
        input_bias,
        output_weight,
        feed_norm_gain,
        up_weight,
        down_weight,
    ]
    locals_f = [p.astype(jnp.float32) for p in params]
    grads = [
        mine[0].reshape(-1),
        mine[1],
        mine[2],
        mine[3],
        mine[4].reshape(-1),
        mine[5].reshape(-1),
        mine[6],
        mine[7].reshape(-1),
        mine[8],
        mine[9],
    ]
    matrix_slots = [1, 2, 3, 6, 8, 9]
    vector_slots = [0, 4, 5, 7]
    rows_old = [forget_rows, input_rows, candidate_rows, output_rows, up_rows, down_rows]
    columns_old = [
        forget_columns,
        input_columns,
        candidate_columns,
        output_columns,
        up_columns,
        down_columns,
    ]
    seconds_old = [mixer_second, forget_second, input_second, feed_second]
    counts = [params[k].size * groups * inners for k in range(10)]
    first_inner = (lax.axis_index("inner") == 0).astype(jnp.float32)
    scales = lax.psum(
        jnp.stack(
            [jnp.sum(w * w) for w in locals_f] + [jnp.sum(r) * first_inner for r in rows_old]
        ),
        ("grp", "inner"),
    )
    mats = [grads[k] for k in matrix_slots]
    row_parts = [jnp.sum(g * g, axis=1) for g in mats]
    column_parts = [jnp.sum(g * g, axis=0) for g in mats]
    row_totals = lax.psum(
        (row_parts[0], row_parts[1], row_parts[2], row_parts[3], row_parts[4], row_parts[5]),
        "inner",
    )
    column_totals = lax.psum(
        (
            column_parts[0],
            column_parts[1],
            column_parts[2],
            column_parts[3],
            column_parts[4],
            column_parts[5],
        ),
        "grp",
    )
    grand = lax.psum(jnp.stack([jnp.sum(v) for v in row_totals]), "grp")
    scaled_all = [None] * 10
    new_states = [None] * 16
    state_places = {1: (1, 2), 2: (3, 4), 3: (5, 6), 6: (9, 10), 8: (12, 13), 9: (14, 15)}
    second_places = {0: 0, 4: 7, 5: 8, 7: 11}
    for k in range(6):
        slot = matrix_slots[k]
        grad = mats[k]
        full_rows = grad.shape[0] * groups
        full_columns = grad.shape[1] * inners
        rows = 0.5 * rows_old[k] + 0.5 * (row_totals[k] / full_columns + TINY)
        columns = 0.5 * columns_old[k] + 0.5 * (column_totals[k] / full_rows + TINY)
        row_mean = 0.5 * scales[10 + k] / full_rows + 0.5 * (
            grand[k] / (full_rows * full_columns) + TINY
        )
        scaled_all[slot] = grad * lax.rsqrt(rows[:, None] * columns[None, :] / row_mean)
        new_states[state_places[slot][0]] = rows
        new_states[state_places[slot][1]] = columns
    for k in range(4):
        slot = vector_slots[k]
        grad = grads[slot]
        second = 0.5 * seconds_old[k] + 0.5 * (grad * grad + TINY)
        scaled_all[slot] = grad * lax.rsqrt(second)
        new_states[second_places[slot]] = second
    clip = lax.psum(jnp.stack([jnp.sum(s * s) for s in scaled_all]), ("grp", "inner"))
    count_array = jnp.array(counts, jnp.float32)
    update_norms = jnp.sqrt(clip / count_array)
    fresh = [
        locals_f[k]
        + -jnp.sqrt(scales[k] / counts[k]) * scaled_all[k] / jnp.maximum(CLIP, update_norms[k])
        for k in range(10)
    ]
    return (
        block_output,
        tokens_grad,
        grads[0],
        grads[1],
        grads[2],
        grads[3],
        grads[4],
        grads[5],
        grads[6],
        grads[7],
        grads[8],
        grads[9],
        fresh[0],
        fresh[1],
        fresh[2],
        fresh[3],
        fresh[4],
        fresh[5],
        fresh[6],
        fresh[7],
        fresh[8],
        fresh[9],
        new_states[0],
        new_states[1],
        new_states[2],
        new_states[3],
        new_states[4],
        new_states[5],
        new_states[6],
        new_states[7],
        new_states[8],
        new_states[9],
        new_states[10],
        new_states[11],
        new_states[12],
        new_states[13],
        new_states[14],
        new_states[15],
        update_norms,
    )


def solution(mesh):
    return jax.shard_map(
        body,
        mesh=mesh,
        in_specs=(
            P(("grp", "inner"), None, None),
            P(("grp", "inner"), None, None),
            P(("grp", "inner")),
            P("grp", "inner"),
            P("grp", "inner"),
            P("grp", "inner"),
            P(("grp", "inner")),
            P(("grp", "inner")),
            P("grp", "inner"),
            P(("grp", "inner")),
            P("grp", "inner"),
            P("grp", "inner"),
            P(("grp", "inner")),
            P("grp"),
            P("inner"),
            P("grp"),
            P("inner"),
            P("grp"),
            P("inner"),
            P(("grp", "inner")),
            P(("grp", "inner")),
            P("grp"),
            P("inner"),
            P(("grp", "inner")),
            P("grp"),
            P("inner"),
            P("grp"),
            P("inner"),
        ),
        out_specs=(
            P(("grp", "inner"), None, None),
            P(("grp", "inner"), None, None),
            P(("grp", "inner")),
            P("grp", "inner"),
            P("grp", "inner"),
            P("grp", "inner"),
            P(("grp", "inner")),
            P(("grp", "inner")),
            P("grp", "inner"),
            P(("grp", "inner")),
            P("grp", "inner"),
            P("grp", "inner"),
            P(("grp", "inner")),
            P("grp", "inner"),
            P("grp", "inner"),
            P("grp", "inner"),
            P(("grp", "inner")),
            P(("grp", "inner")),
            P("grp", "inner"),
            P(("grp", "inner")),
            P("grp", "inner"),
            P("grp", "inner"),
            P(("grp", "inner")),
            P("grp"),
            P("inner"),
            P("grp"),
            P("inner"),
            P("grp"),
            P("inner"),
            P(("grp", "inner")),
            P(("grp", "inner")),
            P("grp"),
            P("inner"),
            P(("grp", "inner")),
            P("grp"),
            P("inner"),
            P("grp"),
            P("inner"),
            P(),
        ),
        check_vma=False,
    )
```

profile of v0, /device:TPU:0, one launch (start us, length us, event | category | flops | bytes accessed | tf_op | source)
XLA Modules:
  0.0 1446.5 jit_solution(3870636916183454871)
XLA Ops:
  7.3 16.1 %all_gather.74 = bf16[128,1024]{1,0:T(8,128)(2,1)} all-gather(bf16[128,128]{1,0:T(8,128)(2,1)} %param.33), channel_id=1, replica_groups=mesh['grp'=4,'inner'=8] {'inner'}, dimensions={1}, use_global_device_ids=true | all-gather | bytes 294912 | tf_op jit(solution)/shard_map/all_gather | solution.py:92
  390.6 16.5 %pad.389 = f32[1,1024,1024]{2,1,0:T(8,128)} pad(f32[1,512,1024]{2,1,0:T(8,128)} %add.651, f32[]{:T(128)} %constant.172.clone.1), padding=0_0_0x1_0_1x0_0_0 | pad | bytes 6291460 | tf_op jit(solution)/shard_map/jvp()/pad | solution.py:33
  412.6 16.7 %pad.388 = f32[1,1024,1024]{2,1,0:T(8,128)} pad(f32[1,512,1024]{2,1,0:T(8,128)} %pad_maximum_fusion, f32[]{:T(128)} %constant.172.clone.1), padding=0_0_0x0_1_1x0_0_0 | pad | bytes 6291460 | tf_op jit(solution)/shard_map/jvp()/pad | solution.py:33
  440.5 24.5 %multiply_convert_fusion = (bf16[1024,2048]{1,0:T(8,128)(2,1)}, f32[1024,2048]{1,0:T(8,128)}, f32[1024,2048]{1,0:T(8,128)}) fusion(bf16[512,2048]{1,0:T(8,128)(2,1)} %all-gather.27.cloned.1.call-done, f32[1024,512]{0,1:T(8,128)} %get-tuple-element.347, f32[512]{0:T(512)} %bitcast.293, f32[1024]{0:T(1024)} %fusion.108), kind=kOutput, calls=%fused_computation.18 | convolution fusion | flops 2285371392 | bytes 25171968 | tf_op jit(solution)/shard_map/dot_general | solution.py:42
  644.5 16.8 %pad.455 = f32[1,1024,1024]{2,1,0:T(8,128)} pad(f32[1,512,1024]{2,1,0:T(8,128)} %copy-done.5, f32[]{:T(128)} %constant.172.clone.1), padding=0_0_0x1_0_1x0_0_0 | pad | bytes 6291460 | tf_op jit(solution)/shard_map/transpose(jvp())/pad | solution.py:33
  671.0 16.7 %pad.483 = f32[1,1024,1024]{2,1,0:T(8,128)} pad(f32[1,512,1024]{2,1,0:T(8,128)} %get-tuple-element.192, f32[]{:T(128)} %constant.172.clone.1), padding=0_0_0x1_0_1x0_0_0 | pad | bytes 6291460 | tf_op jit(solution)/shard_map/transpose(jvp())/pad | solution.py:33
  696.7 16.9 %pad.392 = f32[1,1024,1024]{2,1,0:T(8,128)} pad(f32[1,511,1024]{2,1,0:T(8,128)} %get-tuple-element.218, f32[]{:T(128)} %constant.172.clone.1), padding=0_0_0x2_1_1x0_0_0 | pad | bytes 6287364 | tf_op jit(solution)/shard_map/transpose(jvp())/pad | solution.py:33
  722.5 20.6 %convert_reduce_fusion = (f32[1024]{0:T(1024)S(1)}, bf16[1,1024,1024]{2,1,0:T(8,128)(2,1)}, f32[1,1024,1024]{2,1,0:T(8,128)S(1)}, f32[1,1024,1024]{2,1,0:T(8,128)}) fusion(f32[1024,1024]{1,0:T(8,128)} %get-tuple-element.343, f32[1024]{0:T(1024)S(1)} %bitcast.291, f32[1,1024,1024]{2,1,0:T(8,128)} %get-tuple-element.213, f32[1,1024,1024]{2,1,0:T(8,128)} %pad.484, ...), kind=kLoop, calls=%fused_computation.84 | loop fusion | flops 58719232 | bytes 48246784 | tf_op jit(solution)/shard_map/reduce_sum | solution.py:186
  798.3 22.9 %reduce-scatter.33.cloned.1.call-done = f32[512,128]{1,0:T(8,128)} async-done(((f32[512,1024]{1,0:T(8,128)}), f32[512,128]{1,0:T(8,128)}) %reduce-scatter.33.cloned.1.call-update) | async-done | bytes 262160 | tf_op jit(solution)/shard_map/reduce_scatter | solution.py:203
  821.3 36.7 %reduce-scatter.29.cloned.1.call-done = f32[512,128]{1,0:T(8,128)} async-done(((f32[512,1024]{1,0:T(8,128)}), f32[512,128]{1,0:T(8,128)}) %reduce-scatter.29.cloned.1.call-update) | async-done | bytes 262160 | tf_op jit(solution)/shard_map/reduce_scatter | solution.py:202
  858.1 36.5 %reduce-scatter.37.cloned.1.call-done = f32[1024,64]{0,1:T(8,128)} async-done(((f32[1024,512]{0,1:T(8,128)}), f32[1024,64]{0,1:T(8,128)}) %reduce-scatter.37.cloned.1.call-update) | async-done | bytes 262160 | tf_op jit(solution)/shard_map/reduce_scatter | solution.py:206
  894.7 51.1 %reduce-scatter.41.cloned.1.call-done = f32[512,256]{1,0:T(8,128)} async-done(((f32[512,2048]{1,0:T(8,128)}), f32[512,256]{1,0:T(8,128)}) %reduce-scatter.41.cloned.1.call-update) | async-done | bytes 524304 | tf_op jit(solution)/shard_map/reduce_scatter | solution.py:210
  950.1 46.0 %reduce-scatter.45.cloned.1.call-done = f32[2048,64]{0,1:T(8,128)} async-done(((f32[2048,512]{0,1:T(8,128)}), f32[2048,64]{0,1:T(8,128)}) %reduce-scatter.45.cloned.1.call-update) | async-done | bytes 524304 | tf_op jit(solution)/shard_map/reduce_scatter | solution.py:211
  1027.9 30.2 %reduce-scatter.55.cloned.1.call-done = f32[16,4]{1,0:T(8,128)} async-done(((f32[128,4]{1,0:T(8,128)}), f32[16,4]{1,0:T(8,128)}) %reduce-scatter.55.cloned.1.call-update) | async-done | bytes 272
  1058.8 30.2 %reduce-scatter.51.cloned.1.call-done = f32[32,4]{1,0:T(8,128)} async-done(((f32[256,4]{1,0:T(8,128)}), f32[32,4]{1,0:T(8,128)}) %reduce-scatter.51.cloned.1.call-update) | async-done | bytes 528
  1089.9 24.9 %reduce-scatter.27.cloned.1.call-done = f32[128,128]{1,0:T(8,128)} async-done(((f32[512,128]{1,0:T(8,128)}), f32[128,128]{1,0:T(8,128)}) %reduce-scatter.27.cloned.1.call-update) | async-done | bytes 65552 | tf_op jit(solution)/shard_map/reduce_scatter | solution.py:215
  1115.8 26.3 %reduce-scatter.35.cloned.1.call-done = f32[128,128]{1,0:T(8,128)} async-done(((f32[512,128]{1,0:T(8,128)}), f32[128,128]{1,0:T(8,128)}) %reduce-scatter.35.cloned.1.call-update) | async-done | bytes 65552 | tf_op jit(solution)/shard_map/reduce_scatter | solution.py:217
  1143.1 26.5 %reduce-scatter.31.cloned.1.call-done = f32[128,128]{1,0:T(8,128)} async-done(((f32[512,128]{1,0:T(8,128)}), f32[128,128]{1,0:T(8,128)}) %reduce-scatter.31.cloned.1.call-update) | async-done | bytes 65552 | tf_op jit(solution)/shard_map/reduce_scatter | solution.py:216
  1170.6 26.4 %reduce-scatter.39.cloned.1.call-done = f32[256,64]{0,1:T(8,128)} async-done(((f32[1024,64]{0,1:T(8,128)}), f32[256,64]{0,1:T(8,128)}) %reduce-scatter.39.cloned.1.call-update) | async-done | bytes 65552 | tf_op jit(solution)/shard_map/reduce_scatter | solution.py:220
  1198.1 27.3 %reduce-scatter.43.cloned.1.call-done = f32[128,256]{1,0:T(8,128)} async-done(((f32[512,256]{1,0:T(8,128)}), f32[128,256]{1,0:T(8,128)}) %reduce-scatter.43.cloned.1.call-update) | async-done | bytes 131088 | tf_op jit(solution)/shard_map/reduce_scatter | solution.py:222
  1226.4 27.1 %reduce-scatter.47.cloned.1.call-done = f32[512,64]{0,1:T(8,128)} async-done(((f32[2048,64]{0,1:T(8,128)}), f32[512,64]{0,1:T(8,128)}) %reduce-scatter.47.cloned.1.call-update) | async-done | bytes 131088 | tf_op jit(solution)/shard_map/reduce_scatter | solution.py:223
  1254.5 16.5 %all-reduce.103 = (f32[128]{0:T(128)S(1)}, f32[128]{0:T(128)S(1)}, f32[128]{0:T(128)S(1)}, f32[256]{0:T(256)S(1)}, f32[128]{0:T(128)S(1)}, /*index=5*/f32[512]{0:T(512)S(1)}) all-reduce(f32[128]{0:T(128)S(1)} %get-tuple-element.152, f32[128]{0:T(128)S(1)} %get-tuple-element.150, ...), channel_id=1, replica_groups=mesh['grp'=4,'inner'=8] {'inner'}, use_global_device_ids=true, to_apply=%region_47.49 | all-reduce | flops 1280 | bytes 10240 | tf_op jit(solution)/shard_map/psum | solution.py:273
  1287.5 37.7 %psum.105 = f32[16]{0:T(128)S(1)} all-reduce(f32[16]{0:T(128)S(1)} %stack.121), channel_id=1, replica_groups=mesh['grp'=4,'inner'=8] {'grp','inner'}, use_global_device_ids=true, to_apply=%region_44.46 | all-reduce | flops 16 | bytes 128 | tf_op jit(solution)/shard_map/psum | solution.py:264
  1376.4 40.5 %psum.119 = f32[10]{0:T(128)S(1)} all-reduce(f32[10]{0:T(128)S(1)} %stack.139), channel_id=1, replica_groups=mesh['grp'=4,'inner'=8] {'grp','inner'}, use_global_device_ids=true, to_apply=%region_86.88 | all-reduce | flops 10 | bytes 80 | tf_op jit(solution)/shard_map/psum | solution.py:312
  (814 shorter events, 750.9 us)
Async XLA Ops:
  7.3 143.9 %all-gather.19.cloned.1.call-start = ((), (), s32[]{:S(2)}) async-start(), calls=%async_computation.16 | async-start | bytes 1310720 | tf_op jit(solution)/shard_map/all_gather | solution.py:104
  23.5 132.3 %all-gather.21.cloned.1.call-start = ((), (), s32[]{:S(2)}) async-start(), calls=%async_computation.17 | async-start | bytes 1310720 | tf_op jit(solution)/shard_map/all_gather | solution.py:105
  37.8 130.9 %all-gather.23.cloned.1.call-start = ((), (), s32[]{:S(2)}) async-start(), calls=%async_computation.18 | async-start | bytes 1310720 | tf_op jit(solution)/shard_map/all_gather | solution.py:106
  52.2 382.6 %all-gather.25.cloned.1.call-start = ((), (), s32[]{:S(2)}) async-start(), calls=%async_computation.19 | async-start | bytes 1310720 | tf_op jit(solution)/shard_map/all_gather | solution.py:109
  67.8 372.7 %all-gather.27.cloned.1.call-start = ((), (), s32[]{:S(2)}) async-start(), calls=%async_computation.20 | async-start | bytes 2621440 | tf_op jit(solution)/shard_map/all_gather | solution.py:111
  83.9 381.1 %all-gather.29.cloned.1.call-start = ((), (), s32[]{:S(2)}) async-start(), calls=%async_computation.21 | async-start | bytes 2621440 | tf_op jit(solution)/shard_map/all_gather | solution.py:112
  100.0 697.8 %reduce-scatter.25.cloned.1.call-start = ((), (), s32[]{:S(2)}) async-start(), calls=%async_computation.22 | async-start | bytes 2359296 | tf_op jit(solution)/shard_map/reduce_scatter | solution.py:201
  751.2 70.0 %reduce-scatter.33.cloned.1.call-start = ((), (), s32[]{:S(2)}) async-start(), calls=%async_computation.26 | async-start | bytes 2359296 | tf_op jit(solution)/shard_map/reduce_scatter | solution.py:203
  762.9 95.1 %reduce-scatter.29.cloned.1.call-start = ((), (), s32[]{:S(2)}) async-start(), calls=%async_computation.24 | async-start | bytes 2359296 | tf_op jit(solution)/shard_map/reduce_scatter | solution.py:202
  767.6 127.0 %reduce-scatter.37.cloned.1.call-start = ((), (), s32[]{:S(2)}) async-start(), calls=%async_computation.28 | async-start | bytes 2359296 | tf_op jit(solution)/shard_map/reduce_scatter | solution.py:206
  771.9 173.9 %reduce-scatter.41.cloned.1.call-start = ((), (), s32[]{:S(2)}) async-start(), calls=%async_computation.30 | async-start | bytes 4718592 | tf_op jit(solution)/shard_map/reduce_scatter | solution.py:210
  779.3 216.9 %reduce-scatter.45.cloned.1.call-start = ((), (), s32[]{:S(2)}) async-start(), calls=%async_computation.32 | async-start | bytes 4718592 | tf_op jit(solution)/shard_map/reduce_scatter | solution.py:211
  787.1 240.0 %reduce-scatter.49.cloned.1.call-start = ((), (), s32[]{:S(2)}) async-start(), calls=%async_computation.34 | async-start | bytes 73728
  796.0 262.1 %reduce-scatter.55.cloned.1.call-start = ((), (), s32[]{:S(2)}) async-start(), calls=%async_computation.37 | async-start | bytes 73728
  796.8 292.3 %reduce-scatter.51.cloned.1.call-start = ((), (), s32[]{:S(2)}) async-start(), calls=%async_computation.35 | async-start | bytes 147456
  797.7 317.1 %reduce-scatter.27.cloned.1.call-start = ((), (), s32[]{:S(2)}) async-start(), calls=%async_computation.23 | async-start | bytes 327680 | tf_op jit(solution)/shard_map/reduce_scatter | solution.py:215
  798.3 343.8 %reduce-scatter.35.cloned.1.call-start = ((), (), s32[]{:S(2)}) async-start(), calls=%async_computation.27 | async-start | bytes 327680 | tf_op jit(solution)/shard_map/reduce_scatter | solution.py:217
  821.3 348.3 %reduce-scatter.31.cloned.1.call-start = ((), (), s32[]{:S(2)}) async-start(), calls=%async_computation.25 | async-start | bytes 327680 | tf_op jit(solution)/shard_map/reduce_scatter | solution.py:216
  858.1 339.0 %reduce-scatter.39.cloned.1.call-start = ((), (), s32[]{:S(2)}) async-start(), calls=%async_computation.29 | async-start | bytes 327680 | tf_op jit(solution)/shard_map/reduce_scatter | solution.py:220
  894.7 330.7 %reduce-scatter.43.cloned.1.call-start = ((), (), s32[]{:S(2)}) async-start(), calls=%async_computation.31 | async-start | bytes 655360 | tf_op jit(solution)/shard_map/reduce_scatter | solution.py:222
  945.8 307.7 %reduce-scatter.47.cloned.1.call-start = ((), (), s32[]{:S(2)}) async-start(), calls=%async_computation.33 | async-start | bytes 655360 | tf_op jit(solution)/shard_map/reduce_scatter | solution.py:223
  996.1 290.5 %reduce-scatter.53.cloned.1.call-start = ((), (), s32[]{:S(2)}) async-start(), calls=%async_computation.36 | async-start | bytes 147456
  1005.3 352.9 %copy-start.182 = (f32[16]{0:T(128)S(1)}, f32[16]{0:T(128)}, u32[]{:S(2)}) copy-start(f32[16]{0:T(128)} %param.53) | copy-start | bytes 196
  1005.3 411.6 %copy-start.199 = (f32[10]{0:T(128)S(1)}, f32[10]{0:T(128)}, u32[]{:S(2)}) copy-start(f32[10]{0:T(128)} %constant.418) | copy-start | bytes 124
  (201 other events, 12682.7 us)
Sparse Core Ops, SparseCore 0:
  23.6 26.3 all-gather.18
  51.8 26.6 all-gather.20
  80.3 26.6 all-gather.22
  108.7 26.5 all-gather.24
  136.9 35.2 all-gather.26
  173.9 35.1 all-gather.28
  751.3 33.1 reduce-scatter.24
  786.8 34.4 reduce-scatter.32
  823.6 34.4 reduce-scatter.28
  860.2 34.4 reduce-scatter.36
  897.0 48.7 reduce-scatter.40
  947.9 48.1 reduce-scatter.44
  998.9 28.1 reduce-scatter.48
  1029.8 28.1 reduce-scatter.54
  1060.7 28.3 reduce-scatter.50
  1092.5 22.2 reduce-scatter.26
  1117.9 24.0 reduce-scatter.34
  1145.5 24.0 reduce-scatter.30
  1172.9 24.0 reduce-scatter.38
  1200.5 24.7 reduce-scatter.42
  1228.7 24.7 reduce-scatter.46
  1256.4 30.2 reduce-scatter.52
where the time goes:
time: 1460 us; the launch traced here: 1450 us
  local copies, waits for them, and re-layouts  447 us (31%)
  waiting for transfers between devices  432 us (30%)
  blocking collectives  248 us (17%)
  other arithmetic  164 us (11%)
  matrix products  111 us (8%)
  between operations  43.9 us (3%)
    pad x79, local copies, waits for them, and re-layouts, mixer(): _, state = lax.associative_scan(linear_combine, (keep, inflow), axis=1)  213 us
    slice x78, local copies, waits for them, and re-layouts, mixer(): _, state = lax.associative_scan(linear_combine, (keep, inflow), axis=1)  187 us
    unnamed x26, waiting for transfers between devices  80 us
    dot_general x6, matrix products, matmul(): jnp.dot(left_operand, right_operand, preferred_element_type=jnp.float32)  63.5 us
    reduce_scatter x1, waiting for transfers between devices, body(): lax.psum_scatter(up_term, 'inner', scatter_dimension=1, tiled=True)  51.1 us
    reduce_scatter x1, waiting for transfers between devices, body(): lax.psum_scatter(down_term, 'inner', scatter_dimension=1, tiled=True)  46 us
    psum x1, blocking collectives, body(): lax.psum(jnp.stack([jnp.sum(s * s) for s in scaled_all]), ('grp', 'inner'))  40.5 us
    psum x1, blocking collectives, body(): lax.psum(jnp.stack([jnp.sum(w * w) for w in locals_f] + [jnp.sum(r) * fir...  37.7 us
  transfers between devices with their start and end apart: 22, of which 15 were waited for; matrix products, arithmetic and copies ran while one was open for 27% of the time, Pallas kernels for 0%

commit v1 on v0

--- a/solution.py
+++ b/solution.py
@@ -1,57 +1,460 @@
+import functools
+import math
 import jax
 import jax.numpy as jnp
 from jax import lax
+from jax.experimental import pallas as pl
 from jax.sharding import PartitionSpec as P
+from jax.experimental.pallas import tpu as pltpu
 
 EPS = 1e-06
+F32 = jnp.float32
+BF16 = jnp.bfloat16
+C = 256
+LANES = 128
+SUB = 8
+ERFC = (
+    0.2256758669, 0.2256693636, 0.2078460312, 0.1685204197, 0.1415057621,
+    -0.005753053848, 0.1692475449, -0.182997133, 0.05028532412,
+)
+
+
+def dot(a, b):
+    return jnp.dot(a, b, preferred_element_type=F32)
+
+
+def dot_t(a, b):
+    return lax.dot_general(a, b, (((1,), (1,)), ((), ())), preferred_element_type=F32)
+
+
+def loop(steps, body):
+    def run(i, carry):
+        body(i)
+        return carry
+
+    lax.fori_loop(0, steps, run, 0)
+
+
+def at(i, size):
+    return pl.ds(pl.multiple_of(i * size, size), size)
+
+
+def gelu_parts(x):
+    ax = jnp.abs(x)
+    e = jnp.exp(-0.5 * (x * x))
+    t = 1.0 / (1.0 + (0.4 * math.sqrt(0.5)) * ax)
+    poly = jnp.full_like(t, ERFC[-1])
+    for c in ERFC[-2::-1]:
+        poly = poly * t + c
+    half = 0.5 * (poly * t * e)
+    cdf = jnp.where(x >= 0, 1.0 - half, half)
+    return x * cdf, cdf + (x * e) * (1.0 / math.sqrt(2.0 * math.pi))
+
+
+def strided(ref, j, n):
+    return ref[pl.ds(j, SUB, stride=n), :]
+
+def gather_rows(tmp, j0, n, D):
+    columns = [
+        jnp.concatenate([tmp[q, pl.ds(j0 + jj, SUB, stride=n), :] for jj in range(16)], axis=0)
+        for q in range(D // LANES)
+    ]
+    return jnp.concatenate(columns, axis=1)
+
+
+def scatter_rows(tmp, j0, n, out):
+    for q in range(out.shape[1] // LANES):
+        for jj in range(16):
+            tmp[q, pl.ds(j0 + jj, SUB, stride=n), :] = out[
+                jj * SUB : (jj + 1) * SUB, q * LANES : (q + 1) * LANES
+            ]
+
+
+def norm_in(refs, T):
+    n = T // SUB
+    tmp, xf, g1 = refs.pre, refs.xf, refs.g1
+    D = xf.shape[1]
+
+    def widen(i):
+        rows = at(i, LANES)
+        wide = refs.tok[rows, :].astype(F32)
+        for q in range(D // LANES):
+            tmp[q, rows, :] = wide[:, q * LANES : (q + 1) * LANES]
+
+    loop(T // LANES, widen)
+
+    def place(i):
+        x = gather_rows(tmp, i * 16, n, D)
+        y = x * lax.rsqrt(jnp.mean(x * x, axis=-1, keepdims=True) + EPS) * g1[...]
+        rows = at(i, LANES)
+        xf[rows, :] = x
+        refs.min[rows, :] = y.astype(BF16)
+        refs.min_t[:, rows] = y.T.astype(BF16)
+
+    loop(T // LANES, place)
+
+
+def cot_in(refs, T):
+    n = T // SUB
+    tmp = refs.pre
+    D = refs.xf.shape[1]
+
+    def widen(i):
+        rows = at(i, LANES)
+        wide = refs.cot[rows, :].astype(F32)
+        for q in range(D // LANES):
+            tmp[q, rows, :] = wide[:, q * LANES : (q + 1) * LANES]
+
+    loop(T // LANES, widen)
+
+    def place(i):
+        x = gather_rows(tmp, i * 16, n, D)
+        rows = at(i, LANES)
+        refs.cot_p[rows, :] = x.astype(BF16)
+        refs.cot_t[:, rows] = x.T.astype(BF16)
+
+    loop(T // LANES, place)
+
+
+def mixer_forward(refs, z, T):
+    pre, ac, st = refs.pre, refs.buf_a, refs.st
+    halves = C // LANES
+    width = 3 * LANES
+
+    def project(i):
+        rows = at(i, 256)
+        out = dot(refs.min[rows, :], refs.wmix[z])
+        for q in range(3 * halves):
+            pre[q, rows, :] = out[:, q * LANES : (q + 1) * LANES]
+
+    loop(T // 256, project)
+    fb = refs.fb[z]
+    ib = refs.ib[z]
+
+    def gates(i, carry):
+        r0 = pl.multiple_of(i * 64, 64)
+        out = []
+        for h in range(halves):
+            a, b = carry[h]
+            lanes = slice(h * LANES, (h + 1) * LANES)
+            pf = pre[3 * h, pl.ds(r0, 64), :] + fb[:, lanes]
+            pi = pre[3 * h + 1, pl.ds(r0, 64), :] + ib[:, lanes]
+            pc = pre[3 * h + 2, pl.ds(r0, 64), :]
+            m = jnp.minimum(jnp.minimum(pf, pi), 0.0)
+            e0 = jnp.exp(m)
+            ef = jnp.exp(m - pf)
+            ei = jnp.exp(m - pi)
+            nk = e0 + ei
+            na = e0 + ef
+            inv = 1.0 / (nk + na)
+            keep = nk * inv
+            admit = na * inv
+            not_f = 1.0 / (1.0 + jnp.exp(pf))
+            not_i = 1.0 / (1.0 + jnp.exp(pi))
+            ec = jnp.exp(jnp.minimum(pc, 0.0))
+            sg = ec / (1.0 + ec)
+            positive = pc >= 0
+            value = jnp.where(positive, pc + 0.5, sg)
+            slope = jnp.where(positive, 1.0, sg * (1.0 - sg))
+            refs.keep[z, pl.ds(r0, 64), lanes] = keep
+            refs.k_f[z, pl.ds(r0, 64), lanes] = keep * not_f
+            refs.k_i[z, pl.ds(r0, 64), lanes] = keep * not_i
+            refs.k_c[z, pl.ds(r0, 64), lanes] = admit * slope
+            inflow = admit * value
+            alist, blist = [], []
+            for j in range(8):
+                kj = keep[j * SUB : (j + 1) * SUB]
+                b = kj * b + inflow[j * SUB : (j + 1) * SUB]
+                a = kj * a
+                alist.append(a)
+                blist.append(b)
+            ac[pl.ds(r0, 64), lanes] = jnp.concatenate(alist, axis=0)
+            st[z, pl.ds(r0 + SUB, 64), lanes] = jnp.concatenate(blist, axis=0)
+            out.append((a, b))
+        return tuple(out)
+
+    one = jnp.ones((SUB, LANES), F32)
+    zero = jnp.zeros((SUB, LANES), F32)
+    ends = lax.fori_loop(0, T // 64, gates, tuple((one, zero) for _ in range(halves)))
+    for h in range(halves):
+        a, b = ends[h]
+        rows = [jnp.zeros((1, LANES), F32)]
+        for s in range(SUB - 1):
+            rows.append(a[s : s + 1] * rows[-1] + b[s : s + 1])
+        st[z, 0:SUB, h * LANES : (h + 1) * LANES] = jnp.concatenate(rows, axis=0)
+    first = st[z, 0:SUB, :]
+
+    def finish(i):
+        r0 = pl.multiple_of(i * 64, 64)
+        a = ac[pl.ds(r0, 64), :].reshape(8, SUB, C)
+        b = st[z, pl.ds(r0 + SUB, 64), :].reshape(8, SUB, C)
+        s = (b + a * first[None]).reshape(64, C)
+        st[z, pl.ds(r0 + SUB, 64), :] = s
+        refs.slow[z, pl.ds(r0, 64), :] = s.astype(BF16)
+
+    loop(T // 64, finish)
+
+
+def mix_out(refs, T):
+    Z = refs.wot.shape[0]
+
+    def body(i):
+        rows = at(i, 256)
+        acc = refs.xf[rows, :]
+        for z in range(Z):
+            acc = acc + dot_t(refs.slow[z, rows, :], refs.wot[z])
+        refs.resid[rows, :] = acc
+        for k in range(2):
+            x = acc[k * LANES : (k + 1) * LANES]
+            y = x * lax.rsqrt(jnp.mean(x * x, axis=-1, keepdims=True) + EPS) * refs.g2[...]
+            sub = pl.ds(pl.multiple_of(i * 256 + k * LANES, LANES), LANES)
+            refs.fin[sub, :] = y.astype(BF16)
+            refs.fin_t[:, sub] = y.T.astype(BF16)
+
+    loop(T // 256, body)
+
+
+def feed(refs, f, T):
+    wup, wdt = refs.wup, refs.wdt
+
+    def body(i):
+        rows = at(i, 256)
+        refs.buf_a[rows, :] = dot(refs.fin[rows, :], wup[f])
+        refs.buf_b[rows, :] = dot(refs.cot_p[rows, :], wdt[f])
+        for k in range(4):
+            sub = pl.ds(pl.multiple_of(i * 256 + k * 64, 64), 64)
+            act, slope = gelu_parts(refs.buf_a[sub, :])
+            refs.act[sub, :] = act.astype(BF16)
+            refs.dup[sub, :] = (refs.buf_b[sub, :] * slope).astype(BF16)
+        refs.oacc[rows, :] += dot_t(refs.act[rows, :], wdt[f])
+        refs.dfe[rows, :] += dot_t(refs.dup[rows, :], wup[f])
+
+    loop(T // 256, body)
+
+
+def feed_back(refs, T):
+    n = T // SUB
+    tmp = refs.pre
+    D = refs.xf.shape[1]
+
+    def body(i, total):
+        rows = at(i, LANES)
+        x = refs.resid[rows, :]
+        df = refs.dfe[rows, :]
+        out = x + refs.oacc[rows, :]
+        scatter_rows(tmp, i * 16, n, out)
+        r = lax.rsqrt(jnp.mean(x * x, axis=-1, keepdims=True) + EPS)
+        nrm = x * r
+        dn = df * refs.g2[...]
+        mean = jnp.mean(dn * nrm, axis=-1, keepdims=True)
+        dres = refs.cot_p[rows, :].astype(F32) + r * (dn - nrm * mean)
+        refs.dfe[rows, :] = dres
+        refs.fin[rows, :] = dres.astype(BF16)
+        refs.fin_t[:, rows] = dres.T.astype(BF16)
+        return total + (df * nrm).reshape(16, SUB, D).sum(axis=0)
+
+    total = lax.fori_loop(0, T // LANES, body, jnp.zeros((SUB, D), F32))
+    refs.fgg[...] = jnp.sum(total, axis=0, keepdims=True)
+
+    def emit(i):
+        rows = at(i, LANES)
+        for q in range(D // LANES):
+            refs.block[rows, q * LANES : (q + 1) * LANES] = tmp[q, rows, :].astype(BF16)
+
+    loop(T // LANES, emit)
+
+
+def mixer_back(refs, z, T):
+    ds, dc, st = refs.buf_a, refs.buf_b, refs.st
+    halves = C // LANES
+    width = 3 * LANES
+
+    def project(i):
+        rows = at(i, 256)
+        ds[rows, :] = dot(refs.fin[rows, :], refs.wot[z])
+
+    loop(T // 256, project)
+    steps = T // 64
+
+    def local(i, carry):
+        r0 = pl.multiple_of((steps - 1 - i) * 64, 64)
+        d = ds[pl.ds(r0, 64), :]
+        k = refs.keep[z, pl.ds(r0, 64), :]
+        e, dk = carry
+        plist, dlist = [None] * 8, [None] * 8
+        for j in range(7, -1, -1):
+            kj = k[j * SUB : (j + 1) * SUB]
+            p = d[j * SUB : (j + 1) * SUB] + e
+            plist[j] = p
+            dlist[j] = dk
+            e = kj * p
+            dk = kj * dk
+        ds[pl.ds(r0, 64), :] = jnp.concatenate(plist, axis=0)
+        dc[pl.ds(r0, 64), :] = jnp.concatenate(dlist, axis=0)
+        return e, dk
+
+    e, dk = lax.fori_loop(0, steps, local, (jnp.zeros((SUB, C), F32), jnp.ones((SUB, C), F32)))
+    rows = [jnp.zeros((1, C), F32)]
+    for s in range(SUB - 1, 0, -1):
+        rows.insert(0, e[s : s + 1] + dk[s : s + 1] * rows[0])
+    tail = jnp.concatenate(rows, axis=0)
+
+    def grads(i, sums):
+        r0 = pl.multiple_of(i * 64, 64)
+        out = []
+        for h in range(halves):
+            lanes = slice(h * LANES, (h + 1) * LANES)
+            sub = pl.ds(r0, 64)
+            p0 = ds[sub, lanes].reshape(8, SUB, LANES)
+            d0 = dc[sub, lanes].reshape(8, SUB, LANES)
+            p = (p0 + d0 * tail[None, :, lanes]).reshape(64, LANES)
+            x = p * (st[z, pl.ds(r0 + SUB, 64), lanes] - st[z, sub, lanes])
+            df = -(refs.k_f[z, sub, lanes] * x)
+            di = refs.k_i[z, sub, lanes] * x
+            dcand = refs.k_c[z, sub, lanes] * p
+            df16 = df.astype(BF16)
+            di16 = di.astype(BF16)
+            refs.dpre[sub, h * width : h * width + LANES] = df16
+            refs.dpre[sub, h * width + LANES : h * width + 2 * LANES] = di16
+            refs.dpre[sub, h * width + 2 * LANES : h * width + 3 * LANES] = dcand.astype(BF16)
+            sf, si = sums[h]
+            out.append(
+                (
+                    sf + df16.astype(F32).reshape(8, SUB, LANES).sum(axis=0),
+                    si + di16.astype(F32).reshape(8, SUB, LANES).sum(axis=0),
+                )
+            )
+        return tuple(out)
+
+    zero = jnp.zeros((SUB, LANES), F32)
+    sums = lax.fori_loop(0, T // 64, grads, tuple((zero, zero) for _ in range(halves)))
+    for h in range(halves):
+        lanes = slice(h * LANES, (h + 1) * LANES)
+        refs.fbg[z, :, lanes] = jnp.sum(sums[h][0], axis=0, keepdims=True)
+        refs.ibg[z, :, lanes] = jnp.sum(sums[h][1], axis=0, keepdims=True)
+
+    def back(i):
+        rows = at(i, 256)
+        refs.oacc[rows, :] += dot_t(refs.dpre[rows, :], refs.wmix[z])
+
+    loop(T // 256, back)
+
+
+def norm_back(refs, T):
+    n = T // SUB
+    tmp = refs.pre
+    D = refs.xf.shape[1]
+
+    def body(i, total):
+        rows = at(i, LANES)
+        x = refs.xf[rows, :]
+        d_in = refs.oacc[rows, :]
+        r = lax.rsqrt(jnp.mean(x * x, axis=-1, keepdims=True) + EPS)
+        nrm = x * r
+        dn = d_in * refs.g1[...]
+        mean = jnp.mean(dn * nrm, axis=-1, keepdims=True)
+        out = refs.dfe[rows, :] + r * (dn - nrm * mean)
+        scatter_rows(tmp, i * 16, n, out)
+        return total + (d_in * nrm).reshape(16, SUB, D).sum(axis=0)
+
+    total = lax.fori_loop(0, T // LANES, body, jnp.zeros((SUB, D), F32))
+    refs.mgg[...] = jnp.sum(total, axis=0, keepdims=True)
+
+    def emit(i):
+        rows = at(i, LANES)
+        for q in range(D // LANES):
+            refs.tgrad[rows, q * LANES : (q + 1) * LANES] = tmp[q, rows, :].astype(BF16)
+
+    loop(T // LANES, emit)
+
+
+class Refs:
+    def __init__(self, args):
+        (
+            self.tok, self.cot, self.wmix, self.wot, self.wup, self.wdt, self.g1, self.g2, self.fb, self.ib,
+            self.block, self.tgrad, self.gmix, self.got, self.gup, self.gdt, self.fgg, self.mgg, self.fbg, self.ibg,
+            self.xf, self.min, self.min_t, self.fin, self.fin_t, self.cot_p, self.cot_t, self.resid, self.oacc, self.dfe,
+            self.pre, self.buf_a, self.buf_b, self.act, self.dup, self.dpre, self.slow, self.st, self.keep, self.k_f,
+            self.k_i, self.k_c, self.gst, self.gsem,
+        ) = args
+
+
+def layer_kernel(*args):
+    refs = Refs(args)
+    T, D = refs.tok.shape
+    Z = refs.wmix.shape[0]
+    F = refs.wup.shape[0]
+    gst, sem = refs.gst, refs.gsem
+    norm_in(refs, T)
+    loop(Z, lambda z: mixer_forward(refs, z, T))
+    mix_out(refs, T)
+    cot_in(refs, T)
+    refs.oacc[...] = jnp.zeros_like(refs.oacc)
+    refs.dfe[...] = jnp.zeros_like(refs.dfe)
+
+    def feed_step(f):
+        feed(refs, f, T)
+        gst[0, :, 0:C] = dot(refs.cot_t[...], refs.act[...])
+        gst[1, :, 0:C] = dot(refs.fin_t[...], refs.dup[...])
+        one = pltpu.make_async_copy(gst.at[0, :, 0:C], refs.gdt.at[f], sem.at[0])
+        two = pltpu.make_async_copy(gst.at[1, :, 0:C], refs.gup.at[f], sem.at[1])
+        one.start()
+        two.start()
+        one.wait()
+        two.wait()
+
+    loop(F, feed_step)
+    feed_back(refs, T)
+    refs.oacc[...] = jnp.zeros_like(refs.oacc)
+
+    def mixer_step(z):
+        gst[0, :, 0:C] = dot(refs.fin_t[...], refs.slow[z])
+        mixer_back(refs, z, T)
+        gst[1, :, :] = dot(refs.min_t[...], refs.dpre[...])
+        one = pltpu.make_async_copy(gst.at[0, :, 0:C], refs.got.at[z], sem.at[0])
+        two = pltpu.make_async_copy(gst.at[1], refs.gmix.at[z], sem.at[1])
+        one.start()
+        two.start()
+        one.wait()
+        two.wait()
+
+    loop(Z, mixer_step)
+    norm_back(refs, T)
+
+
+def layer(tok, cot, wmix, wot, wup, wdt, g1, g2, fb, ib):
+    T, D = tok.shape
+    Z, F = wmix.shape[0], wup.shape[0]
+    sds = jax.ShapeDtypeStruct
+    vm = pl.BlockSpec(memory_space=pltpu.VMEM)
+    anyspec = pl.BlockSpec(memory_space=pl.ANY)
+    out_shape = (
+        sds((T, D), BF16), sds((T, D), BF16),
+        sds((Z, D, 3 * C), F32), sds((Z, D, C), F32), sds((F, D, C), F32), sds((F, D, C), F32),
+        sds((1, D), F32), sds((1, D), F32), sds((Z, 1, C), F32), sds((Z, 1, C), F32),
+    )
+    V = pltpu.VMEM
+    scratch = [
+        V((T, D), F32), V((T, D), BF16), V((D, T), BF16), V((T, D), BF16), V((D, T), BF16),
+        V((T, D), BF16), V((D, T), BF16), V((T, D), F32), V((T, D), F32), V((T, D), F32),
+        V((3 * C // LANES, T, LANES), F32), V((T, C), F32), V((T, C), F32), V((T, C), BF16), V((T, C), BF16),
+        V((T, 3 * C), BF16), V((Z, T, C), BF16), V((Z, T + SUB, C), F32),
+        V((Z, T, C), F32), V((Z, T, C), F32), V((Z, T, C), F32), V((Z, T, C), F32),
+        V((2, D, 3 * C), F32), pltpu.SemaphoreType.DMA((2,)),
+    ]
+    return pl.pallas_call(
+        layer_kernel,
+        out_shape=out_shape,
+        in_specs=[vm] * 10,
+        out_specs=(vm, vm, anyspec, anyspec, anyspec, anyspec, vm, vm, vm, vm),
+        scratch_shapes=scratch,
+        compiler_params=pltpu.CompilerParams(vmem_limit_bytes=67043328),
+        name="layer",
+    )(tok, cot, wmix, wot, wup, wdt, g1, g2, fb, ib)
+
+
 TINY = 1e-30
 CLIP = 0.01
-
-
-def rms_norm(values, gain):
-    return values * lax.rsqrt(jnp.mean(values * values, axis=-1, keepdims=True) + EPS) * gain
-
-
-def log_value(candidate_preact):
-    return jnp.where(
-        candidate_preact >= 0,
-        jnp.log(jnp.maximum(candidate_preact, 0.0) + 0.5),
-        -jax.nn.softplus(-candidate_preact),
-    )
-
-
-def linear_combine(first, second):
-    return (first[0] * second[0], second[0] * first[1] + second[1])
-
-
-def mixer(pre_forget, pre_input, candidate_preact):
-    gap = jax.nn.softplus(-pre_forget) - jax.nn.softplus(-pre_input)
-    log_keep = -jax.nn.softplus(gap)
-    log_admit = -jax.nn.softplus(-gap)
-    keep = jnp.exp(log_keep)
-    inflow = jnp.exp(log_admit + log_value(candidate_preact))
-    _, state = lax.associative_scan(linear_combine, (keep, inflow), axis=1)
-    return state
-
-
-def gelu_exact(values):
-    return jax.nn.gelu(values, approximate=False)
-
-
-def matmul(left_operand, right_operand):
-    return jnp.dot(left_operand, right_operand, preferred_element_type=jnp.float32)
-
-
-def over_rows(left_operand, right_operand):
-    return lax.dot_general(
-        left_operand, right_operand, (((0,), (0,)), ((), ())), preferred_element_type=jnp.float32
-    )
-
-
-def by_transpose(left_operand, right_operand):
-    return lax.dot_general(
-        left_operand, right_operand, (((1,), (1,)), ((), ())), preferred_element_type=jnp.float32
-    )
 
 
 def body(
@@ -87,113 +490,41 @@
     groups = lax.axis_size("grp")
     inners = lax.axis_size("inner")
     seqs, length, width = tokens.shape
-    inner_parts = (
-        lax.all_gather(mixer_gain.reshape(1, -1), "inner", axis=1, tiled=True),
-        lax.all_gather(forget_weight, "inner", axis=1, tiled=True),
-        lax.all_gather(input_gate_weight, "inner", axis=1, tiled=True),
-        lax.all_gather(candidate_weight, "inner", axis=1, tiled=True),
-        lax.all_gather(forget_bias.reshape(1, -1), "inner", axis=1, tiled=True),
-        lax.all_gather(input_bias.reshape(1, -1), "inner", axis=1, tiled=True),
-        lax.all_gather(output_weight, "inner", axis=1, tiled=True),
-        lax.all_gather(feed_norm_gain.reshape(1, -1), "inner", axis=1, tiled=True),
-        lax.all_gather(up_weight, "inner", axis=1, tiled=True),
-        lax.all_gather(down_weight, "inner", axis=1, tiled=True),
-    )
-    whole = (
-        lax.all_gather(inner_parts[0], "grp", axis=0, tiled=True),
-        lax.all_gather(inner_parts[1], "grp", axis=0, tiled=True),
-        lax.all_gather(inner_parts[2], "grp", axis=0, tiled=True),
-        lax.all_gather(inner_parts[3], "grp", axis=0, tiled=True),
-        lax.all_gather(inner_parts[4], "grp", axis=0, tiled=True),
-        lax.all_gather(inner_parts[5], "grp", axis=0, tiled=True),
-        lax.all_gather(inner_parts[6], "grp", axis=0, tiled=True),
-        lax.all_gather(inner_parts[7], "grp", axis=0, tiled=True),
-        lax.all_gather(inner_parts[8], "grp", axis=0, tiled=True),
-        lax.all_gather(inner_parts[9], "grp", axis=0, tiled=True),
-    )
-    gain_first = whole[0].reshape(-1).astype(jnp.float32)
-    forget_full = whole[1]
-    input_full = whole[2]
-    cand_full = whole[3]
-    fbias_full = whole[4].reshape(-1).astype(jnp.float32)
-    ibias_full = whole[5].reshape(-1).astype(jnp.float32)
-    output_full = whole[6]
-    gain_second = whole[7].reshape(-1).astype(jnp.float32)
-    upper_full = whole[8]
-    lower_full = whole[9]
-    hidden_width = forget_full.shape[1]
-    flat = tokens.reshape(seqs * length, width).astype(jnp.float32)
-    normed_in, pull_first = jax.vjp(rms_norm, flat, gain_first)
-    mixer_in = normed_in.astype(jnp.bfloat16)
-    pre_forget = matmul(mixer_in, forget_full) + fbias_full
-    pre_input = matmul(mixer_in, input_full) + ibias_full
-    candidate_preact = matmul(mixer_in, cand_full)
-    state, pull_mixer = jax.vjp(
-        mixer,
-        pre_forget.reshape(seqs, length, hidden_width),
-        pre_input.reshape(seqs, length, hidden_width),
-        candidate_preact.reshape(seqs, length, hidden_width),
-    )
-    state_low = state.reshape(seqs * length, hidden_width).astype(jnp.bfloat16)
-    resid = flat + matmul(state_low, output_full)
-    normed_feed, pull_second = jax.vjp(rms_norm, resid, gain_second)
-    feed_in = normed_feed.astype(jnp.bfloat16)
-    up_pre = matmul(feed_in, upper_full)
-    act_value, pull_gelu = jax.vjp(gelu_exact, up_pre)
-    act = act_value.astype(jnp.bfloat16)
-    block_output = (
-        (resid + matmul(act, lower_full)).astype(jnp.bfloat16).reshape(seqs, length, width)
-    )
-    back_parts = (
-        lax.all_gather(forget_weight, "inner", axis=1, tiled=True),
-        lax.all_gather(input_gate_weight, "inner", axis=1, tiled=True),
-        lax.all_gather(candidate_weight, "inner", axis=1, tiled=True),
-        lax.all_gather(output_weight, "inner", axis=1, tiled=True),
-        lax.all_gather(up_weight, "inner", axis=1, tiled=True),
-        lax.all_gather(down_weight, "inner", axis=1, tiled=True),
-    )
-    back_whole = (
-        lax.all_gather(back_parts[0], "grp", axis=0, tiled=True),
-        lax.all_gather(back_parts[1], "grp", axis=0, tiled=True),
-        lax.all_gather(back_parts[2], "grp", axis=0, tiled=True),
-        lax.all_gather(back_parts[3], "grp", axis=0, tiled=True),
-        lax.all_gather(back_parts[4], "grp", axis=0, tiled=True),
-        lax.all_gather(back_parts[5], "grp", axis=0, tiled=True),
-    )
-    forget_back = back_whole[0]
-    input_back = back_whole[1]
-    cand_back = back_whole[2]
-    output_back = back_whole[3]
-    upper_back = back_whole[4]
-    lower_back = back_whole[5]
-    grad_flat = cotangent.reshape(seqs * length, width)
-    down_term = over_rows(act, grad_flat)
-    d_act = by_transpose(grad_flat, lower_back)
-    (d_up,) = pull_gelu(d_act)
-    d_up_low = d_up.astype(jnp.bfloat16)
-    up_term = over_rows(feed_in, d_up_low)
-    d_feed = by_transpose(d_up_low, upper_back)
-    d_resid_norm, gain_second_term = pull_second(d_feed)
-    d_resid = grad_flat.astype(jnp.float32) + d_resid_norm
-    d_mixed = d_resid.astype(jnp.bfloat16)
-    output_term = over_rows(state_low, d_mixed)
-    d_state = by_transpose(d_mixed, output_back)
-    d_forget, d_input, d_cand = pull_mixer(d_state.reshape(seqs, length, hidden_width))
-    d_forget_low = d_forget.reshape(seqs * length, hidden_width).astype(jnp.bfloat16)
-    d_input_low = d_input.reshape(seqs * length, hidden_width).astype(jnp.bfloat16)
-    d_cand_low = d_cand.reshape(seqs * length, hidden_width).astype(jnp.bfloat16)
-    fbias_term = jnp.sum(d_forget_low, axis=0, dtype=jnp.float32)
-    ibias_term = jnp.sum(d_input_low, axis=0, dtype=jnp.float32)
-    forget_term = over_rows(mixer_in, d_forget_low)
-    input_term = over_rows(mixer_in, d_input_low)
-    cand_term = over_rows(mixer_in, d_cand_low)
-    d_in = (
-        by_transpose(d_forget_low, forget_back)
-        + by_transpose(d_input_low, input_back)
-        + by_transpose(d_cand_low, cand_back)
-    )
-    d_flat_norm, gain_first_term = pull_first(d_in)
-    tokens_grad = (d_resid + d_flat_norm).astype(jnp.bfloat16).reshape(seqs, length, width)
+    def whole(w):
+        w = lax.all_gather(w, "inner", axis=1, tiled=True)
+        return lax.all_gather(w, "grp", axis=0, tiled=True)
+
+    hidden = forget_weight.shape[1] * inners
+    ff = up_weight.shape[1] * inners
+    Z, F = hidden // C, ff // C
+    gates = [
+        whole(w).reshape(width, Z, C // LANES, 1, LANES)
+        for w in (forget_weight, input_gate_weight, candidate_weight)
+    ]
+    wmix = jnp.concatenate(gates, axis=3).reshape(width, Z, 3 * C).transpose(1, 0, 2)
+    wot = whole(output_weight).reshape(Z, C, width).transpose(0, 2, 1)
+    wup = whole(up_weight).reshape(width, F, C).transpose(1, 0, 2)
+    wdt = whole(down_weight).reshape(F, C, width).transpose(0, 2, 1)
+    vec = lambda v: lax.all_gather(v, ("grp", "inner"), axis=0, tiled=True).astype(F32)
+    (
+        block_output, tokens_grad, gmix, got, gup, gdt, fgg, mgg, fbg, ibg
+    ) = layer(
+        tokens.reshape(length, width), cotangent.reshape(length, width),
+        wmix, wot, wup, wdt,
+        vec(mixer_gain).reshape(1, width), vec(feed_norm_gain).reshape(1, width),
+        vec(forget_bias).reshape(Z, 1, C), vec(input_bias).reshape(Z, 1, C),
+    )
+    block_output = block_output.reshape(tokens.shape)
+    tokens_grad = tokens_grad.reshape(tokens.shape)
+    split = gmix.transpose(1, 0, 2).reshape(width, Z, C // LANES, 3, LANES)
+    forget_term, input_term, cand_term = [
+        split[:, :, :, k].reshape(width, hidden) for k in range(3)
+    ]
+    output_term = got.transpose(0, 2, 1).reshape(hidden, width)
+    up_term = gup.transpose(1, 0, 2).reshape(width, ff)
+    down_term = gdt.transpose(0, 2, 1).reshape(ff, width)
+    gain_first_term, gain_second_term = mgg.reshape(-1), fgg.reshape(-1)
+    fbias_term, ibias_term = fbg.reshape(-1), ibg.reshape(-1)
     part = (
         lax.psum_scatter(
             gain_first_term.reshape(groups, -1), "inner", scatter_dimension=1, tiled=True

time: 1460 us -> 1030 us (0.71); the launches traced: 1450 us -> 1030 us
  local copies, waits for them, and re-layouts: 447 us -> 100 us
  other arithmetic: 164 us -> 39.8 us
  matrix products: 111 us -> 0 us
  Pallas kernels: 0 us -> 101 us
  waiting for transfers between devices: 432 us -> 511 us
    pad x79 -> x0, local copies, waits for them, and re-layouts: 213 us -> none  [mixer(): _, state = lax.associative_scan(linear_combine, (keep, inflow), axis=1)]
    slice x78 -> x1, local copies, waits for them, and re-layouts: 187 us -> 5.93 us  [body(): split[:, :, :, k].reshape(width, hidden)]
    dot_general x18 -> x0, matrix products: 111 us -> none  [the longest x6 63.5 us: matmul(): jnp.dot(left_operand, right_operand, preferred_element_type=jnp.float32)]
    pallas_call x0 -> x1, Pallas kernels: none -> 101 us  [layer(): pl.pallas_call(layer_kernel, out_shape=out_shape, in_specs=[vm] * 10, out...]
    unnamed x26 -> x28, waiting for transfers between devices: 80 us -> 172 us
    reduce_scatter x2 -> x0, waiting for transfers between devices: 82.5 us -> none  [the longest x1 46 us: body(): lax.psum_scatter(down_term, 'inner', scatter_dimension=1, tiled=True)]
    all_gather x6, waiting for transfers between devices: 0.01 us -> 49.8 us  [whole(): return lax.all_gather(w, 'grp', axis=0, tiled=True)]
    reduce_scatter x1, waiting for transfers between devices: 0.02 us -> 36.7 us  [body(): lax.psum_scatter(forget_term, 'inner', scatter_dimension=1, tiled=True)]
  transfers between devices with their start and end apart: 22 -> 22, of which waited for: 15 -> 18; matrix products, arithmetic and copies ran while one was open for 27% -> 8% of each run, Pallas kernels for 0% -> 0%
where the time goes in v1:
time: 1030 us
  waiting for transfers between devices  511 us (50%)
  blocking collectives  239 us (23%)
  Pallas kernels  101 us (10%)
  local copies, waits for them, and re-layouts  100 us (10%)
  between operations  40.1 us (4%)
  other arithmetic  39.8 us (4%)
    unnamed x28, waiting for transfers between devices  172 us
    pallas_call x1, Pallas kernels, layer(): pl.pallas_call(layer_kernel, out_shape=out_shape, in_specs=[vm] * 10, out...  101 us
    all_gather x6, blocking collectives, whole(): w = lax.all_gather(w, 'inner', axis=1, tiled=True)  89.7 us
    unnamed x2, blocking collectives  54.9 us
    all_gather x6, waiting for transfers between devices, whole(): return lax.all_gather(w, 'grp', axis=0, tiled=True)  49.8 us
    reduce_scatter x1, waiting for transfers between devices, body(): lax.psum_scatter(up_term, 'inner', scatter_dimension=1, tiled=True)  47.7 us
    psum x1, blocking collectives, body(): lax.psum(jnp.stack([jnp.sum(s * s) for s in scaled_all]), ('grp', 'inner'))  40.5 us
    psum x1, blocking collectives, body(): lax.psum(jnp.stack([jnp.sum(w * w) for w in locals_f] + [jnp.sum(r) * fir...  37.8 us
  transfers between devices with their start and end apart: 22, of which 18 were waited for; matrix products, arithmetic and copies ran while one was open for 8% of the time, Pallas kernels for 0%

profile of v1, /device:TPU:0, one launch (start us, length us, event | category | flops | bytes accessed | tf_op | source)
XLA Modules:
  0.0 1031.7 jit_solution(17039041799601563374)
XLA Ops:
  7.3 16.0 %all_gather.48 = bf16[128,1024]{1,0:T(8,128)(2,1)} all-gather(bf16[128,128]{1,0:T(8,128)(2,1)} %param.32), channel_id=1, replica_groups=mesh['grp'=4,'inner'=8] {'inner'}, dimensions={1}, use_global_device_ids=true | all-gather | bytes 294912 | tf_op jit(solution)/shard_map/all_gather | solution.py:494
  67.6 15.8 %all_gather.56 = bf16[128,2048]{0,1:T(8,128)(2,1)} all-gather(bf16[128,256]{0,1:T(8,128)(2,1)S(1)} %copy.106), channel_id=1, replica_groups=mesh['grp'=4,'inner'=8] {'inner'}, dimensions={1}, use_global_device_ids=true | all-gather | bytes 589824 | tf_op jit(solution)/shard_map/all_gather | solution.py:494
  100.5 39.0 %all-reduce.10 = (bf16[512]{0:T(512)(128)(2,1)S(1)}, bf16[512]{0:T(512)(128)(2,1)S(1)}, bf16[1024]{0:T(1024)(128)(2,1)S(1)}, bf16[1024]{0:T(1024)(128)(2,1)S(1)}) all-reduce(bf16[512]{0:T(512)(128)(2,1)S(1)} %dynamic-update-slice, bf16[512]{0:T(512)(128)(2,1)S(1)} %dynamic-update-slice.1, ...), channel_id=1, replica_groups=mesh['grp'=4,'inner'=8] {'grp','inner'}, use_global_device_ids=true, to_apply=%add | all-reduce | flops 3072 | bytes 12288
  156.2 16.6 %all-gather.15.cloned.1.call-done = bf16[512,2048]{0,1:T(8,128)(2,1)} async-done(((bf16[128,2048]{0,1:T(8,128)(2,1)}), bf16[512,2048]{0,1:T(8,128)(2,1)}) %all-gather.15.cloned.1.call-update) | async-done | bytes 2097168 | tf_op jit(solution)/shard_map/all_gather | solution.py:495
  176.7 33.1 %all-gather.17.cloned.1.call-done = bf16[2048,512]{1,0:T(8,128)(2,1)} async-done(((bf16[512,512]{1,0:T(8,128)(2,1)}), bf16[2048,512]{1,0:T(8,128)(2,1)}) %all-gather.17.cloned.1.call-update) | async-done | bytes 2097168 | tf_op jit(solution)/shard_map/all_gather | solution.py:495
  213.8 100.8 %layer.1 = (bf16[1024,512]{1,0:T(8,128)(2,1)}, bf16[1024,512]{1,0:T(8,128)(2,1)}, f32[4,512,768]{2,1,0:T(8,128)}, f32[4,512,256]{2,1,0:T(8,128)}, f32[8,512,256]...) custom-call(bf16[1024,512]{1,0:T(8,128)(2,1)} %bitcast.143, ...), custom_call_target="tpu_custom_call" | custom-call | tf_op jit(solution)/shard_map/layer/pallas_call | solution.py:445
  366.0 36.7 %reduce-scatter.33.cloned.1.call-done = f32[512,128]{1,0:T(8,128)} async-done(((f32[512,1024]{1,0:T(8,128)}), f32[512,128]{1,0:T(8,128)}) %reduce-scatter.33.cloned.1.call-update) | async-done | bytes 262160 | tf_op jit(solution)/shard_map/reduce_scatter | solution.py:533
  402.8 36.7 %reduce-scatter.29.cloned.1.call-done = f32[512,128]{1,0:T(8,128)} async-done(((f32[512,1024]{1,0:T(8,128)}), f32[512,128]{1,0:T(8,128)}) %reduce-scatter.29.cloned.1.call-update) | async-done | bytes 262160 | tf_op jit(solution)/shard_map/reduce_scatter | solution.py:532
  439.6 36.6 %reduce-scatter.55.cloned.1.call-done = f32[64,1024]{1,0:T(8,128)} async-done(((f32[512,1024]{1,0:T(8,128)}), f32[64,1024]{1,0:T(8,128)}) %reduce-scatter.55.cloned.1.call-update) | async-done | bytes 262160
  478.4 48.8 %reduce-scatter.59.cloned.1.call-done = f32[64,2048]{1,0:T(8,128)} async-done(((f32[512,2048]{1,0:T(8,128)}), f32[64,2048]{1,0:T(8,128)}) %reduce-scatter.59.cloned.1.call-update) | async-done | bytes 524304
  529.8 47.7 %reduce-scatter.43.cloned.1.call-done = f32[512,256]{0,1:T(8,128)} async-done(((f32[512,2048]{0,1:T(8,128)}), f32[512,256]{0,1:T(8,128)}) %reduce-scatter.43.cloned.1.call-update) | async-done | bytes 524304 | tf_op jit(solution)/shard_map/reduce_scatter | solution.py:541
  585.5 23.0 %reduce-scatter.49.cloned.1.call-done = f32[16,4]{1,0:T(8,128)} async-done(((f32[128,4]{1,0:T(8,128)}), f32[16,4]{1,0:T(8,128)}) %reduce-scatter.49.cloned.1.call-update) | async-done | bytes 272
  609.3 30.2 %reduce-scatter.57.cloned.1.call-done = f32[16,4]{1,0:T(8,128)} async-done(((f32[128,4]{1,0:T(8,128)}), f32[16,4]{1,0:T(8,128)}) %reduce-scatter.57.cloned.1.call-update) | async-done | bytes 272
  640.2 30.2 %reduce-scatter.51.cloned.1.call-done = f32[32,4]{1,0:T(8,128)} async-done(((f32[256,4]{1,0:T(8,128)}), f32[32,4]{1,0:T(8,128)}) %reduce-scatter.51.cloned.1.call-update) | async-done | bytes 528
  671.2 24.9 %reduce-scatter.39.cloned.1.call-done = f32[128,128]{1,0:T(8,128)} async-done(((f32[512,128]{1,0:T(8,128)}), f32[128,128]{1,0:T(8,128)}) %reduce-scatter.39.cloned.1.call-update) | async-done | bytes 65552 | tf_op jit(solution)/shard_map/reduce_scatter | solution.py:548
  697.0 26.3 %reduce-scatter.35.cloned.1.call-done = f32[128,128]{1,0:T(8,128)} async-done(((f32[512,128]{1,0:T(8,128)}), f32[128,128]{1,0:T(8,128)}) %reduce-scatter.35.cloned.1.call-update) | async-done | bytes 65552 | tf_op jit(solution)/shard_map/reduce_scatter | solution.py:547
  724.3 26.6 %reduce-scatter.31.cloned.1.call-done = f32[128,128]{1,0:T(8,128)} async-done(((f32[512,128]{1,0:T(8,128)}), f32[128,128]{1,0:T(8,128)}) %reduce-scatter.31.cloned.1.call-update) | async-done | bytes 65552 | tf_op jit(solution)/shard_map/reduce_scatter | solution.py:546
  751.9 26.7 %reduce-scatter.41.cloned.1.call-done = f32[256,64]{1,0:T(8,128)} async-done(((f32[1024,64]{1,0:T(8,128)}), f32[256,64]{1,0:T(8,128)}) %reduce-scatter.41.cloned.1.call-update) | async-done | bytes 65552 | tf_op jit(solution)/shard_map/reduce_scatter | solution.py:551
  779.6 29.7 %reduce-scatter.47.cloned.1.call-done = f32[512,64]{1,0:T(8,128)} async-done(((f32[2048,64]{1,0:T(8,128)}), f32[512,64]{1,0:T(8,128)}) %reduce-scatter.47.cloned.1.call-update) | async-done | bytes 131088 | tf_op jit(solution)/shard_map/reduce_scatter | solution.py:554
  810.4 26.4 %reduce-scatter.45.cloned.1.call-done = f32[128,256]{0,1:T(8,128)} async-done(((f32[512,256]{0,1:T(8,128)}), f32[128,256]{0,1:T(8,128)}) %reduce-scatter.45.cloned.1.call-update) | async-done | bytes 131088 | tf_op jit(solution)/shard_map/reduce_scatter | solution.py:553
  838.0 16.5 %all-reduce.8 = (f32[128]{0:T(128)S(1)}, f32[128]{0:T(128)S(1)}, f32[128]{0:T(128)S(1)}, f32[256]{0:T(256)S(1)}, f32[128]{0:T(128)S(1)}, /*index=5*/f32[512]{0:T(512)S(1)}) all-reduce(f32[128]{0:T(128)S(1)} %get-tuple-element.148, f32[128]{0:T(128)S(1)} %get-tuple-element.146, ...), channel_id=1, replica_groups=mesh['grp'=4,'inner'=8] {'inner'}, use_global_device_ids=true, to_apply=%region_39.0 | all-reduce | flops 1280 | bytes 10240 | tf_op jit(solution)/shard_map/psum | solution.py:604
  870.7 37.8 %psum.105 = f32[16]{0:T(128)S(1)} all-reduce(f32[16]{0:T(128)S(1)} %stack.121), channel_id=1, replica_groups=mesh['grp'=4,'inner'=8] {'grp','inner'}, use_global_device_ids=true, to_apply=%region_36.0 | all-reduce | flops 16 | bytes 128 | tf_op jit(solution)/shard_map/psum | solution.py:595
  913.2 15.9 %all-reduce.9 = (f32[4,16]{1,0:T(4,128)S(1)}, f32[4,32]{1,0:T(4,128)S(1)}, f32[4,32]{1,0:T(4,128)S(1)}, f32[4,16]{1,0:T(4,128)S(1)}, f32[6]{0:T(128)S(1)}, /*ind...) all-reduce(f32[4,16]{1,0:T(4,128)S(1)} %copy.127, ...), channel_id=3, replica_groups=mesh['grp'=4,'inner'=8] {'grp'}, use_global_device_ids=true, to_apply=%region_1.0.clone | all-reduce | flops 1158 | bytes 9264
  960.8 40.5 %psum.119 = f32[10]{0:T(128)S(1)} all-reduce(f32[10]{0:T(128)S(1)} %stack.139), channel_id=1, replica_groups=mesh['grp'=4,'inner'=8] {'grp','inner'}, use_global_device_ids=true, to_apply=%region_78.0 | all-reduce | flops 10 | bytes 80 | tf_op jit(solution)/shard_map/psum | solution.py:643
  (291 shorter events, 209.2 us)
Async XLA Ops:
  7.2 134.6 %all-gather.7.cloned.1.call-start = ((), (), s32[]{:S(2)}) async-start(), calls=%async_computation.16 | async-start | bytes 1310720 | tf_op jit(solution)/shard_map/all_gather | solution.py:495
  23.3 120.9 %all-gather.9.cloned.1.call-start = ((), (), s32[]{:S(2)}) async-start(), calls=%async_computation.17 | async-start | bytes 1310720 | tf_op jit(solution)/shard_map/all_gather | solution.py:495
  37.6 108.9 %all-gather.11.cloned.1.call-start = ((), (), s32[]{:S(2)}) async-start(), calls=%async_computation.18 | async-start | bytes 1310720 | tf_op jit(solution)/shard_map/all_gather | solution.py:495
  52.0 101.9 %all-gather.13.cloned.1.call-start = ((), (), s32[]{:S(2)}) async-start(), calls=%async_computation.19 | async-start | bytes 1310720 | tf_op jit(solution)/shard_map/all_gather | solution.py:495
  67.4 105.4 %all-gather.15.cloned.1.call-start = ((), (), s32[]{:S(2)}) async-start(), calls=%async_computation.20 | async-start | bytes 2621440 | tf_op jit(solution)/shard_map/all_gather | solution.py:495
  83.4 126.5 %all-gather.17.cloned.1.call-start = ((), (), s32[]{:S(2)}) async-start(), calls=%async_computation.21 | async-start | bytes 2621440 | tf_op jit(solution)/shard_map/all_gather | solution.py:495
  99.5 266.4 %reduce-scatter.37.cloned.1.call-start = ((), (), s32[]{:S(2)}) async-start(), calls=%async_computation.26 | async-start | bytes 2359296 | tf_op jit(solution)/shard_map/reduce_scatter | solution.py:534
  330.0 72.7 %reduce-scatter.33.cloned.1.call-start = ((), (), s32[]{:S(2)}) async-start(), calls=%async_computation.24 | async-start | bytes 2359296 | tf_op jit(solution)/shard_map/reduce_scatter | solution.py:533
  333.0 106.6 %reduce-scatter.29.cloned.1.call-start = ((), (), s32[]{:S(2)}) async-start(), calls=%async_computation.22 | async-start | bytes 2359296 | tf_op jit(solution)/shard_map/reduce_scatter | solution.py:532
  334.9 141.3 %reduce-scatter.55.cloned.1.call-start = ((), (), s32[]{:S(2)}) async-start(), calls=%async_computation.35 | async-start | bytes 2359296
  338.9 188.3 %reduce-scatter.59.cloned.1.call-start = ((), (), s32[]{:S(2)}) async-start(), calls=%async_computation.37 | async-start | bytes 4718592
  349.8 227.8 %reduce-scatter.43.cloned.1.call-start = ((), (), s32[]{:S(2)}) async-start(), calls=%async_computation.29 | async-start | bytes 4718592 | tf_op jit(solution)/shard_map/reduce_scatter | solution.py:541
  355.4 253.0 %reduce-scatter.49.cloned.1.call-start = ((), (), s32[]{:S(2)}) async-start(), calls=%async_computation.32 | async-start | bytes 73728
  356.9 282.6 %reduce-scatter.57.cloned.1.call-start = ((), (), s32[]{:S(2)}) async-start(), calls=%async_computation.36 | async-start | bytes 73728
  357.7 312.7 %reduce-scatter.51.cloned.1.call-start = ((), (), s32[]{:S(2)}) async-start(), calls=%async_computation.33 | async-start | bytes 147456
  358.6 337.5 %reduce-scatter.39.cloned.1.call-start = ((), (), s32[]{:S(2)}) async-start(), calls=%async_computation.27 | async-start | bytes 327680 | tf_op jit(solution)/shard_map/reduce_scatter | solution.py:548
  366.0 357.4 %reduce-scatter.35.cloned.1.call-start = ((), (), s32[]{:S(2)}) async-start(), calls=%async_computation.25 | async-start | bytes 327680 | tf_op jit(solution)/shard_map/reduce_scatter | solution.py:547
  402.7 348.2 %reduce-scatter.31.cloned.1.call-start = ((), (), s32[]{:S(2)}) async-start(), calls=%async_computation.23 | async-start | bytes 327680 | tf_op jit(solution)/shard_map/reduce_scatter | solution.py:546
  439.6 339.0 %reduce-scatter.41.cloned.1.call-start = ((), (), s32[]{:S(2)}) async-start(), calls=%async_computation.28 | async-start | bytes 655360 | tf_op jit(solution)/shard_map/reduce_scatter | solution.py:551
  478.3 330.9 %reduce-scatter.47.cloned.1.call-start = ((), (), s32[]{:S(2)}) async-start(), calls=%async_computation.31 | async-start | bytes 1310720 | tf_op jit(solution)/shard_map/reduce_scatter | solution.py:554
  529.7 412.0 %copy-start.50 = (f32[16]{0:T(128)S(1)}, f32[16]{0:T(128)}, u32[]{:S(2)}) copy-start(f32[16]{0:T(128)} %param.52) | copy-start | bytes 196
  529.7 471.7 %copy-start.64 = (f32[10]{0:T(128)S(1)}, f32[10]{0:T(128)}, u32[]{:S(2)}) copy-start(f32[10]{0:T(128)} %constant.148) | copy-start | bytes 124
  529.7 307.1 %reduce-scatter.45.cloned.1.call-start = ((), (), s32[]{:S(2)}) async-start(), calls=%async_computation.30 | async-start | bytes 655360 | tf_op jit(solution)/shard_map/reduce_scatter | solution.py:553
  577.5 292.4 %reduce-scatter.53.cloned.1.call-start = ((), (), s32[]{:S(2)}) async-start(), calls=%async_computation.34 | async-start | bytes 147456
  (64 other events, 10260.8 us)
Sparse Core Ops, SparseCore 0:
  23.4 26.3 all-gather.6
  51.6 26.6 all-gather.8
  80.1 26.7 all-gather.10
  108.7 27.0 all-gather.12
  137.4 35.3 all-gather.14
  174.5 35.3 all-gather.16
  330.1 35.7 reduce-scatter.36
  368.2 34.4 reduce-scatter.32
  405.0 34.4 reduce-scatter.28
  441.7 34.4 reduce-scatter.54
  478.5 48.6 reduce-scatter.58
  529.3 48.1 reduce-scatter.42
  580.3 28.1 reduce-scatter.48
  611.2 28.1 reduce-scatter.56
  642.1 28.2 reduce-scatter.50
  673.8 22.2 reduce-scatter.38
  699.3 24.0 reduce-scatter.34
  726.8 24.0 reduce-scatter.30
  753.7 24.7 reduce-scatter.40
  781.5 27.7 reduce-scatter.46
  812.1 24.7 reduce-scatter.44
  839.8 30.1 reduce-scatter.52

commit v2 on v1

--- a/solution.py
+++ b/solution.py
@@ -367,7 +367,6 @@
 
     loop(T // LANES, emit)
 
-
 class Refs:
     def __init__(self, args):
         (
@@ -452,9 +451,466 @@
         name="layer",
     )(tok, cot, wmix, wot, wup, wdt, g1, g2, fb, ib)
 
+MESH = pl.DeviceIdType.MESH
+
+
+def rcopy(src, dst, send, recv, device):
+    return pltpu.make_async_remote_copy(
+        src_ref=src, dst_ref=dst, send_sem=send, recv_sem=recv, device_id=device, device_id_type=MESH
+    )
+
+
+class Place:
+    def __init__(self):
+        self.g = lax.axis_index("grp")
+        self.i = lax.axis_index("inner")
+        self.y, self.x = self.g // 2, self.g % 2
+        self.z, self.c = self.i // 2, self.i % 2
+        self.me = self.g * 8 + self.i
+        self.partner = (self.g, self.z * 2 + 1 - self.c)
+
+    def flip(self, fx, fy):
+        x = (self.x + fx) % 2
+        y = (self.y + fy) % 2
+        return y * 2 + x
+
+    def near(self, z):
+        e = z % 2
+        return self.flip(1 - e, e)
+
+    def far(self, z):
+        e = z % 2
+        return self.flip(e, 1 - e)
+
+    def other(self, k):
+        t = (self.me + k) % 32
+        return (t // 8, t % 8)
+
+
+def entry_barrier(place):
+    barrier = pltpu.get_barrier_semaphore()
+
+    def greet(k):
+        pl.semaphore_signal(barrier, inc=1, device_id=place.other(k + 1), device_id_type=MESH)
+
+    loop(31, greet)
+    pl.semaphore_wait(barrier, 31)
+
+
+def spread(values, start, count, total):
+    lane = lax.broadcasted_iota(jnp.int32, (LANES, total), 1)
+    row = lax.broadcasted_iota(jnp.int32, (LANES, total), 0)
+    sel = jnp.where(row == start + lane % count, 1.0, 0.0).astype(BF16)
+    picked = dot(values, sel)
+    owner = lax.broadcasted_iota(jnp.int32, picked.shape, 0)
+    spot = lax.broadcasted_iota(jnp.int32, picked.shape, 1)
+    return jnp.sum(jnp.where(spot // count == owner, picked, 0.0), axis=0, keepdims=True)
+
+
+def pack_vectors(mg, fb, ib, fg):
+    parts = [mg, fb, ib, fg]
+    used = sum(p.shape[0] for p in parts)
+    rows = [p[...].astype(F32).reshape(1, p.shape[0]) for p in parts]
+    return jnp.concatenate(rows + [jnp.zeros((1, LANES - used), F32)], axis=1)
+
+
+def block_of(refs, a, g, i):
+    if a == 0:
+        return refs.wot.at[g, at(i, 64), :]
+    if a == 1:
+        return refs.wup.at[i, at(g, 128), :]
+    return refs.wdt.at[pl.ds(2 * g, 2), at(i, 64), :]
+
+
+def blocks_of(refs, a, i):
+    if a == 0:
+        return refs.wot.at[:, at(i, 64), :]
+    if a == 1:
+        return refs.wup.at[i]
+    return refs.wdt.at[:, at(i, 64), :]
+
+
+def mix_column(refs, z, c):
+    return refs.wmix.at[z, :, at(c, 384)]
+
+
+def gather_start(refs, p):
+    refs.o16[...] = refs.ow[...].astype(F32).T.astype(BF16)
+    refs.d16[...] = refs.dw[...].astype(F32).T.astype(BF16)
+    local = []
+    for k, w in enumerate((refs.fw, refs.iw, refs.cw)):
+        spot = pl.ds(pl.multiple_of(p.c * 384 + k * 128, 128), 128)
+        local.append(
+            pltpu.make_async_copy(w, refs.wmix.at[p.z, at(p.g, 128), spot], refs.loc_s.at[k])
+        )
+    local.append(pltpu.make_async_copy(refs.o16, block_of(refs, 0, p.g, p.i), refs.loc_s.at[3]))
+    local.append(pltpu.make_async_copy(refs.uw, block_of(refs, 1, p.g, p.i), refs.loc_s.at[4]))
+    for k in range(2):
+        local.append(
+            pltpu.make_async_copy(
+                refs.d16.at[:, k * 256 : (k + 1) * 256],
+                refs.wdt.at[2 * p.g + k, at(p.i, 64), :],
+                refs.loc_s.at[5 + k],
+            )
+        )
+    for c in local:
+        c.start()
+    row = pack_vectors(refs.mg, refs.fbv, refs.ibv, refs.fg)
+    refs.vstage[...] = row
+    refs.vecs[p.me] = row
+    entry_barrier(p)
+    for c in local[:3]:
+        c.wait()
+    own = refs.wmix.at[p.z, at(p.g, 128), at(p.c, 384)]
+    for k in range(1, 4):
+        peer = p.flip(k % 2, k // 2)
+        rcopy(own, own, refs.mxg_s.at[k - 1], refs.mxg_r.at[k - 1], (peer, p.i)).start()
+
+    def vector(k):
+        rcopy(refs.vstage, refs.vecs.at[p.me], refs.vec_s, refs.vec_r, p.other(k + 1)).start()
+
+    loop(31, vector)
+    for c in local[3:]:
+        c.wait()
+    for a in range(3):
+        blk = block_of(refs, a, p.g, p.i)
+        for k in range(1, 4):
+            peer = (p.g, ((p.z + k) % 4) * 2 + p.c)
+            rcopy(blk, blk, refs.ffz_s.at[a, k - 1], refs.ffz_r.at[a, p.z], peer).start()
+
+
+def gather_vectors(refs, p):
+    rows = refs.vecs.at[pl.ds(0, 31)]
+    rcopy(rows, rows, refs.vec_s, refs.vec_r, p.partner).wait()
+    v = refs.vecs[...].reshape(32, LANES).astype(BF16)
+    refs.g1[...] = spread(v, 0, 16, 512)
+    refs.g2[...] = spread(v, 80, 16, 512)
+    fb = spread(v, 16, 32, 1024)
+    ib = spread(v, 48, 32, 1024)
+    for z in range(4):
+        refs.fb[z] = fb[:, z * C : (z + 1) * C]
+        refs.ib[z] = ib[:, z * C : (z + 1) * C]
+
+
+def mix_exchange(refs, p, s):
+    def send_partner(z):
+        col = mix_column(refs, z, p.c)
+        rcopy(col, col, refs.mxp_s.at[z], refs.mxp_r.at[z], p.partner).start()
+
+    def wait_partner(z):
+        col = mix_column(refs, z, 1 - p.c)
+        rcopy(col, col, refs.mxp_s.at[z], refs.mxp_r.at[z], p.partner).wait_recv()
+
+    def send_up(z):
+        col = mix_column(refs, z, p.c)
+        rcopy(col, col, refs.mxu_s.at[z], refs.mxz_r.at[z], (p.g, p.i + 2)).start()
+
+    def send_down(z):
+        col = mix_column(refs, z, p.c)
+        rcopy(col, col, refs.mxd_s.at[z], refs.mxz_r.at[z], (p.g, p.i - 2)).start()
+
+    def wait_line(z):
+        col = mix_column(refs, z, p.c)
+        rcopy(col, col, refs.mxp_s.at[z], refs.mxz_r.at[z], p.partner).wait_recv()
+
+    @pl.when(s == 0)
+    def _():
+        for k in range(1, 4):
+            peer = p.flip(k % 2, k // 2)
+            blk = refs.wmix.at[p.z, at(peer, 128), at(p.c, 384)]
+            rcopy(blk, blk, refs.mxg_s.at[k - 1], refs.mxg_r.at[k - 1], (peer, p.i)).wait()
+
+        @pl.when(p.z < 3)
+        def _():
+            send_up(p.z)
+
+        @pl.when(p.z > 0)
+        def _():
+            send_down(p.z)
+
+        send_partner(p.z)
+        wait_partner(p.z)
+
+    below, above = p.z - s, p.z + s
+
+    @pl.when((s > 0) & (below >= 0))
+    def _():
+        wait_line(below)
+
+        @pl.when(p.z < 3)
+        def _():
+            send_up(below)
+
+        send_partner(below)
+
+    @pl.when((s > 0) & (above < 4))
+    def _():
+        wait_line(above)
+
+        @pl.when(p.z > 0)
+        def _():
+            send_down(above)
+
+        send_partner(above)
+
+    @pl.when((s > 0) & (below >= 0))
+    def _():
+        wait_partner(below)
+
+    @pl.when((s > 0) & (above < 4))
+    def _():
+        wait_partner(above)
+
+
+def mix_drain(refs, p):
+    for z in range(4):
+        col = mix_column(refs, z, p.c)
+        rcopy(col, col, refs.mxp_s.at[z], refs.mxp_r.at[z], p.partner).wait_send()
+
+        @pl.when((z <= p.z) & (p.z < 3))
+        def _():
+            rcopy(col, col, refs.mxu_s.at[z], refs.mxz_r.at[z], p.partner).wait_send()
+
+        @pl.when((z >= p.z) & (p.z > 0))
+        def _():
+            rcopy(col, col, refs.mxd_s.at[z], refs.mxz_r.at[z], p.partner).wait_send()
+
+
+def feed_second(refs, p):
+    for a in range(3):
+        for z in range(4):
+            blk = block_of(refs, a, p.g, z * 2 + p.c)
+
+            @pl.when(p.z != z)
+            def _():
+                rcopy(blk, blk, refs.ffp_s.at[a, z], refs.ffz_r.at[a, z], p.partner).wait_recv()
+
+            rcopy(blk, blk, refs.ff2_s.at[a, z], refs.ff2_r.at[a, z], (p.near(z), p.i)).start()
+
+
+def feed_third(refs, p):
+    for a in range(3):
+        for z in range(4):
+            mine = block_of(refs, a, p.g, z * 2 + p.c)
+            near = block_of(refs, a, p.near(z), z * 2 + p.c)
+            far = (p.far(z), p.i)
+            rcopy(near, near, refs.ff2_s.at[a, z], refs.ff2_r.at[a, z], (p.near(z), p.i)).wait_recv()
+            rcopy(mine, mine, refs.ff3_s.at[a, z, 0], refs.ff3_r.at[a, z, 0], far).start()
+            rcopy(near, near, refs.ff3_s.at[a, z, 1], refs.ff3_r.at[a, z, 1], far).start()
+
+
+def feed_fourth(refs, p):
+    for a in range(3):
+        for z in range(4):
+            blk = block_of(refs, a, p.g, z * 2 + p.c)
+            far = (p.far(z), p.i)
+            for k in range(2):
+                rcopy(blk, blk, refs.ff3_s.at[a, z, k], refs.ff3_r.at[a, z, k], far).wait_recv()
+            full = blocks_of(refs, a, z * 2 + p.c)
+            rcopy(full, full, refs.ffp_s.at[a, z], refs.ffp_r.at[a, z], p.partner).start()
+
+
+def feed_last(refs, p):
+    for a in range(3):
+        for z in range(4):
+            full = blocks_of(refs, a, z * 2 + 1 - p.c)
+            rcopy(full, full, refs.ffp_s.at[a, z], refs.ffp_r.at[a, z], p.partner).wait_recv()
+
+
+def feed_drain(refs, p):
+    for a in range(3):
+        for k in range(1, 4):
+            blk = block_of(refs, a, p.g, p.i)
+            rcopy(blk, blk, refs.ffz_s.at[a, k - 1], refs.ffz_r.at[a, p.z], p.partner).wait_send()
+        for z in range(4):
+            blk = block_of(refs, a, p.g, z * 2 + p.c)
+            rcopy(blk, blk, refs.ff2_s.at[a, z], refs.ff2_r.at[a, z], p.partner).wait_send()
+            for k in range(2):
+                rcopy(blk, blk, refs.ff3_s.at[a, z, k], refs.ff3_r.at[a, z, k], p.partner).wait_send()
+            full = blocks_of(refs, a, z * 2 + p.c)
+            rcopy(full, full, refs.ffp_s.at[a, z], refs.ffp_r.at[a, z], p.partner).wait_send()
+
+
+def slot_chunk(p, s):
+    low = jnp.minimum(p.z, 3 - p.z)
+    shift = jnp.where(s == 0, 1, jnp.where(s == 1, -1, 0))
+    m = s + low * shift
+    return jnp.where(p.z < 2, m, 3 - m)
+
+
+def mixer_slots(refs, p, T):
+    def slot(s):
+        mix_exchange(refs, p, s)
+        mixer_forward(refs, slot_chunk(p, s), T)
+
+        @pl.when(s == 0)
+        def _():
+            feed_second(refs, p)
+
+        @pl.when(s == 1)
+        def _():
+            feed_third(refs, p)
+
+        @pl.when(s == 2)
+        def _():
+            feed_fourth(refs, p)
+
+    loop(4, slot)
+    mix_drain(refs, p)
+    feed_last(refs, p)
+    feed_drain(refs, p)
+
+class GatherRefs:
+    def __init__(self, args):
+        (
+            self.tok, self.cot, self.fw, self.iw, self.cw, self.ow, self.uw, self.dw,
+            self.mg, self.fbv, self.ibv, self.fg,
+            self.block, self.tgrad, self.gmix, self.got, self.gup, self.gdt,
+            self.fgg, self.mgg, self.fbg, self.ibg,
+            self.wmix, self.wot, self.wup, self.wdt, self.g1, self.g2, self.fb, self.ib,
+            self.vecs, self.vstage, self.o16, self.d16,
+            self.xf, self.min, self.min_t, self.fin, self.fin_t, self.cot_p, self.cot_t,
+            self.resid, self.oacc, self.dfe,
+            self.pre, self.buf_a, self.buf_b, self.act, self.dup, self.dpre,
+            self.slow, self.st, self.keep, self.k_f, self.k_i, self.k_c, self.gsem,
+            self.loc_s, self.mxg_s, self.mxg_r, self.mxu_s, self.mxd_s, self.mxz_r,
+            self.mxp_s, self.mxp_r, self.vec_s, self.vec_r, self.ffz_s, self.ffz_r,
+            self.ff2_s, self.ff2_r, self.ff3_s, self.ff3_r, self.ffp_s, self.ffp_r,
+        ) = args
+
+
+def grad_slot(refs, k, D):
+    return refs.pre.at[:, k * D : (k + 1) * D, :]
+
+
+def put_grad(refs, k, value):
+    D = value.shape[0]
+    for q in range(value.shape[1] // LANES):
+        refs.pre[q, k * D : (k + 1) * D, :] = value[:, q * LANES : (q + 1) * LANES]
+
+
+def send_grad(refs, k, D, width, out, sem):
+    return [
+        pltpu.make_async_copy(
+            refs.pre.at[q, k * D : (k + 1) * D, :],
+            out.at[:, q * LANES : (q + 1) * LANES],
+            sem.at[q],
+        )
+        for q in range(width // LANES)
+    ]
+
+
+def layer_ag_kernel(*args):
+    refs = GatherRefs(args)
+    T, D = refs.tok.shape
+    Z = refs.wmix.shape[0]
+    F = refs.wup.shape[0]
+    p = Place()
+    gather_start(refs, p)
+    cot_in(refs, T)
+    gather_vectors(refs, p)
+    norm_in(refs, T)
+    mixer_slots(refs, p, T)
+    mix_out(refs, T)
+    refs.oacc[...] = jnp.zeros_like(refs.oacc)
+    refs.dfe[...] = jnp.zeros_like(refs.dfe)
+
+    def feed_step(f):
+        feed(refs, f, T)
+        put_grad(refs, 0, dot(refs.cot_t[...], refs.act[...]))
+        put_grad(refs, 1, dot(refs.fin_t[...], refs.dup[...]))
+        copies = send_grad(refs, 0, D, C, refs.gdt.at[f], refs.gsem.at[0])
+        copies += send_grad(refs, 1, D, C, refs.gup.at[f], refs.gsem.at[1])
+        for c in copies:
+            c.start()
+        for c in copies:
+            c.wait()
+
+    loop(F, feed_step)
+    feed_back(refs, T)
+    refs.oacc[...] = jnp.zeros_like(refs.oacc)
+
+    def mixer_step(z):
+        put_grad(refs, 0, dot(refs.fin_t[...], refs.slow[z]))
+        mixer_back(refs, z, T)
+        put_grad(refs, 1, dot(refs.min_t[...], refs.dpre[...]))
+        copies = send_grad(refs, 0, D, C, refs.got.at[z], refs.gsem.at[0])
+        copies += send_grad(refs, 1, D, 3 * C, refs.gmix.at[z], refs.gsem.at[1])
+        for c in copies:
+            c.start()
+        for c in copies:
+            c.wait()
+
+    loop(Z, mixer_step)
+    norm_back(refs, T)
+
+
+def layer_ag(tok, cot, fw, iw, cw, ow, uw, dw, mg, fb, ib, fg):
+    T, D = tok.shape
+    Z, F = 4, 8
+    sds = jax.ShapeDtypeStruct
+    vm = pl.BlockSpec(memory_space=pltpu.VMEM)
+    anyspec = pl.BlockSpec(memory_space=pl.ANY)
+    out_shape = (
+        sds((T, D), BF16), sds((T, D), BF16),
+        sds((Z, D, 3 * C), F32), sds((Z, D, C), F32), sds((F, D, C), F32), sds((F, D, C), F32),
+        sds((1, D), F32), sds((1, D), F32), sds((Z, 1, C), F32), sds((Z, 1, C), F32),
+    )
+    V = pltpu.VMEM
+    S = pltpu.SemaphoreType.DMA
+    scratch = [
+        V((Z, D, 3 * C), BF16), V((Z, D, C), BF16), V((F, D, C), BF16), V((F, D, C), BF16),
+        V((1, D), F32), V((1, D), F32), V((Z, 1, C), F32), V((Z, 1, C), F32),
+        V((32, 1, LANES), F32), V((1, LANES), F32), V((64, C), BF16), V((64, 2 * C), BF16),
+        V((T, D), F32), V((T, D), BF16), V((D, T), BF16), V((T, D), BF16), V((D, T), BF16),
+        V((T, D), BF16), V((D, T), BF16), V((T, D), F32), V((T, D), F32), V((T, D), F32),
+        V((3 * C // LANES, T, LANES), F32), V((T, C), F32), V((T, C), F32),
+        V((T, C), BF16), V((T, C), BF16),
+        V((T, 3 * C), BF16), V((Z, T, C), BF16), V((Z, T + SUB, C), F32),
+        V((Z, T, C), F32), V((Z, T, C), F32), V((Z, T, C), F32), V((Z, T, C), F32),
+        S((2, 6)),
+        S((7,)), S((3,)), S((3,)), S((4,)), S((4,)), S((4,)),
+        S((4,)), S((4,)), S(()), S(()), S((3, 3)), S((3, 4)),
+        S((3, 4)), S((3, 4)), S((3, 4, 2)), S((3, 4, 2)), S((3, 4)), S((3, 4)),
+    ]
+    return pl.pallas_call(
+        layer_ag_kernel,
+        out_shape=out_shape,
+        in_specs=[vm] * 12,
+        out_specs=(vm, vm, anyspec, anyspec, anyspec, anyspec, vm, vm, vm, vm),
+        scratch_shapes=scratch,
+        compiler_params=pltpu.CompilerParams(
+            vmem_limit_bytes=67043328, collective_id=0, has_side_effects=True
+        ),
+        name="layer_ag",
+    )(tok, cot, fw, iw, cw, ow, uw, dw, mg, fb, ib, fg)
+
 
 TINY = 1e-30
 CLIP = 0.01
+
+
+def gathered_layer(tok, cot, mix, ow, uw, dw, mg, fb, ib, fg):
+    def whole(w):
+        w = lax.all_gather(w, "inner", axis=1, tiled=True)
+        return lax.all_gather(w, "grp", axis=0, tiled=True)
+
+    def vec(v):
+        return lax.all_gather(v, ("grp", "inner"), axis=0, tiled=True).astype(F32)
+
+    width = tok.shape[1]
+    inners = lax.axis_size("inner")
+    Z, F = mix[0].shape[1] * inners // C, uw.shape[1] * inners // C
+    gates = [whole(w).reshape(width, Z, C // LANES, 1, LANES) for w in mix]
+    wmix = jnp.concatenate(gates, axis=3).reshape(width, Z, 3 * C).transpose(1, 0, 2)
+    wot = whole(ow).reshape(Z, C, width).transpose(0, 2, 1)
+    wup = whole(uw).reshape(width, F, C).transpose(1, 0, 2)
+    wdt = whole(dw).reshape(F, C, width).transpose(0, 2, 1)
+    return layer(
+        tok, cot, wmix, wot, wup, wdt,
+        vec(mg).reshape(1, width), vec(fg).reshape(1, width),
+        vec(fb).reshape(Z, 1, C), vec(ib).reshape(Z, 1, C),
+    )
 
 
 def body(
@@ -490,30 +946,25 @@
     groups = lax.axis_size("grp")
     inners = lax.axis_size("inner")
     seqs, length, width = tokens.shape
-    def whole(w):
-        w = lax.all_gather(w, "inner", axis=1, tiled=True)
-        return lax.all_gather(w, "grp", axis=0, tiled=True)
-
+    paired = (groups, inners) == (4, 8) and (length, width) == (1024, 512)
     hidden = forget_weight.shape[1] * inners
     ff = up_weight.shape[1] * inners
     Z, F = hidden // C, ff // C
-    gates = [
-        whole(w).reshape(width, Z, C // LANES, 1, LANES)
-        for w in (forget_weight, input_gate_weight, candidate_weight)
-    ]
-    wmix = jnp.concatenate(gates, axis=3).reshape(width, Z, 3 * C).transpose(1, 0, 2)
-    wot = whole(output_weight).reshape(Z, C, width).transpose(0, 2, 1)
-    wup = whole(up_weight).reshape(width, F, C).transpose(1, 0, 2)
-    wdt = whole(down_weight).reshape(F, C, width).transpose(0, 2, 1)
-    vec = lambda v: lax.all_gather(v, ("grp", "inner"), axis=0, tiled=True).astype(F32)
-    (
-        block_output, tokens_grad, gmix, got, gup, gdt, fgg, mgg, fbg, ibg
-    ) = layer(
-        tokens.reshape(length, width), cotangent.reshape(length, width),
-        wmix, wot, wup, wdt,
-        vec(mixer_gain).reshape(1, width), vec(feed_norm_gain).reshape(1, width),
-        vec(forget_bias).reshape(Z, 1, C), vec(input_bias).reshape(Z, 1, C),
-    )
+    if paired:
+        results = layer_ag(
+            tokens.reshape(length, width), cotangent.reshape(length, width),
+            forget_weight, input_gate_weight, candidate_weight,
+            output_weight, up_weight, down_weight,
+            mixer_gain, forget_bias, input_bias, feed_norm_gain,
+        )
+    else:
+        results = gathered_layer(
+            tokens.reshape(length, width), cotangent.reshape(length, width),
+            (forget_weight, input_gate_weight, candidate_weight),
+            output_weight, up_weight, down_weight,
+            mixer_gain, forget_bias, input_bias, feed_norm_gain,
+        )
+    block_output, tokens_grad, gmix, got, gup, gdt, fgg, mgg, fbg, ibg = results
     block_output = block_output.reshape(tokens.shape)
     tokens_grad = tokens_grad.reshape(tokens.shape)
     split = gmix.transpose(1, 0, 2).reshape(width, Z, C // LANES, 3, LANES)

time: 1030 us -> 898 us (0.87)
  blocking collectives: 239 us -> 111 us
  Pallas kernels: 101 us -> 138 us
  waiting for transfers between devices: 511 us -> 490 us
  local copies, waits for them, and re-layouts: 100 us -> 81.7 us
    all_gather x6 -> x0, blocking collectives: 89.7 us -> none  [whole(): w = lax.all_gather(w, 'inner', axis=1, tiled=True)]
    all_gather x6 -> x0, waiting for transfers between devices: 49.8 us -> none  [whole(): return lax.all_gather(w, 'grp', axis=0, tiled=True)]
    unnamed x2 -> x1, blocking collectives: 54.9 us -> 16.8 us
    pallas_call x1, Pallas kernels: 101 us -> 138 us  [layer_ag(): pl.pallas_call(layer_ag_kernel, out_shape=out_shape, in_specs=[vm] * 12,...]
    unnamed x28 -> x22, waiting for transfers between devices: 172 us -> 200 us
    reshape x4 -> x0, local copies, waits for them, and re-layouts: 13 us -> none  [the longest x1 3.92 us: body(): wup = whole(up_weight).reshape(width, F, C).transpose(1, 0, 2)]
    unnamed x162 -> x146, local copies, waits for them, and re-layouts: 26.1 us -> 29.8 us
  transfers between devices with their start and end apart: 22 -> 16, of which waited for: 18 -> 16; matrix products, arithmetic and copies ran while one was open for 8% -> 5% of each run, Pallas kernels for 0% -> 0%
where the time goes in v2:
time: 898 us; the launch traced here: 896 us
  waiting for transfers between devices  490 us (55%)
  Pallas kernels  138 us (15%)
  blocking collectives  111 us (12%)
  local copies, waits for them, and re-layouts  81.7 us (9%)
  between operations  39.7 us (4%)
  other arithmetic  35.1 us (4%)
    unnamed x22, waiting for transfers between devices  200 us
    pallas_call x1, Pallas kernels, layer_ag(): pl.pallas_call(layer_ag_kernel, out_shape=out_shape, in_specs=[vm] * 12,...  138 us
    reduce_scatter x1, waiting for transfers between devices, body(): lax.psum_scatter(up_term, 'inner', scatter_dimension=1, tiled=True)  48.9 us
    psum x1, blocking collectives, body(): lax.psum(jnp.stack([jnp.sum(s * s) for s in scaled_all]), ('grp', 'inner'))  40.6 us
    psum x1, blocking collectives, body(): lax.psum(jnp.stack([jnp.sum(w * w) for w in locals_f] + [jnp.sum(r) * fir...  36.8 us
    reduce_scatter x1, waiting for transfers between devices, body(): lax.psum_scatter(forget_term, 'inner', scatter_dimension=1, tiled=True)  36.8 us
    reduce_scatter x1, waiting for transfers between devices, body(): lax.psum_scatter(input_term, 'inner', scatter_dimension=1, tiled=True)  36.8 us
    reduce_scatter x1, waiting for transfers between devices, body(): lax.psum_scatter(part[9], 'grp', scatter_dimension=0, tiled=True)  30.2 us
  transfers between devices with their start and end apart: 16, of which 16 were waited for; matrix products, arithmetic and copies ran while one was open for 5% of the time, Pallas kernels for 0%

profile of v2, /device:TPU:0, one launch (start us, length us, event | category | flops | bytes accessed | tf_op | source)
XLA Modules:
  0.0 896.0 jit_solution(5518130508424523995)
XLA Ops:
  10.4 137.8 %layer_ag.1 = (bf16[1024,512]{1,0:T(8,128)(2,1)}, bf16[1024,512]{1,0:T(8,128)(2,1)}, f32[4,512,768]{2,1,0:T(8,128)}, f32[4,512,256]{2,1,0:T(8,128)}, f32[8,512,2...) custom-call(bf16[1024,512]{1,0:T(8,128)(2,1)} %bitcast.117, ...), custom_call_target="tpu_custom_call" | custom-call | tf_op jit(solution)/shard_map/layer_ag/pallas_call | solution.py:876
  148.2 6.5 copy.93
  192.8 6.2 reduce-scatter.37.cloned.1.call-done
  199.1 36.8 %reduce-scatter.33.cloned.1.call-done = f32[512,128]{1,0:T(8,128)} async-done(((f32[512,1024]{1,0:T(8,128)}), f32[512,128]{1,0:T(8,128)}) %reduce-scatter.33.cloned.1.call-update) | async-done | bytes 262160 | tf_op jit(solution)/shard_map/reduce_scatter | solution.py:984
  235.9 36.8 %reduce-scatter.29.cloned.1.call-done = f32[512,128]{1,0:T(8,128)} async-done(((f32[512,1024]{1,0:T(8,128)}), f32[512,128]{1,0:T(8,128)}) %reduce-scatter.29.cloned.1.call-update) | async-done | bytes 262160 | tf_op jit(solution)/shard_map/reduce_scatter | solution.py:983
  272.8 36.7 %reduce-scatter.55.cloned.1.call-done = f32[64,1024]{1,0:T(8,128)} async-done(((f32[512,1024]{1,0:T(8,128)}), f32[64,1024]{1,0:T(8,128)}) %reduce-scatter.55.cloned.1.call-update) | async-done | bytes 262160
  311.5 48.9 %reduce-scatter.43.cloned.1.call-done = f32[512,256]{0,1:T(8,128)} async-done(((f32[512,2048]{0,1:T(8,128)}), f32[512,256]{0,1:T(8,128)}) %reduce-scatter.43.cloned.1.call-update) | async-done | bytes 524304 | tf_op jit(solution)/shard_map/reduce_scatter | solution.py:992
  363.8 47.0 %reduce-scatter.59.cloned.1.call-done = f32[64,2048]{1,0:T(8,128)} async-done(((f32[512,2048]{1,0:T(8,128)}), f32[64,2048]{1,0:T(8,128)}) %reduce-scatter.59.cloned.1.call-update) | async-done | bytes 524304
  417.2 24.6 %reduce-scatter.49.cloned.1.call-done = f32[16,4]{1,0:T(8,128)} async-done(((f32[128,4]{1,0:T(8,128)}), f32[16,4]{1,0:T(8,128)}) %reduce-scatter.49.cloned.1.call-update) | async-done | bytes 272
  442.5 30.4 %reduce-scatter.57.cloned.1.call-done = f32[16,4]{1,0:T(8,128)} async-done(((f32[128,4]{1,0:T(8,128)}), f32[16,4]{1,0:T(8,128)}) %reduce-scatter.57.cloned.1.call-update) | async-done | bytes 272
  473.7 30.4 %reduce-scatter.51.cloned.1.call-done = f32[32,4]{1,0:T(8,128)} async-done(((f32[256,4]{1,0:T(8,128)}), f32[32,4]{1,0:T(8,128)}) %reduce-scatter.51.cloned.1.call-update) | async-done | bytes 528
  504.9 30.3 %reduce-scatter.53.cloned.1.call-done = f32[32,4]{1,0:T(8,128)} async-done(((f32[256,4]{1,0:T(8,128)}), f32[32,4]{1,0:T(8,128)}) %reduce-scatter.53.cloned.1.call-update) | async-done | bytes 528
  536.0 24.9 %reduce-scatter.39.cloned.1.call-done = f32[128,128]{1,0:T(8,128)} async-done(((f32[512,128]{1,0:T(8,128)}), f32[128,128]{1,0:T(8,128)}) %reduce-scatter.39.cloned.1.call-update) | async-done | bytes 65552 | tf_op jit(solution)/shard_map/reduce_scatter | solution.py:999
  561.8 26.6 %reduce-scatter.35.cloned.1.call-done = f32[128,128]{1,0:T(8,128)} async-done(((f32[512,128]{1,0:T(8,128)}), f32[128,128]{1,0:T(8,128)}) %reduce-scatter.35.cloned.1.call-update) | async-done | bytes 65552 | tf_op jit(solution)/shard_map/reduce_scatter | solution.py:998
  589.3 26.5 %reduce-scatter.31.cloned.1.call-done = f32[128,128]{1,0:T(8,128)} async-done(((f32[512,128]{1,0:T(8,128)}), f32[128,128]{1,0:T(8,128)}) %reduce-scatter.31.cloned.1.call-update) | async-done | bytes 65552 | tf_op jit(solution)/shard_map/reduce_scatter | solution.py:997
  616.8 27.4 %reduce-scatter.41.cloned.1.call-done = f32[256,64]{1,0:T(8,128)} async-done(((f32[1024,64]{1,0:T(8,128)}), f32[256,64]{1,0:T(8,128)}) %reduce-scatter.41.cloned.1.call-update) | async-done | bytes 65552 | tf_op jit(solution)/shard_map/reduce_scatter | solution.py:1002
  645.3 26.4 %reduce-scatter.45.cloned.1.call-done = f32[128,256]{0,1:T(8,128)} async-done(((f32[512,256]{0,1:T(8,128)}), f32[128,256]{0,1:T(8,128)}) %reduce-scatter.45.cloned.1.call-update) | async-done | bytes 131088 | tf_op jit(solution)/shard_map/reduce_scatter | solution.py:1004
  672.7 30.2 %reduce-scatter.47.cloned.1.call-done = f32[512,64]{1,0:T(8,128)} async-done(((f32[2048,64]{1,0:T(8,128)}), f32[512,64]{1,0:T(8,128)}) %reduce-scatter.47.cloned.1.call-update) | async-done | bytes 131088 | tf_op jit(solution)/shard_map/reduce_scatter | solution.py:1005
  704.1 16.6 %all-reduce.4 = (f32[128]{0:T(128)S(1)}, f32[128]{0:T(128)S(1)}, f32[128]{0:T(128)S(1)}, f32[256]{0:T(256)S(1)}, f32[128]{0:T(128)S(1)}, /*index=5*/f32[512]{0:T(512)S(1)}) all-reduce(f32[128]{0:T(128)S(1)} %get-tuple-element.148, f32[128]{0:T(128)S(1)} %get-tuple-element.146, ...), channel_id=1, replica_groups=mesh['grp'=4,'inner'=8] {'inner'}, use_global_device_ids=true, to_apply=%region_39.0 | all-reduce | flops 1280 | bytes 10240 | tf_op jit(solution)/shard_map/psum | solution.py:1055
  727.1 6.6 stack.121
  735.3 36.8 %psum.105 = f32[16]{0:T(128)S(1)} all-reduce(f32[16]{0:T(128)S(1)} %stack.121), channel_id=1, replica_groups=mesh['grp'=4,'inner'=8] {'grp','inner'}, use_global_device_ids=true, to_apply=%region_36.0 | all-reduce | flops 16 | bytes 128 | tf_op jit(solution)/shard_map/psum | solution.py:1046
  776.1 16.8 %all-reduce.5 = (f32[4,16]{1,0:T(4,128)S(1)}, f32[4,32]{1,0:T(4,128)S(1)}, f32[4,32]{1,0:T(4,128)S(1)}, f32[4,16]{1,0:T(4,128)S(1)}, f32[6]{0:T(128)S(1)}, /*ind...) all-reduce(f32[4,16]{1,0:T(4,128)S(1)} %copy.110, ...), channel_id=3, replica_groups=mesh['grp'=4,'inner'=8] {'grp'}, use_global_device_ids=true, to_apply=%region_1.0.clone | all-reduce | flops 1158 | bytes 9264
  823.8 6.5 stack.139
  830.3 40.6 %psum.119 = f32[10]{0:T(128)S(1)} all-reduce(f32[10]{0:T(128)S(1)} %stack.139), channel_id=1, replica_groups=mesh['grp'=4,'inner'=8] {'grp','inner'}, use_global_device_ids=true, to_apply=%region_78.0 | all-reduce | flops 10 | bytes 80 | tf_op jit(solution)/shard_map/psum | solution.py:1094
  (236 shorter events, 98.3 us)
Async XLA Ops:
  7.2 191.8 %reduce-scatter.37.cloned.1.call-start = ((), (), s32[]{:S(2)}) async-start(), calls=%async_computation.20 | async-start | bytes 2359296 | tf_op jit(solution)/shard_map/reduce_scatter | solution.py:985
  163.7 72.2 %reduce-scatter.33.cloned.1.call-start = ((), (), s32[]{:S(2)}) async-start(), calls=%async_computation.18 | async-start | bytes 2359296 | tf_op jit(solution)/shard_map/reduce_scatter | solution.py:984
  166.7 106.1 %reduce-scatter.29.cloned.1.call-start = ((), (), s32[]{:S(2)}) async-start(), calls=%async_computation.16 | async-start | bytes 2359296 | tf_op jit(solution)/shard_map/reduce_scatter | solution.py:983
  168.6 140.8 %reduce-scatter.55.cloned.1.call-start = ((), (), s32[]{:S(2)}) async-start(), calls=%async_computation.29 | async-start | bytes 2359296
  172.5 187.9 %reduce-scatter.43.cloned.1.call-start = ((), (), s32[]{:S(2)}) async-start(), calls=%async_computation.23 | async-start | bytes 4718592 | tf_op jit(solution)/shard_map/reduce_scatter | solution.py:992
  177.9 232.8 %reduce-scatter.59.cloned.1.call-start = ((), (), s32[]{:S(2)}) async-start(), calls=%async_computation.31 | async-start | bytes 4718592
  188.9 252.9 %reduce-scatter.49.cloned.1.call-start = ((), (), s32[]{:S(2)}) async-start(), calls=%async_computation.26 | async-start | bytes 73728
  190.2 282.8 %reduce-scatter.57.cloned.1.call-start = ((), (), s32[]{:S(2)}) async-start(), calls=%async_computation.30 | async-start | bytes 73728
  191.0 313.1 %reduce-scatter.51.cloned.1.call-start = ((), (), s32[]{:S(2)}) async-start(), calls=%async_computation.27 | async-start | bytes 147456
  191.9 343.4 %reduce-scatter.53.cloned.1.call-start = ((), (), s32[]{:S(2)}) async-start(), calls=%async_computation.28 | async-start | bytes 147456
  192.8 368.1 %reduce-scatter.39.cloned.1.call-start = ((), (), s32[]{:S(2)}) async-start(), calls=%async_computation.21 | async-start | bytes 327680 | tf_op jit(solution)/shard_map/reduce_scatter | solution.py:999
  199.0 389.4 %reduce-scatter.35.cloned.1.call-start = ((), (), s32[]{:S(2)}) async-start(), calls=%async_computation.19 | async-start | bytes 327680 | tf_op jit(solution)/shard_map/reduce_scatter | solution.py:998
  235.9 380.0 %reduce-scatter.31.cloned.1.call-start = ((), (), s32[]{:S(2)}) async-start(), calls=%async_computation.17 | async-start | bytes 327680 | tf_op jit(solution)/shard_map/reduce_scatter | solution.py:997
  272.7 371.4 %reduce-scatter.41.cloned.1.call-start = ((), (), s32[]{:S(2)}) async-start(), calls=%async_computation.22 | async-start | bytes 655360 | tf_op jit(solution)/shard_map/reduce_scatter | solution.py:1002
  311.5 360.1 %reduce-scatter.45.cloned.1.call-start = ((), (), s32[]{:S(2)}) async-start(), calls=%async_computation.24 | async-start | bytes 655360 | tf_op jit(solution)/shard_map/reduce_scatter | solution.py:1004
  360.5 342.5 %reduce-scatter.47.cloned.1.call-start = ((), (), s32[]{:S(2)}) async-start(), calls=%async_computation.25 | async-start | bytes 1310720 | tf_op jit(solution)/shard_map/reduce_scatter | solution.py:1005
  410.7 397.0 %copy-start.57 = (f32[64]{0:T(128)S(1)}, f32[64]{0:T(128)}, u32[]{:S(2)}) copy-start(f32[64]{0:T(128)} %param.51) | copy-start | bytes 772
  410.7 397.0 %copy-start.58 = (f32[64]{0:T(128)S(1)}, f32[64]{0:T(128)}, u32[]{:S(2)}) copy-start(f32[64]{0:T(128)} %param.56) | copy-start | bytes 772
  410.7 397.0 %copy-start.44 = (f32[256]{0:T(256)S(1)}, f32[256]{0:T(256)}, u32[]{:S(2)}) copy-start(f32[256]{0:T(256)} %param.54) | copy-start | bytes 3076
  410.8 397.0 %copy-start.50 = (f32[16]{0:T(128)S(1)}, f32[16]{0:T(128)}, u32[]{:S(2)}) copy-start(f32[16]{0:T(128)} %param.41) | copy-start | bytes 196
  410.8 398.3 %copy-start.51 = (f32[32]{0:T(128)S(1)}, f32[32]{0:T(128)}, u32[]{:S(2)}) copy-start(f32[32]{0:T(128)} %param.48) | copy-start | bytes 388
  410.8 399.6 %copy-start.52 = (f32[32]{0:T(128)S(1)}, f32[32]{0:T(128)}, u32[]{:S(2)}) copy-start(f32[32]{0:T(128)} %param.49) | copy-start | bytes 388
  410.8 400.8 %copy-start.53 = (f32[16]{0:T(128)S(1)}, f32[16]{0:T(128)}, u32[]{:S(2)}) copy-start(f32[16]{0:T(128)} %param.52) | copy-start | bytes 196
  413.2 457.6 %copy-start.59 = (f32[10]{0:T(128)S(1)}, f32[10]{0:T(128)}, u32[]{:S(2)}) copy-start(f32[10]{0:T(128)} %constant.148) | copy-start | bytes 124
  (53 other events, 8033.5 us)
Sparse Core Ops, SparseCore 0:
  163.8 35.1 reduce-scatter.36
  201.3 34.5 reduce-scatter.32
  238.1 34.5 reduce-scatter.28
  274.9 34.5 reduce-scatter.54
  311.6 48.7 reduce-scatter.42
  362.5 48.1 reduce-scatter.58
  413.5 28.1 reduce-scatter.48
  444.7 28.2 reduce-scatter.56
  475.7 28.3 reduce-scatter.50
  506.9 28.3 reduce-scatter.52
  538.6 22.2 reduce-scatter.38
  564.3 24.0 reduce-scatter.34
  591.7 24.0 reduce-scatter.30
  619.3 24.7 reduce-scatter.40
  646.8 24.7 reduce-scatter.44
  675.2 27.6 reduce-scatter.46

commit v3 on v2

--- a/solution.py
+++ b/solution.py
@@ -885,9 +885,475 @@
         name="layer_ag",
     )(tok, cot, fw, iw, cw, ow, uw, dw, mg, fb, ib, fg)
 
-
+SHAPES = ((128, 256), (128, 256), (128, 384), (64, 256))
+UP, DOWN, MIX, OUT = 0, 1, 2, 3
 TINY = 1e-30
 CLIP = 0.01
+MATRICES = (
+    (512, 1024), (512, 1024), (512, 1024), (1024, 512), (512, 2048), (2048, 512)
+)
+MATRIX_SLOTS = (1, 2, 3, 6, 8, 9)
+VECTORS = ((0, 0, 16), (4, 16, 32), (5, 48, 32), (7, 80, 16))
+COUNTS = (512, 524288, 524288, 524288, 1024, 1024, 524288, 512, 1048576, 1048576)
+
+
+def piece(refs, a, g, z, c):
+    i = z * 2 + c
+    if a == UP:
+        return refs.gup[i, g * 128 : (g + 1) * 128, :]
+    if a == DOWN:
+        return jnp.concatenate([refs.gdt[2 * g + h, at(i, 64), :] for h in range(2)], axis=0)
+    if a == MIX:
+        return refs.gmix[z, g * 128 : (g + 1) * 128, at(c, 384)]
+    return refs.got[g, at(i, 64), :]
+
+
+def rs_fill(refs, p, a, z):
+    for g in range(4):
+        refs.psend[a][z, g] = piece(refs, a, g, z, 1 - p.c).astype(BF16)
+
+
+def rs_copy(refs, p, stage, a, z):
+    if stage == 0:
+        src, dst, dev = refs.psend[a].at[z], refs.precv[a].at[z], p.partner
+    elif stage == 1:
+        src, dst, dev = refs.buf1[a].at[z, 1], refs.r1[a].at[z], (p.near(z), p.i)
+    else:
+        src, dst, dev = refs.buf2[a].at[z, 1], refs.r2[a].at[z], (p.far(z), p.i)
+    return rcopy(src, dst, refs.rs_s.at[stage, a, z], refs.rs_r.at[stage, a, z], dev)
+
+
+def rs_first(refs, p, a, z):
+    rs_copy(refs, p, 0, a, z).wait_recv()
+    e = z % 2
+    for g in range(4):
+        y, x = g // 2, g % 2
+        v = piece(refs, a, g, z, p.c) + refs.precv[a][z, g].astype(F32)
+        role = (1 - e) * ((x + p.x) % 2) + e * ((y + p.y) % 2)
+        refs.buf1[a][z, role, (1 - e) * y + e * x] = v.astype(BF16)
+
+
+def rs_second(refs, p, a, z):
+    rs_copy(refs, p, 1, a, z).wait_recv()
+    e = z % 2
+    for k in range(2):
+        v = refs.buf1[a][z, 0, k].astype(F32) + refs.r1[a][z, k].astype(F32)
+        refs.buf2[a][z, (k + (1 - e) * p.y + e * p.x) % 2] = v.astype(BF16)
+
+
+def rs_line(refs, p, a, z, owner):
+    return rcopy(
+        refs.buf3[a].at[z], refs.r3[a].at[owner], refs.r3_s.at[a, z], refs.r3_r.at[a, owner],
+        (p.g, z * 2 + p.c),
+    )
+
+
+def rs_third(refs, p, a, z):
+    rs_copy(refs, p, 2, a, z).wait_recv()
+    v = refs.buf2[a][z, 0].astype(F32) + refs.r2[a][z].astype(F32)
+    refs.buf3[a][z] = v.astype(BF16)
+
+    @pl.when(z == p.z)
+    def _():
+        refs.fin[a][...] = v
+
+
+def rs_third_send(refs, p, a, z):
+    @pl.when(z != p.z)
+    def _():
+        rs_line(refs, p, a, z, p.z).start()
+
+
+def rs_last(refs, p, a):
+    for k in range(1, 4):
+        z = (p.z + k) % 4
+        rs_line(refs, p, a, z, z).wait_recv()
+        refs.fin[a][...] += refs.r3[a][z].astype(F32)
+
+
+def rs_drain(refs, p):
+    def one(z):
+        for a in range(4):
+            for stage in range(3):
+                rs_copy(refs, p, stage, a, z).wait_send()
+
+            @pl.when(z != p.z)
+            def _():
+                rs_line(refs, p, a, z, p.z).wait_send()
+
+    loop(4, one)
+
+
+def own_row(x):
+    return jnp.sum(x, axis=0, keepdims=True)
+
+
+def lane_sum(x):
+    folded = sum(x[:, k : k + LANES] for k in range(0, x.shape[1], LANES))
+    return own_row(folded.T)
+
+
+def wide(row):
+    return jnp.concatenate([row, jnp.zeros((1, LANES - row.shape[1]), F32)], axis=1)
+
+
+def cut(row):
+    return [row[:, k : k + LANES] for k in range(0, row.shape[1], LANES)]
+
+
+def stand(row):
+    return jnp.broadcast_to(row, (LANES, LANES)).T
+
+
+def scalars(values):
+    lane = lax.broadcasted_iota(jnp.int32, (1, LANES), 1)
+    out = jnp.zeros((1, LANES), F32)
+    for k, v in enumerate(values):
+        out = out + jnp.where(lane == k, v, 0.0)
+    return out
+
+
+def total(x):
+    return jnp.sum(jnp.sum(x, axis=0, keepdims=True), axis=1, keepdims=True)
+
+
+def segment(row, start, count):
+    lane = lax.broadcasted_iota(jnp.int32, row.shape, 1)
+    keep = (lane >= start) & (lane < start + count)
+    return jnp.sum(jnp.where(keep, row, 0.0), axis=1, keepdims=True)
+
+
+def gather_row(term, start, count):
+    size = term.shape[1]
+    owner = lax.broadcasted_iota(jnp.int32, (32, size), 0)
+    spot = lax.broadcasted_iota(jnp.int32, (32, size), 1)
+    masked = jnp.where(spot // count == owner, term, 0.0)
+    lane = lax.broadcasted_iota(jnp.int32, (LANES, size), 0)
+    from_spot = lax.broadcasted_iota(jnp.int32, (LANES, size), 1)
+    sel = jnp.where(lane == start + from_spot % count, 1.0, 0.0).astype(BF16)
+    out = jnp.zeros((32, LANES), F32)
+    for _ in range(3):
+        part = masked.astype(BF16)
+        out = out + dot_t(part, sel)
+        masked = masked - part.astype(F32)
+    return out
+
+
+def parameter_blocks(refs):
+    return [
+        refs.fw[...].astype(F32), refs.iw[...].astype(F32), refs.cw[...].astype(F32),
+        refs.ow[...].astype(F32).T, refs.uw[...].astype(F32), refs.dw[...].astype(F32).T,
+    ]
+
+
+def old_rows(refs):
+    rows = []
+    for r in (refs.row_f, refs.row_i, refs.row_c, refs.row_o, refs.row_u, refs.row_d):
+        rows += cut(r[...].reshape(1, r.shape[0]))
+    return rows
+
+
+def old_columns(refs):
+    rows = []
+    for r in (refs.col_f, refs.col_i, refs.col_c, refs.col_o, refs.col_u, refs.col_d):
+        row = r[...].reshape(1, r.shape[0])
+        rows += [wide(row)] if r.shape[0] < LANES else cut(row)
+    return rows
+
+
+ROW_PLACES = ((0, 1), (1, 2), (2, 3), (3, 5), (5, 6), (6, 10))
+COLUMN_PLACES = ((0, 1), (1, 2), (2, 3), (3, 4), (4, 6), (6, 7))
+
+
+def broadcast_row(src, box, send, recv, p):
+    def one(k):
+        rcopy(src, box.at[p.me], send, recv, p.other(k + 1)).start()
+
+    loop(31, one)
+
+
+def settle_row(box, send, recv, p):
+    rows = box.at[pl.ds(0, 31)]
+    rcopy(rows, rows, send, recv, p.partner).wait()
+
+
+def vector_exchange(refs, p):
+    rows = (
+        gather_row(refs.mgg[...], 0, 16)
+        + gather_row(jnp.concatenate([refs.fbg[z] for z in range(4)], axis=1), 16, 32)
+        + gather_row(jnp.concatenate([refs.ibg[z] for z in range(4)], axis=1), 48, 32)
+        + gather_row(refs.fgg[...], 80, 16)
+    )
+    refs.vout[...] = rows.reshape(32, 1, LANES)
+    refs.vin[p.me] = refs.vout[p.me]
+
+    def one(k):
+        t = (p.me + k + 1) % 32
+        rcopy(refs.vout.at[t], refs.vin.at[p.me], refs.vex_s, refs.vex_r, p.other(k + 1)).start()
+
+    loop(31, one)
+
+
+def gradient_blocks(refs):
+    mix = refs.fin[MIX][...]
+    down = refs.fin[DOWN][...]
+    return [
+        mix[:, 0:128], mix[:, 128:256], mix[:, 256:384], refs.fin[OUT][...], refs.fin[UP][...],
+        jnp.concatenate([down[0:64], down[64:128]], axis=1),
+    ]
+
+
+def adafactor(refs, p):
+    grads = gradient_blocks(refs)
+    flipped = (False, False, False, True, False, True)
+    row_parts, column_parts, totals = [], [], []
+    for grad, flip in zip(grads, flipped):
+        sq = grad * grad
+        down, across = own_row(sq), lane_sum(sq)
+        row_parts += cut(down) if flip else [across]
+        column_parts += [wide(across)] if flip else cut(down)
+        totals.append(jnp.sum(down, axis=1, keepdims=True))
+    refs.rowst[...] = jnp.concatenate(row_parts + [jnp.zeros((6, LANES), F32)], axis=0)
+    refs.colst[...] = jnp.concatenate(column_parts + [jnp.zeros((1, LANES), F32)], axis=0)
+    weights = parameter_blocks(refs)
+    params = pack_vectors(refs.mg, refs.fbv, refs.ibv, refs.fg)
+    squares = [None] * 10
+    for slot, w in zip(MATRIX_SLOTS, weights):
+        squares[slot] = total(w * w)
+    for slot, start, count in VECTORS:
+        squares[slot] = segment(params * params, start, count)
+    rows_old, columns_old = old_rows(refs), old_columns(refs)
+    first = jnp.where(p.i == 0, 1.0, 0.0)
+    row_sums = [first * total(jnp.concatenate(rows_old[a:b], axis=0)) for a, b in ROW_PLACES]
+    refs.scal[...] = scalars(totals + squares + row_sums)
+    refs.rowin[p.i] = refs.rowst[...]
+    refs.colin[p.g] = refs.colst[...]
+    refs.scin[p.me] = refs.scal[...]
+    for k in range(1, 8):
+        peer = (p.g, (p.i + k) % 8)
+        rcopy(
+            refs.rowst, refs.rowin.at[p.i], refs.row_s.at[k - 1], refs.row_r.at[k - 1], peer
+        ).start()
+    for k in range(1, 4):
+        peer = ((p.g + k) % 4, p.i)
+        rcopy(
+            refs.colst, refs.colin.at[p.g], refs.col_s.at[k - 1], refs.col_r.at[k - 1], peer
+        ).start()
+    broadcast_row(refs.scal, refs.scin, refs.sc_s, refs.sc_r, p)
+    vec_rows = refs.vin.at[pl.ds(0, 31)]
+    rcopy(vec_rows, vec_rows, refs.vex_s, refs.vex_r, p.partner).wait()
+    vector_grad = jnp.sum(refs.vin[...].reshape(32, LANES), axis=0, keepdims=True)
+    seconds = pack_vectors(refs.sec_m, refs.sec_f, refs.sec_i, refs.sec_g)
+    second = 0.5 * seconds + 0.5 * (vector_grad * vector_grad + TINY)
+    vector_scaled = vector_grad * lax.rsqrt(second)
+    for k in range(1, 8):
+        rcopy(
+            refs.rowst, refs.rowin.at[p.i], refs.row_s.at[k - 1], refs.row_r.at[k - 1], p.partner
+        ).wait()
+    for k in range(1, 4):
+        rcopy(
+            refs.colst, refs.colin.at[p.g], refs.col_s.at[k - 1], refs.col_r.at[k - 1], p.partner
+        ).wait()
+    settle_row(refs.scin, refs.sc_s, refs.sc_r, p)
+    row_total = sum(refs.rowin[k] for k in range(8))
+    column_total = sum(refs.colin[k] for k in range(4))
+    sc = jnp.sum(refs.scin[...].reshape(32, LANES), axis=0, keepdims=True)
+    rows_new, columns_new, scaled = [], [], []
+    for k, (r, c) in enumerate(MATRICES):
+        ra, rb = ROW_PLACES[k]
+        ca, cb = COLUMN_PLACES[k]
+        rows = [
+            0.5 * rows_old[j] + 0.5 * (row_total[j : j + 1] / c + TINY) for j in range(ra, rb)
+        ]
+        columns = [
+            0.5 * columns_old[j] + 0.5 * (column_total[j : j + 1] / r + TINY)
+            for j in range(ca, cb)
+        ]
+        mean = 0.5 * sc[:, 16 + k : 17 + k] / r + 0.5 * (sc[:, k : k + 1] / (r * c) + TINY)
+        lying, standing = (rows, columns) if flipped[k] else (columns, rows)
+        tall = stand(standing[0])[0 : grads[k].shape[0]]
+        lying = jnp.concatenate(lying, axis=1)
+        tall = jnp.concatenate([tall] * (lying.shape[1] // LANES), axis=1)
+        scaled.append(grads[k] * lax.rsqrt(tall * lying / mean))
+        rows_new += rows
+        columns_new += columns
+    refs.rows_out[...] = jnp.concatenate(rows_new + [jnp.zeros((6, LANES), F32)], axis=0)
+    refs.columns_out[...] = jnp.concatenate(columns_new + [jnp.zeros((1, LANES), F32)], axis=0)
+    clips = [None] * 10
+    for slot, s in zip(MATRIX_SLOTS, scaled):
+        clips[slot] = total(s * s)
+    for slot, start, count in VECTORS:
+        clips[slot] = segment(vector_scaled * vector_scaled, start, count)
+    refs.clip[...] = scalars(clips)
+    refs.clin[p.me] = refs.clip[...]
+    broadcast_row(refs.clip, refs.clin, refs.cl_s, refs.cl_r, p)
+    settle_row(refs.clin, refs.cl_s, refs.cl_r, p)
+    clip = jnp.sum(refs.clin[...].reshape(32, LANES), axis=0, keepdims=True)
+    norms = [jnp.sqrt(clip[:, k : k + 1] / COUNTS[k]) for k in range(10)]
+    steps = [
+        -jnp.sqrt(sc[:, 6 + k : 7 + k] / COUNTS[k]) / jnp.maximum(CLIP, norms[k])
+        for k in range(10)
+    ]
+    fresh = [w + steps[slot] * s for slot, w, s in zip(MATRIX_SLOTS, weights, scaled)]
+    refs.grad_mix[...] = refs.fin[MIX][...]
+    refs.grad_out[...] = grads[3]
+    refs.grad_up[...] = grads[4]
+    refs.grad_down[...] = grads[5]
+    refs.new_mix[...] = jnp.concatenate(fresh[0:3], axis=1)
+    refs.new_out[...] = fresh[3]
+    refs.new_up[...] = fresh[4]
+    refs.new_down[...] = fresh[5]
+    lane = lax.broadcasted_iota(jnp.int32, (1, LANES), 1)
+    step_row = jnp.zeros((1, LANES), F32)
+    for slot, start, count in VECTORS:
+        step_row = step_row + jnp.where((lane >= start) & (lane < start + count), steps[slot], 0.0)
+    refs.vectors[...] = jnp.concatenate(
+        [vector_grad, params + step_row * vector_scaled, second, scalars(norms)]
+        + [jnp.zeros((4, LANES), F32)],
+        axis=0,
+    )
+
+
+class ExchangeRefs:
+    def __init__(self, args):
+        (
+            self.gmix, self.got, self.gup, self.gdt, self.fgg, self.mgg, self.fbg, self.ibg,
+            self.fw, self.iw, self.cw, self.ow, self.uw, self.dw,
+            self.mg, self.fbv, self.ibv, self.fg,
+            self.sec_m, self.row_f, self.col_f, self.row_i, self.col_i, self.row_c, self.col_c,
+            self.sec_f, self.sec_i, self.row_o, self.col_o, self.sec_g,
+            self.row_u, self.col_u, self.row_d, self.col_d,
+            self.grad_mix, self.grad_out, self.grad_up, self.grad_down,
+            self.new_mix, self.new_out, self.new_up, self.new_down,
+            self.vectors, self.rows_out, self.columns_out,
+        ) = args[:45]
+        rest = list(args[45:])
+        take = lambda n: [rest.pop(0) for _ in range(n)]
+        self.psend, self.precv, self.buf1, self.r1 = take(4), take(4), take(4), take(4)
+        self.buf2, self.r2, self.buf3, self.r3, self.fin = (
+            take(4), take(4), take(4), take(4), take(4)
+        )
+        (
+            self.vout, self.vin, self.rowst, self.rowin, self.colst, self.colin,
+            self.scal, self.scin, self.clip, self.clin,
+            self.rs_s, self.rs_r, self.r3_s, self.r3_r, self.vex_s, self.vex_r,
+            self.row_s, self.row_r, self.col_s, self.col_r, self.sc_s, self.sc_r,
+            self.cl_s, self.cl_r,
+        ) = rest
+
+
+def exchange_kernel(*args):
+    refs = ExchangeRefs(args)
+    p = Place()
+    entry_barrier(p)
+    arrays = (UP, DOWN, OUT, MIX)
+    for a in arrays:
+        loop(4, lambda z: rs_fill(refs, p, a, z))
+        loop(4, lambda z: rs_copy(refs, p, 0, a, z).start())
+    vector_exchange(refs, p)
+    for a in arrays:
+        loop(4, lambda z: rs_first(refs, p, a, z))
+        loop(4, lambda z: rs_copy(refs, p, 1, a, z).start())
+    for a in arrays:
+        loop(4, lambda z: rs_second(refs, p, a, z))
+        loop(4, lambda z: rs_copy(refs, p, 2, a, z).start())
+    for a in arrays:
+        loop(4, lambda z: rs_third(refs, p, a, z))
+        loop(4, lambda z: rs_third_send(refs, p, a, z))
+    for a in arrays:
+        rs_last(refs, p, a)
+    rs_drain(refs, p)
+    adafactor(refs, p)
+
+
+def finish_kernel(
+    grad_mix, grad_out, grad_up, grad_down, new_mix, new_out, new_up, new_down,
+    vectors, rows, columns,
+    g_mg, g_f, g_i, g_c, g_fb, g_ib, g_o, g_fg, g_u, g_d,
+    n_mg, n_f, n_i, n_c, n_fb, n_ib, n_o, n_fg, n_u, n_d,
+    s_m, r_f, c_f, r_i, c_i, r_c, c_c, s_f, s_i, r_o, c_o, s_g, r_u, c_u, r_d, c_d, norms,
+):
+    for src, outs in ((grad_mix, (g_f, g_i, g_c)), (new_mix, (n_f, n_i, n_c))):
+        for k, o in enumerate(outs):
+            o[...] = src[:, k * 128 : (k + 1) * 128]
+    for src, o in ((grad_out, g_o), (new_out, n_o), (grad_down, g_d), (new_down, n_d)):
+        o[...] = src[...].T
+    g_u[...] = grad_up[...]
+    n_u[...] = new_up[...]
+    for row, outs in (
+        (0, (g_mg, g_fb, g_ib, g_fg)), (1, (n_mg, n_fb, n_ib, n_fg)), (2, (s_m, s_f, s_i, s_g))
+    ):
+        for (_, start, count), o in zip(VECTORS, outs):
+            o[...] = vectors[row, start : start + count]
+    norms[...] = vectors[3, 0:10]
+    for src, places, outs in (
+        (rows, ROW_PLACES, (r_f, r_i, r_c, r_o, r_u, r_d)),
+        (columns, COLUMN_PLACES, (c_f, c_i, c_c, c_o, c_u, c_d)),
+    ):
+        for (a, b), o in zip(places, outs):
+            if b - a == 1:
+                o[...] = src[a, 0 : o.shape[0]]
+            else:
+                for k in range(a, b):
+                    o[(k - a) * LANES : (k - a + 1) * LANES] = src[k, :]
+
+
+def exchange(grads, shards, states):
+    sds = jax.ShapeDtypeStruct
+    vm = pl.BlockSpec(memory_space=pltpu.VMEM)
+    V = pltpu.VMEM
+    S = pltpu.SemaphoreType.DMA
+    packed = (
+        sds((128, 384), F32), sds((64, 256), F32), sds((128, 256), F32), sds((64, 512), F32),
+        sds((128, 384), F32), sds((64, 256), F32), sds((128, 256), F32), sds((64, 512), F32),
+        sds((8, LANES), F32), sds((16, LANES), F32), sds((8, LANES), F32),
+    )
+    scratch = (
+        [V((4, 4) + s, BF16) for s in SHAPES] * 2
+        + [V((4, 2, 2) + s, BF16) for s in SHAPES]
+        + [V((4, 2) + s, BF16) for s in SHAPES]
+        + [V((4, 2) + s, BF16) for s in SHAPES]
+        + [V((4,) + s, BF16) for s in SHAPES] * 3
+        + [V(s, F32) for s in SHAPES]
+    )
+    row = V((1, LANES), F32)
+    box = V((32, 1, LANES), F32)
+    scratch += [
+        box, box, V((16, LANES), F32), V((8, 16, LANES), F32),
+        V((8, LANES), F32), V((4, 8, LANES), F32), row, box, row, box,
+        S((3, 4, 4)), S((3, 4, 4)), S((4, 4)), S((4, 4)), S(()), S(()),
+        S((7,)), S((7,)), S((3,)), S((3,)), S(()), S(()), S(()), S(()),
+    ]
+    args = (*grads, *shards, *states)
+    return pl.pallas_call(
+        exchange_kernel,
+        out_shape=packed,
+        in_specs=[vm] * len(args),
+        out_specs=(vm,) * len(packed),
+        scratch_shapes=scratch,
+        compiler_params=pltpu.CompilerParams(
+            vmem_limit_bytes=67043328, collective_id=1, has_side_effects=True
+        ),
+        name="exchange",
+    )(*args)
+
+
+def finish(packed):
+    sds = jax.ShapeDtypeStruct
+    f = lambda *s: sds(s, F32)
+    block = [f(16), f(128, 128), f(128, 128), f(128, 128), f(32), f(32), f(256, 64), f(16),
+             f(128, 256), f(512, 64)]
+    states = [f(16), f(128), f(128), f(128), f(128), f(128), f(128), f(32), f(32), f(256), f(64),
+              f(16), f(128), f(256), f(512), f(64)]
+    outs = tuple(block + block + states + [f(10)])
+    vm = pl.BlockSpec(memory_space=pltpu.VMEM)
+    return pl.pallas_call(
+        finish_kernel,
+        out_shape=outs,
+        in_specs=[vm] * len(packed),
+        out_specs=(vm,) * len(outs),
+        name="finish",
+    )(*packed)
 
 
 def gathered_layer(tok, cot, mix, ow, uw, dw, mg, fb, ib, fg):
@@ -963,6 +1429,24 @@
             (forget_weight, input_gate_weight, candidate_weight),
             output_weight, up_weight, down_weight,
             mixer_gain, forget_bias, input_bias, feed_norm_gain,
+        )
+    if paired:
+        packed = exchange(
+            results[2:],
+            (
+                forget_weight, input_gate_weight, candidate_weight,
+                output_weight, up_weight, down_weight,
+                mixer_gain, forget_bias, input_bias, feed_norm_gain,
+            ),
+            (
+                mixer_second, forget_rows, forget_columns, input_rows, input_columns,
+                candidate_rows, candidate_columns, forget_second, input_second,
+                output_rows, output_columns, feed_second,
+                up_rows, up_columns, down_rows, down_columns,
+            ),
+        )
+        return (
+            results[0].reshape(tokens.shape), results[1].reshape(tokens.shape), *finish(packed)
         )
     block_output, tokens_grad, gmix, got, gup, gdt, fgg, mgg, fbg, ibg = results
     block_output = block_output.reshape(tokens.shape)

time: 898 us -> 231 us (0.26)
  waiting for transfers between devices: 490 us -> 0 us
  blocking collectives: 111 us -> 0 us
  Pallas kernels: 138 us -> 217 us
  local copies, waits for them, and re-layouts: 81.7 us -> 13 us
  between operations: 39.7 us -> 0.72 us
  other arithmetic: 35.1 us -> 0 us
    reduce_scatter x10 -> x0, waiting for transfers between devices: 291 us -> none  [the longest x1 48.9 us: body(): lax.psum_scatter(up_term, 'inner', scatter_dimension=1, tiled=True)]
    unnamed x22 -> x0, waiting for transfers between devices: 200 us -> none
    psum x3 -> x0, blocking collectives: 94 us -> none  [the longest x1 40.6 us: body(): lax.psum(jnp.stack([jnp.sum(s * s) for s in scaled_all]), ('grp', 'inner'))]
    pallas_call x0 -> x2, Pallas kernels: none -> 79 us  [the longest x1 76.1 us: exchange(): pl.pallas_call(exchange_kernel, out_shape=packed, in_specs=[vm] * len(arg...]
    reduce_sum x26 -> x0, other arithmetic: 27.1 us -> none  [the longest x10 14.7 us: body(): jnp.sum(s * s)]
    another operation x6 -> x0, local copies, waits for them, and re-layouts: 24.7 us -> none  [the longest x3 7.72 us: body(): split[:, :, :, k].reshape(width, hidden)]
    transpose x4 -> x0, local copies, waits for them, and re-layouts: 19.2 us -> none  [the longest x1 6.53 us: body(): split = gmix.transpose(1, 0, 2).reshape(width, Z, C // LANES, 3, LANES)]
    unnamed x146 -> x10, local copies, waits for them, and re-layouts: 29.8 us -> 13 us
  transfers between devices with their start and end apart: 16 -> 0, of which waited for: 16 -> 0; matrix products, arithmetic and copies ran while one was open for 5% -> 0% of each run, Pallas kernels for 0% -> 0%
where the time goes in v3:
time: 231 us; the launch traced here: 230 us
  Pallas kernels  217 us (94%)
  local copies, waits for them, and re-layouts  13 us (6%)
    pallas_call x1, Pallas kernels, layer_ag(): pl.pallas_call(layer_ag_kernel, out_shape=out_shape, in_specs=[vm] * 12,...  138 us
    pallas_call x1, Pallas kernels, exchange(): pl.pallas_call(exchange_kernel, out_shape=packed, in_specs=[vm] * len(arg...  76.1 us
    unnamed x10, local copies, waits for them, and re-layouts  13 us

profile of v3, /device:TPU:0, one launch (start us, length us, event | category | flops | bytes accessed | tf_op | source)
XLA Modules:
  0.0 230.3 jit_solution(572034076740615597)
XLA Ops:
  0.7 1.5 copy.67.args_5_.args_11_
  2.2 1.6 copy.68.args_7_.args_13_
  3.8 137.6 %layer_ag.1 = (bf16[1024,512]{1,0:T(8,128)(2,1)}, bf16[1024,512]{1,0:T(8,128)(2,1)}, f32[4,512,768]{2,1,0:T(8,128)}, f32[4,512,256]{2,1,0:T(8,128)}, f32[8,512,2...) custom-call(bf16[1024,512]{1,0:T(8,128)(2,1)} %bitcast.4, ...), custom_call_target="tpu_custom_call" | custom-call | tf_op jit(solution)/shard_map/layer_ag/pallas_call | solution.py:876
  141.4 76.1 %exchange.1 = (f32[128,384]{1,0:T(8,128)}, f32[64,256]{1,0:T(8,128)}, f32[128,256]{1,0:T(8,128)}, f32[64,512]{1,0:T(8,128)}, f32[128,384]{1,0:T(8,128)}, /*index...) custom-call(f32[4,512,768]{2,1,0:T(8,128)} %get-tuple-element.99.arg, ...), custom_call_target="tpu_custom_call" | custom-call | tf_op jit(solution)/shard_map/exchange/pallas_call | solution.py:1328
  217.5 0.0 copy-start
  217.5 2.8 %finish.1 = (f32[16]{0:T(128)}, f32[128,128]{1,0:T(8,128)}, f32[128,128]{1,0:T(8,128)}, f32[128,128]{1,0:T(8,128)}, f32[32]{0:T(128)}, /*index=5*/f32[32]{0:T(12...) custom-call(f32[128,384]{1,0:T(8,128)} %get-tuple-element.107.grad_m, ...), custom_call_target="tpu_custom_call" | custom-call | tf_op jit(solution)/shard_map/finish/pallas_call | solution.py:1350
  220.4 1.6 copy.71
  222.0 1.6 copy.73
  223.6 1.7 copy.72
  225.3 1.7 copy.74
  227.1 2.3 copy.77
  229.3 0.0 copy-done
  229.3 1.0 copy.78
Async XLA Ops:
  217.5 11.8 %copy-start = (bf16[1024,512]{1,0:T(8,128)(2,1)S(1)}, bf16[1024,512]{1,0:T(8,128)(2,1)}, u32[]{:S(2)}) copy-start(bf16[1024,512]{1,0:T(8,128)(2,1)} %get-tuple-element.98) | copy-start | bytes 3145732

commit v4 on v3

--- a/solution.py
+++ b/solution.py
@@ -54,6 +54,7 @@
 def strided(ref, j, n):
     return ref[pl.ds(j, SUB, stride=n), :]
 
+
 def gather_rows(tmp, j0, n, D):
     columns = [
         jnp.concatenate([tmp[q, pl.ds(j0 + jj, SUB, stride=n), :] for jj in range(16)], axis=0)
@@ -70,10 +71,30 @@
             ]
 
 
+def load_planes(ref, rows, start=0, count=None):
+    count = ref.shape[0] if count is None else count
+    return jnp.concatenate([ref[q, rows, :] for q in range(start, start + count)], axis=1)
+
+
+def store_planes(ref, rows, value, start=0):
+    for q in range(value.shape[1] // LANES):
+        ref[start + q, rows, :] = value[:, q * LANES : (q + 1) * LANES]
+
+
+def add_planes(ref, rows, value):
+    for q in range(value.shape[1] // LANES):
+        ref[q, rows, :] += value[:, q * LANES : (q + 1) * LANES]
+
+
+def clear(ref, T):
+    for q in range(4):
+        ref[q, 0:T, :] = jnp.zeros((T, LANES), F32)
+
+
 def norm_in(refs, T):
     n = T // SUB
-    tmp, xf, g1 = refs.pre, refs.xf, refs.g1
-    D = xf.shape[1]
+    tmp, g1 = refs.buf, refs.g1
+    D = g1.shape[1]
 
     def widen(i):
         rows = at(i, LANES)
@@ -87,7 +108,7 @@
         x = gather_rows(tmp, i * 16, n, D)
         y = x * lax.rsqrt(jnp.mean(x * x, axis=-1, keepdims=True) + EPS) * g1[...]
         rows = at(i, LANES)
-        xf[rows, :] = x
+        refs.tok_p[rows, :] = x.astype(BF16)
         refs.min[rows, :] = y.astype(BF16)
         refs.min_t[:, rows] = y.T.astype(BF16)
 
@@ -96,8 +117,8 @@
 
 def cot_in(refs, T):
     n = T // SUB
-    tmp = refs.pre
-    D = refs.xf.shape[1]
+    tmp = refs.buf
+    D = refs.g1.shape[1]
 
     def widen(i):
         rows = at(i, LANES)
@@ -117,7 +138,7 @@
 
 
 def mixer_forward(refs, z, T):
-    pre, ac, st = refs.pre, refs.buf_a, refs.st
+    pre, ac, st = refs.pre, refs.buf, refs.st
     halves = C // LANES
     width = 3 * LANES
 
@@ -168,7 +189,7 @@
                 a = kj * a
                 alist.append(a)
                 blist.append(b)
-            ac[pl.ds(r0, 64), lanes] = jnp.concatenate(alist, axis=0)
+            ac[h, pl.ds(r0, 64), :] = jnp.concatenate(alist, axis=0)
             st[z, pl.ds(r0 + SUB, 64), lanes] = jnp.concatenate(blist, axis=0)
             out.append((a, b))
         return tuple(out)
@@ -186,7 +207,7 @@
 
     def finish(i):
         r0 = pl.multiple_of(i * 64, 64)
-        a = ac[pl.ds(r0, 64), :].reshape(8, SUB, C)
+        a = load_planes(ac, pl.ds(r0, 64), 0, 2).reshape(8, SUB, C)
         b = st[z, pl.ds(r0 + SUB, 64), :].reshape(8, SUB, C)
         s = (b + a * first[None]).reshape(64, C)
         st[z, pl.ds(r0 + SUB, 64), :] = s
@@ -200,10 +221,10 @@
 
     def body(i):
         rows = at(i, 256)
-        acc = refs.xf[rows, :]
+        acc = refs.tok_p[rows, :].astype(F32)
         for z in range(Z):
             acc = acc + dot_t(refs.slow[z, rows, :], refs.wot[z])
-        refs.resid[rows, :] = acc
+        store_planes(refs.resid, rows, acc)
         for k in range(2):
             x = acc[k * LANES : (k + 1) * LANES]
             y = x * lax.rsqrt(jnp.mean(x * x, axis=-1, keepdims=True) + EPS) * refs.g2[...]
@@ -219,29 +240,29 @@
 
     def body(i):
         rows = at(i, 256)
-        refs.buf_a[rows, :] = dot(refs.fin[rows, :], wup[f])
-        refs.buf_b[rows, :] = dot(refs.cot_p[rows, :], wdt[f])
+        store_planes(refs.buf, rows, dot(refs.fin[rows, :], wup[f]))
+        store_planes(refs.buf, rows, dot(refs.cot_p[rows, :], wdt[f]), 2)
         for k in range(4):
             sub = pl.ds(pl.multiple_of(i * 256 + k * 64, 64), 64)
-            act, slope = gelu_parts(refs.buf_a[sub, :])
-            refs.act[sub, :] = act.astype(BF16)
-            refs.dup[sub, :] = (refs.buf_b[sub, :] * slope).astype(BF16)
-        refs.oacc[rows, :] += dot_t(refs.act[rows, :], wdt[f])
-        refs.dfe[rows, :] += dot_t(refs.dup[rows, :], wup[f])
+            act, slope = gelu_parts(load_planes(refs.buf, sub, 0, 2))
+            refs.dpre[sub, 0:C] = act.astype(BF16)
+            refs.dpre[sub, C : 2 * C] = (load_planes(refs.buf, sub, 2, 2) * slope).astype(BF16)
+        add_planes(refs.oacc, rows, dot_t(refs.dpre[rows, 0:C], wdt[f]))
+        refs.dfe[rows, :] += dot_t(refs.dpre[rows, C : 2 * C], wup[f])
 
     loop(T // 256, body)
 
 
 def feed_back(refs, T):
     n = T // SUB
-    tmp = refs.pre
-    D = refs.xf.shape[1]
+    tmp = refs.buf
+    D = refs.g1.shape[1]
 
     def body(i, total):
         rows = at(i, LANES)
-        x = refs.resid[rows, :]
+        x = load_planes(refs.resid, rows)
         df = refs.dfe[rows, :]
-        out = x + refs.oacc[rows, :]
+        out = x + load_planes(refs.oacc, rows, 0, D // LANES)
         scatter_rows(tmp, i * 16, n, out)
         r = lax.rsqrt(jnp.mean(x * x, axis=-1, keepdims=True) + EPS)
         nrm = x * r
@@ -265,20 +286,20 @@
 
 
 def mixer_back(refs, z, T):
-    ds, dc, st = refs.buf_a, refs.buf_b, refs.st
+    buf, st = refs.buf, refs.st
     halves = C // LANES
     width = 3 * LANES
 
     def project(i):
         rows = at(i, 256)
-        ds[rows, :] = dot(refs.fin[rows, :], refs.wot[z])
+        store_planes(buf, rows, dot(refs.fin[rows, :], refs.wot[z]))
 
     loop(T // 256, project)
     steps = T // 64
 
     def local(i, carry):
         r0 = pl.multiple_of((steps - 1 - i) * 64, 64)
-        d = ds[pl.ds(r0, 64), :]
+        d = load_planes(buf, pl.ds(r0, 64), 0, 2)
         k = refs.keep[z, pl.ds(r0, 64), :]
         e, dk = carry
         plist, dlist = [None] * 8, [None] * 8
@@ -289,8 +310,8 @@
             dlist[j] = dk
             e = kj * p
             dk = kj * dk
-        ds[pl.ds(r0, 64), :] = jnp.concatenate(plist, axis=0)
-        dc[pl.ds(r0, 64), :] = jnp.concatenate(dlist, axis=0)
+        store_planes(buf, pl.ds(r0, 64), jnp.concatenate(plist, axis=0))
+        store_planes(buf, pl.ds(r0, 64), jnp.concatenate(dlist, axis=0), 2)
         return e, dk
 
     e, dk = lax.fori_loop(0, steps, local, (jnp.zeros((SUB, C), F32), jnp.ones((SUB, C), F32)))
@@ -305,8 +326,8 @@
         for h in range(halves):
             lanes = slice(h * LANES, (h + 1) * LANES)
             sub = pl.ds(r0, 64)
-            p0 = ds[sub, lanes].reshape(8, SUB, LANES)
-            d0 = dc[sub, lanes].reshape(8, SUB, LANES)
+            p0 = buf[h, sub, :].reshape(8, SUB, LANES)
+            d0 = buf[2 + h, sub, :].reshape(8, SUB, LANES)
             p = (p0 + d0 * tail[None, :, lanes]).reshape(64, LANES)
             x = p * (st[z, pl.ds(r0 + SUB, 64), lanes] - st[z, sub, lanes])
             df = -(refs.k_f[z, sub, lanes] * x)
@@ -335,20 +356,20 @@
 
     def back(i):
         rows = at(i, 256)
-        refs.oacc[rows, :] += dot_t(refs.dpre[rows, :], refs.wmix[z])
+        add_planes(refs.oacc, rows, dot_t(refs.dpre[rows, :], refs.wmix[z]))
 
     loop(T // 256, back)
 
 
 def norm_back(refs, T):
     n = T // SUB
-    tmp = refs.pre
-    D = refs.xf.shape[1]
+    tmp = refs.buf
+    D = refs.g1.shape[1]
 
     def body(i, total):
         rows = at(i, LANES)
-        x = refs.xf[rows, :]
-        d_in = refs.oacc[rows, :]
+        x = refs.tok_p[rows, :].astype(F32)
+        d_in = load_planes(refs.oacc, rows, 0, D // LANES)
         r = lax.rsqrt(jnp.mean(x * x, axis=-1, keepdims=True) + EPS)
         nrm = x * r
         dn = d_in * refs.g1[...]
@@ -367,13 +388,14 @@
 
     loop(T // LANES, emit)
 
+
 class Refs:
     def __init__(self, args):
         (
             self.tok, self.cot, self.wmix, self.wot, self.wup, self.wdt, self.g1, self.g2, self.fb, self.ib,
             self.block, self.tgrad, self.gmix, self.got, self.gup, self.gdt, self.fgg, self.mgg, self.fbg, self.ibg,
-            self.xf, self.min, self.min_t, self.fin, self.fin_t, self.cot_p, self.cot_t, self.resid, self.oacc, self.dfe,
-            self.pre, self.buf_a, self.buf_b, self.act, self.dup, self.dpre, self.slow, self.st, self.keep, self.k_f,
+            self.tok_p, self.min, self.min_t, self.fin, self.fin_t, self.cot_p, self.cot_t, self.resid, self.oacc, self.dfe,
+            self.pre, self.buf, self.dpre, self.slow, self.st, self.keep, self.k_f,
             self.k_i, self.k_c, self.gst, self.gsem,
         ) = args
 
@@ -384,17 +406,17 @@
     Z = refs.wmix.shape[0]
     F = refs.wup.shape[0]
     gst, sem = refs.gst, refs.gsem
+    cot_in(refs, T)
     norm_in(refs, T)
     loop(Z, lambda z: mixer_forward(refs, z, T))
     mix_out(refs, T)
-    cot_in(refs, T)
-    refs.oacc[...] = jnp.zeros_like(refs.oacc)
+    clear(refs.oacc, T)
     refs.dfe[...] = jnp.zeros_like(refs.dfe)
 
     def feed_step(f):
         feed(refs, f, T)
-        gst[0, :, 0:C] = dot(refs.cot_t[...], refs.act[...])
-        gst[1, :, 0:C] = dot(refs.fin_t[...], refs.dup[...])
+        gst[0, :, 0:C] = dot(refs.cot_t[...], refs.dpre[:, 0:C])
+        gst[1, :, 0:C] = dot(refs.fin_t[...], refs.dpre[:, C : 2 * C])
         one = pltpu.make_async_copy(gst.at[0, :, 0:C], refs.gdt.at[f], sem.at[0])
         two = pltpu.make_async_copy(gst.at[1, :, 0:C], refs.gup.at[f], sem.at[1])
         one.start()
@@ -404,7 +426,7 @@
 
     loop(F, feed_step)
     feed_back(refs, T)
-    refs.oacc[...] = jnp.zeros_like(refs.oacc)
+    clear(refs.oacc, T)
 
     def mixer_step(z):
         gst[0, :, 0:C] = dot(refs.fin_t[...], refs.slow[z])
@@ -434,9 +456,9 @@
     )
     V = pltpu.VMEM
     scratch = [
-        V((T, D), F32), V((T, D), BF16), V((D, T), BF16), V((T, D), BF16), V((D, T), BF16),
-        V((T, D), BF16), V((D, T), BF16), V((T, D), F32), V((T, D), F32), V((T, D), F32),
-        V((3 * C // LANES, T, LANES), F32), V((T, C), F32), V((T, C), F32), V((T, C), BF16), V((T, C), BF16),
+        V((T, D), BF16), V((T, D), BF16), V((D, T), BF16), V((T, D), BF16), V((D, T), BF16),
+        V((T, D), BF16), V((D, T), BF16), V((D // LANES, T, LANES), F32),
+        V((D // LANES, T, LANES), F32), V((T, D), F32), V((3 * C // LANES, T, LANES), F32), V((4, T, LANES), F32),
         V((T, 3 * C), BF16), V((Z, T, C), BF16), V((Z, T + SUB, C), F32),
         V((Z, T, C), F32), V((Z, T, C), F32), V((Z, T, C), F32), V((Z, T, C), F32),
         V((2, D, 3 * C), F32), pltpu.SemaphoreType.DMA((2,)),
@@ -451,6 +473,7 @@
         name="layer",
     )(tok, cot, wmix, wot, wup, wdt, g1, g2, fb, ib)
 
+
 MESH = pl.DeviceIdType.MESH
 
 
@@ -535,20 +558,18 @@
 
 
 def gather_start(refs, p):
-    refs.o16[...] = refs.ow[...].astype(F32).T.astype(BF16)
-    refs.d16[...] = refs.dw[...].astype(F32).T.astype(BF16)
     local = []
     for k, w in enumerate((refs.fw, refs.iw, refs.cw)):
         spot = pl.ds(pl.multiple_of(p.c * 384 + k * 128, 128), 128)
         local.append(
             pltpu.make_async_copy(w, refs.wmix.at[p.z, at(p.g, 128), spot], refs.loc_s.at[k])
         )
-    local.append(pltpu.make_async_copy(refs.o16, block_of(refs, 0, p.g, p.i), refs.loc_s.at[3]))
+    local.append(pltpu.make_async_copy(refs.ow, block_of(refs, 0, p.g, p.i), refs.loc_s.at[3]))
     local.append(pltpu.make_async_copy(refs.uw, block_of(refs, 1, p.g, p.i), refs.loc_s.at[4]))
     for k in range(2):
         local.append(
             pltpu.make_async_copy(
-                refs.d16.at[:, k * 256 : (k + 1) * 256],
+                refs.dw.at[:, k * 256 : (k + 1) * 256],
                 refs.wdt.at[2 * p.g + k, at(p.i, 64), :],
                 refs.loc_s.at[5 + k],
             )
@@ -760,130 +781,6 @@
     feed_last(refs, p)
     feed_drain(refs, p)
 
-class GatherRefs:
-    def __init__(self, args):
-        (
-            self.tok, self.cot, self.fw, self.iw, self.cw, self.ow, self.uw, self.dw,
-            self.mg, self.fbv, self.ibv, self.fg,
-            self.block, self.tgrad, self.gmix, self.got, self.gup, self.gdt,
-            self.fgg, self.mgg, self.fbg, self.ibg,
-            self.wmix, self.wot, self.wup, self.wdt, self.g1, self.g2, self.fb, self.ib,
-            self.vecs, self.vstage, self.o16, self.d16,
-            self.xf, self.min, self.min_t, self.fin, self.fin_t, self.cot_p, self.cot_t,
-            self.resid, self.oacc, self.dfe,
-            self.pre, self.buf_a, self.buf_b, self.act, self.dup, self.dpre,
-            self.slow, self.st, self.keep, self.k_f, self.k_i, self.k_c, self.gsem,
-            self.loc_s, self.mxg_s, self.mxg_r, self.mxu_s, self.mxd_s, self.mxz_r,
-            self.mxp_s, self.mxp_r, self.vec_s, self.vec_r, self.ffz_s, self.ffz_r,
-            self.ff2_s, self.ff2_r, self.ff3_s, self.ff3_r, self.ffp_s, self.ffp_r,
-        ) = args
-
-
-def grad_slot(refs, k, D):
-    return refs.pre.at[:, k * D : (k + 1) * D, :]
-
-
-def put_grad(refs, k, value):
-    D = value.shape[0]
-    for q in range(value.shape[1] // LANES):
-        refs.pre[q, k * D : (k + 1) * D, :] = value[:, q * LANES : (q + 1) * LANES]
-
-
-def send_grad(refs, k, D, width, out, sem):
-    return [
-        pltpu.make_async_copy(
-            refs.pre.at[q, k * D : (k + 1) * D, :],
-            out.at[:, q * LANES : (q + 1) * LANES],
-            sem.at[q],
-        )
-        for q in range(width // LANES)
-    ]
-
-
-def layer_ag_kernel(*args):
-    refs = GatherRefs(args)
-    T, D = refs.tok.shape
-    Z = refs.wmix.shape[0]
-    F = refs.wup.shape[0]
-    p = Place()
-    gather_start(refs, p)
-    cot_in(refs, T)
-    gather_vectors(refs, p)
-    norm_in(refs, T)
-    mixer_slots(refs, p, T)
-    mix_out(refs, T)
-    refs.oacc[...] = jnp.zeros_like(refs.oacc)
-    refs.dfe[...] = jnp.zeros_like(refs.dfe)
-
-    def feed_step(f):
-        feed(refs, f, T)
-        put_grad(refs, 0, dot(refs.cot_t[...], refs.act[...]))
-        put_grad(refs, 1, dot(refs.fin_t[...], refs.dup[...]))
-        copies = send_grad(refs, 0, D, C, refs.gdt.at[f], refs.gsem.at[0])
-        copies += send_grad(refs, 1, D, C, refs.gup.at[f], refs.gsem.at[1])
-        for c in copies:
-            c.start()
-        for c in copies:
-            c.wait()
-
-    loop(F, feed_step)
-    feed_back(refs, T)
-    refs.oacc[...] = jnp.zeros_like(refs.oacc)
-
-    def mixer_step(z):
-        put_grad(refs, 0, dot(refs.fin_t[...], refs.slow[z]))
-        mixer_back(refs, z, T)
-        put_grad(refs, 1, dot(refs.min_t[...], refs.dpre[...]))
-        copies = send_grad(refs, 0, D, C, refs.got.at[z], refs.gsem.at[0])
-        copies += send_grad(refs, 1, D, 3 * C, refs.gmix.at[z], refs.gsem.at[1])
-        for c in copies:
-            c.start()
-        for c in copies:
-            c.wait()
-
-    loop(Z, mixer_step)
-    norm_back(refs, T)
-
-
-def layer_ag(tok, cot, fw, iw, cw, ow, uw, dw, mg, fb, ib, fg):
-    T, D = tok.shape
-    Z, F = 4, 8
-    sds = jax.ShapeDtypeStruct
-    vm = pl.BlockSpec(memory_space=pltpu.VMEM)
-    anyspec = pl.BlockSpec(memory_space=pl.ANY)
-    out_shape = (
-        sds((T, D), BF16), sds((T, D), BF16),
-        sds((Z, D, 3 * C), F32), sds((Z, D, C), F32), sds((F, D, C), F32), sds((F, D, C), F32),
-        sds((1, D), F32), sds((1, D), F32), sds((Z, 1, C), F32), sds((Z, 1, C), F32),
-    )
-    V = pltpu.VMEM
-    S = pltpu.SemaphoreType.DMA
-    scratch = [
-        V((Z, D, 3 * C), BF16), V((Z, D, C), BF16), V((F, D, C), BF16), V((F, D, C), BF16),
-        V((1, D), F32), V((1, D), F32), V((Z, 1, C), F32), V((Z, 1, C), F32),
-        V((32, 1, LANES), F32), V((1, LANES), F32), V((64, C), BF16), V((64, 2 * C), BF16),
-        V((T, D), F32), V((T, D), BF16), V((D, T), BF16), V((T, D), BF16), V((D, T), BF16),
-        V((T, D), BF16), V((D, T), BF16), V((T, D), F32), V((T, D), F32), V((T, D), F32),
-        V((3 * C // LANES, T, LANES), F32), V((T, C), F32), V((T, C), F32),
-        V((T, C), BF16), V((T, C), BF16),
-        V((T, 3 * C), BF16), V((Z, T, C), BF16), V((Z, T + SUB, C), F32),
-        V((Z, T, C), F32), V((Z, T, C), F32), V((Z, T, C), F32), V((Z, T, C), F32),
-        S((2, 6)),
-        S((7,)), S((3,)), S((3,)), S((4,)), S((4,)), S((4,)),
-        S((4,)), S((4,)), S(()), S(()), S((3, 3)), S((3, 4)),
-        S((3, 4)), S((3, 4)), S((3, 4, 2)), S((3, 4, 2)), S((3, 4)), S((3, 4)),
-    ]
-    return pl.pallas_call(
-        layer_ag_kernel,
-        out_shape=out_shape,
-        in_specs=[vm] * 12,
-        out_specs=(vm, vm, anyspec, anyspec, anyspec, anyspec, vm, vm, vm, vm),
-        scratch_shapes=scratch,
-        compiler_params=pltpu.CompilerParams(
-            vmem_limit_bytes=67043328, collective_id=0, has_side_effects=True
-        ),
-        name="layer_ag",
-    )(tok, cot, fw, iw, cw, ow, uw, dw, mg, fb, ib, fg)
 
 SHAPES = ((128, 256), (128, 256), (128, 384), (64, 256))
 UP, DOWN, MIX, OUT = 0, 1, 2, 3
@@ -897,65 +794,109 @@
 COUNTS = (512, 524288, 524288, 524288, 1024, 1024, 524288, 512, 1048576, 1048576)
 
 
-def piece(refs, a, g, z, c):
-    i = z * 2 + c
-    if a == UP:
-        return refs.gup[i, g * 128 : (g + 1) * 128, :]
-    if a == DOWN:
-        return jnp.concatenate([refs.gdt[2 * g + h, at(i, 64), :] for h in range(2)], axis=0)
-    if a == MIX:
-        return refs.gmix[z, g * 128 : (g + 1) * 128, at(c, 384)]
-    return refs.got[g, at(i, 64), :]
-
-
-def rs_fill(refs, p, a, z):
-    for g in range(4):
-        refs.psend[a][z, g] = piece(refs, a, g, z, 1 - p.c).astype(BF16)
-
-
-def rs_copy(refs, p, stage, a, z):
-    if stage == 0:
-        src, dst, dev = refs.psend[a].at[z], refs.precv[a].at[z], p.partner
-    elif stage == 1:
-        src, dst, dev = refs.buf1[a].at[z, 1], refs.r1[a].at[z], (p.near(z), p.i)
+def spot(a, g, z):
+    return (g, z) if a == DOWN else (z, g)
+
+
+def rs_store(refs, a, g, z, value):
+    refs.psend[a][(*spot(a, g, z),)] = value.astype(BF16)
+
+
+def rs_role(p, g, z):
+    e = z % 2
+    y, x = g // 2, g % 2
+    return (1 - e) * ((x + p.x) % 2) + e * ((y + p.y) % 2)
+
+
+def rs_pair(refs, p, a, u):
+    if a == OUT:
+        src, dst = refs.psend[a], refs.precv[a]
     else:
-        src, dst, dev = refs.buf2[a].at[z, 1], refs.r2[a].at[z], (p.far(z), p.i)
-    return rcopy(src, dst, refs.rs_s.at[stage, a, z], refs.rs_r.at[stage, a, z], dev)
-
-
-def rs_first(refs, p, a, z):
-    rs_copy(refs, p, 0, a, z).wait_recv()
+        src, dst = refs.psend[a].at[u], refs.precv[a].at[u]
+    return rcopy(src, dst, refs.rp_s.at[a, u], refs.rp_r.at[a, u], p.partner)
+
+
+def rs_merge(refs, p, a, g, z, own):
+    place = spot(a, g, z)
+    v = own + refs.precv[a][place].astype(F32)
+    role = rs_role(p, g, z)
+
+    @pl.when(role == 1)
+    def _():
+        refs.psend[a][place] = v.astype(BF16)
+
+    @pl.when(role == 0)
+    def _():
+        refs.precv[a][place] = v.astype(BF16)
+
+
+def rs_group(p, z, k, sent):
     e = z % 2
-    for g in range(4):
-        y, x = g // 2, g % 2
-        v = piece(refs, a, g, z, p.c) + refs.precv[a][z, g].astype(F32)
-        role = (1 - e) * ((x + p.x) % 2) + e * ((y + p.y) % 2)
-        refs.buf1[a][z, role, (1 - e) * y + e * x] = v.astype(BF16)
+    x = (1 - e) * ((p.x + sent) % 2) + e * k
+    y = (1 - e) * k + e * ((p.y + sent) % 2)
+    return y * 2 + x
+
+
+def rs_first_copy(refs, p, a, z, k):
+    g = rs_group(p, z, k, 1)
+    return rcopy(
+        refs.psend[a].at[spot(a, g, z)], refs.r1[a].at[z, k],
+        refs.r1_s.at[a, z, k], refs.r1_r.at[a, z, k], (p.near(z), p.i),
+    )
+
+
+def rs_first_send(refs, p, a, z):
+    for k in range(2):
+        rs_first_copy(refs, p, a, z, k).start()
 
 
 def rs_second(refs, p, a, z):
-    rs_copy(refs, p, 1, a, z).wait_recv()
     e = z % 2
+    mine = (1 - e) * p.y + e * p.x
     for k in range(2):
-        v = refs.buf1[a][z, 0, k].astype(F32) + refs.r1[a][z, k].astype(F32)
-        refs.buf2[a][z, (k + (1 - e) * p.y + e * p.x) % 2] = v.astype(BF16)
+        rs_first_copy(refs, p, a, z, k).wait_recv()
+    for k in range(2):
+        place = spot(a, rs_group(p, z, k, 0), z)
+        v = (refs.precv[a][place].astype(F32) + refs.r1[a][z, k].astype(F32)).astype(BF16)
+
+        @pl.when(mine == k)
+        def _():
+            refs.precv[a][place] = v
+
+        @pl.when(mine != k)
+        def _():
+            refs.psend[a][place] = v
+
+
+def rs_second_copy(refs, p, a, z):
+    e = z % 2
+    other = 1 - ((1 - e) * p.y + e * p.x)
+    place = spot(a, rs_group(p, z, other, 0), z)
+    return rcopy(
+        refs.psend[a].at[place], refs.r2[a].at[z], refs.r2_s.at[a, z], refs.r2_r.at[a, z],
+        (p.far(z), p.i),
+    )
+
+
+def rs_third(refs, p, a, z):
+    rs_second_copy(refs, p, a, z).wait_recv()
+    place = spot(a, p.g, z)
+    v = refs.precv[a][place].astype(F32) + refs.r2[a][z].astype(F32)
+
+    @pl.when(z == p.z)
+    def _():
+        refs.fin_g[a][...] = v
+
+    @pl.when(z != p.z)
+    def _():
+        refs.psend[a][place] = v.astype(BF16)
 
 
 def rs_line(refs, p, a, z, owner):
     return rcopy(
-        refs.buf3[a].at[z], refs.r3[a].at[owner], refs.r3_s.at[a, z], refs.r3_r.at[a, owner],
-        (p.g, z * 2 + p.c),
+        refs.psend[a].at[spot(a, p.g, z)], refs.r3[a].at[owner],
+        refs.r3_s.at[a, z], refs.r3_r.at[a, owner], (p.g, z * 2 + p.c),
     )
-
-
-def rs_third(refs, p, a, z):
-    rs_copy(refs, p, 2, a, z).wait_recv()
-    v = refs.buf2[a][z, 0].astype(F32) + refs.r2[a][z].astype(F32)
-    refs.buf3[a][z] = v.astype(BF16)
-
-    @pl.when(z == p.z)
-    def _():
-        refs.fin[a][...] = v
 
 
 def rs_third_send(refs, p, a, z):
@@ -968,14 +909,15 @@
     for k in range(1, 4):
         z = (p.z + k) % 4
         rs_line(refs, p, a, z, z).wait_recv()
-        refs.fin[a][...] += refs.r3[a][z].astype(F32)
+        refs.fin_g[a][...] += refs.r3[a][z].astype(F32)
 
 
 def rs_drain(refs, p):
     def one(z):
         for a in range(4):
-            for stage in range(3):
-                rs_copy(refs, p, stage, a, z).wait_send()
+            for k in range(2):
+                rs_first_copy(refs, p, a, z, k).wait_send()
+            rs_second_copy(refs, p, a, z).wait_send()
 
             @pl.when(z != p.z)
             def _():
@@ -1042,7 +984,7 @@
 def parameter_blocks(refs):
     return [
         refs.fw[...].astype(F32), refs.iw[...].astype(F32), refs.cw[...].astype(F32),
-        refs.ow[...].astype(F32).T, refs.uw[...].astype(F32), refs.dw[...].astype(F32).T,
+        refs.ow[...].astype(F32), refs.uw[...].astype(F32), refs.dw[...].astype(F32),
     ]
 
 
@@ -1095,10 +1037,10 @@
 
 
 def gradient_blocks(refs):
-    mix = refs.fin[MIX][...]
-    down = refs.fin[DOWN][...]
+    mix = refs.fin_g[MIX][...]
+    down = refs.fin_g[DOWN][...]
     return [
-        mix[:, 0:128], mix[:, 128:256], mix[:, 256:384], refs.fin[OUT][...], refs.fin[UP][...],
+        mix[:, 0:128], mix[:, 128:256], mix[:, 256:384], refs.fin_g[OUT][...], refs.fin_g[UP][...],
         jnp.concatenate([down[0:64], down[64:128]], axis=1),
     ]
 
@@ -1195,7 +1137,7 @@
         for k in range(10)
     ]
     fresh = [w + steps[slot] * s for slot, w, s in zip(MATRIX_SLOTS, weights, scaled)]
-    refs.grad_mix[...] = refs.fin[MIX][...]
+    refs.grad_mix[...] = refs.fin_g[MIX][...]
     refs.grad_out[...] = grads[3]
     refs.grad_up[...] = grads[4]
     refs.grad_down[...] = grads[5]
@@ -1214,58 +1156,6 @@
     )
 
 
-class ExchangeRefs:
-    def __init__(self, args):
-        (
-            self.gmix, self.got, self.gup, self.gdt, self.fgg, self.mgg, self.fbg, self.ibg,
-            self.fw, self.iw, self.cw, self.ow, self.uw, self.dw,
-            self.mg, self.fbv, self.ibv, self.fg,
-            self.sec_m, self.row_f, self.col_f, self.row_i, self.col_i, self.row_c, self.col_c,
-            self.sec_f, self.sec_i, self.row_o, self.col_o, self.sec_g,
-            self.row_u, self.col_u, self.row_d, self.col_d,
-            self.grad_mix, self.grad_out, self.grad_up, self.grad_down,
-            self.new_mix, self.new_out, self.new_up, self.new_down,
-            self.vectors, self.rows_out, self.columns_out,
-        ) = args[:45]
-        rest = list(args[45:])
-        take = lambda n: [rest.pop(0) for _ in range(n)]
-        self.psend, self.precv, self.buf1, self.r1 = take(4), take(4), take(4), take(4)
-        self.buf2, self.r2, self.buf3, self.r3, self.fin = (
-            take(4), take(4), take(4), take(4), take(4)
-        )
-        (
-            self.vout, self.vin, self.rowst, self.rowin, self.colst, self.colin,
-            self.scal, self.scin, self.clip, self.clin,
-            self.rs_s, self.rs_r, self.r3_s, self.r3_r, self.vex_s, self.vex_r,
-            self.row_s, self.row_r, self.col_s, self.col_r, self.sc_s, self.sc_r,
-            self.cl_s, self.cl_r,
-        ) = rest
-
-
-def exchange_kernel(*args):
-    refs = ExchangeRefs(args)
-    p = Place()
-    entry_barrier(p)
-    arrays = (UP, DOWN, OUT, MIX)
-    for a in arrays:
-        loop(4, lambda z: rs_fill(refs, p, a, z))
-        loop(4, lambda z: rs_copy(refs, p, 0, a, z).start())
-    vector_exchange(refs, p)
-    for a in arrays:
-        loop(4, lambda z: rs_first(refs, p, a, z))
-        loop(4, lambda z: rs_copy(refs, p, 1, a, z).start())
-    for a in arrays:
-        loop(4, lambda z: rs_second(refs, p, a, z))
-        loop(4, lambda z: rs_copy(refs, p, 2, a, z).start())
-    for a in arrays:
-        loop(4, lambda z: rs_third(refs, p, a, z))
-        loop(4, lambda z: rs_third_send(refs, p, a, z))
-    for a in arrays:
-        rs_last(refs, p, a)
-    rs_drain(refs, p)
-    adafactor(refs, p)
-
-
 def finish_kernel(
     grad_mix, grad_out, grad_up, grad_down, new_mix, new_out, new_up, new_down,
     vectors, rows, columns,
@@ -1277,7 +1167,7 @@
         for k, o in enumerate(outs):
             o[...] = src[:, k * 128 : (k + 1) * 128]
     for src, o in ((grad_out, g_o), (new_out, n_o), (grad_down, g_d), (new_down, n_d)):
-        o[...] = src[...].T
+        o[...] = src[...]
     g_u[...] = grad_up[...]
     n_u[...] = new_up[...]
     for row, outs in (
@@ -1298,51 +1188,11 @@
                     o[(k - a) * LANES : (k - a + 1) * LANES] = src[k, :]
 
 
-def exchange(grads, shards, states):
-    sds = jax.ShapeDtypeStruct
-    vm = pl.BlockSpec(memory_space=pltpu.VMEM)
-    V = pltpu.VMEM
-    S = pltpu.SemaphoreType.DMA
-    packed = (
-        sds((128, 384), F32), sds((64, 256), F32), sds((128, 256), F32), sds((64, 512), F32),
-        sds((128, 384), F32), sds((64, 256), F32), sds((128, 256), F32), sds((64, 512), F32),
-        sds((8, LANES), F32), sds((16, LANES), F32), sds((8, LANES), F32),
-    )
-    scratch = (
-        [V((4, 4) + s, BF16) for s in SHAPES] * 2
-        + [V((4, 2, 2) + s, BF16) for s in SHAPES]
-        + [V((4, 2) + s, BF16) for s in SHAPES]
-        + [V((4, 2) + s, BF16) for s in SHAPES]
-        + [V((4,) + s, BF16) for s in SHAPES] * 3
-        + [V(s, F32) for s in SHAPES]
-    )
-    row = V((1, LANES), F32)
-    box = V((32, 1, LANES), F32)
-    scratch += [
-        box, box, V((16, LANES), F32), V((8, 16, LANES), F32),
-        V((8, LANES), F32), V((4, 8, LANES), F32), row, box, row, box,
-        S((3, 4, 4)), S((3, 4, 4)), S((4, 4)), S((4, 4)), S(()), S(()),
-        S((7,)), S((7,)), S((3,)), S((3,)), S(()), S(()), S(()), S(()),
-    ]
-    args = (*grads, *shards, *states)
-    return pl.pallas_call(
-        exchange_kernel,
-        out_shape=packed,
-        in_specs=[vm] * len(args),
-        out_specs=(vm,) * len(packed),
-        scratch_shapes=scratch,
-        compiler_params=pltpu.CompilerParams(
-            vmem_limit_bytes=67043328, collective_id=1, has_side_effects=True
-        ),
-        name="exchange",
-    )(*args)
-
-
 def finish(packed):
     sds = jax.ShapeDtypeStruct
     f = lambda *s: sds(s, F32)
-    block = [f(16), f(128, 128), f(128, 128), f(128, 128), f(32), f(32), f(256, 64), f(16),
-             f(128, 256), f(512, 64)]
+    block = [f(16), f(128, 128), f(128, 128), f(128, 128), f(32), f(32), f(64, 256), f(16),
+             f(128, 256), f(64, 512)]
     states = [f(16), f(128), f(128), f(128), f(128), f(128), f(128), f(32), f(32), f(256), f(64),
               f(16), f(128), f(256), f(512), f(64)]
     outs = tuple(block + block + states + [f(10)])
@@ -1354,6 +1204,343 @@
         out_specs=(vm,) * len(outs),
         name="finish",
     )(*packed)
+
+
+class FusedRefs:
+    def __init__(self, args):
+        (
+            self.tok_in, self.cot_in, self.fw, self.iw, self.cw, self.ow, self.uw, self.dw,
+            self.mg, self.fbv, self.ibv, self.fg,
+            self.sec_m, self.row_f, self.col_f, self.row_i, self.col_i, self.row_c, self.col_c,
+            self.sec_f, self.sec_i, self.row_o, self.col_o, self.sec_g,
+            self.row_u, self.col_u, self.row_d, self.col_d,
+            self.block_out, self.tgrad_out,
+            self.grad_mix, self.grad_out, self.grad_up, self.grad_down,
+            self.new_mix, self.new_out, self.new_up, self.new_down,
+            self.vectors, self.rows_out, self.columns_out,
+            self.wmix, self.wot, self.wup, self.wdt, self.g1, self.g2, self.fb, self.ib,
+            self.vecs, self.vstage, self.fgg, self.mgg, self.fbg, self.ibg,
+            self.tok_p, self.fin, self.min_t, self.fin_t, self.cot_p, self.cot_t,
+            self.resid, self.dfe,
+            self.pre, self.buf, self.dpre, self.slow, self.st,
+            self.keep, self.k_f, self.k_i, self.k_c,
+            self.loc_s, self.mxg_s, self.mxg_r, self.mxu_s, self.mxd_s, self.mxz_r,
+            self.mxp_s, self.mxp_r, self.vec_s, self.vec_r, self.ffz_s, self.ffz_r,
+            self.ff2_s, self.ff2_r, self.ff3_s, self.ff3_r, self.ffp_s, self.ffp_r,
+            self.vout, self.vin, self.rowst, self.rowin, self.colst, self.colin,
+            self.scal, self.scin, self.clip, self.clin,
+            self.rp_s, self.rp_r, self.r1_s, self.r1_r, self.r2_s, self.r2_r,
+            self.r3_s, self.r3_r, self.vex_s, self.vex_r,
+            self.row_s, self.row_r, self.col_s, self.col_r, self.sc_s, self.sc_r,
+            self.cl_s, self.cl_r, self.io_s,
+        ) = args[:119]
+        rest = list(args[119:])
+        self.psend, self.precv, self.r1, self.r2, self.r3, self.fin_g = (
+            rest[4 * k : 4 * k + 4] for k in range(6)
+        )
+        self.io = self.dpre.at[:, 0:512]
+        self.oacc = self.pre.at[pl.ds(4, 4)]
+        self.tok = self.cot = self.block = self.tgrad = self.io
+        self.min = self.fin
+
+
+def halves_of(refs, plane, rows):
+    size = rows.size
+    low = refs.pre[plane, rows, :]
+    high = refs.pre[plane, pl.ds(rows.start + 512, size), :]
+    return jnp.concatenate([low, high], axis=1)
+
+
+def put_halves(refs, plane, value):
+    refs.pre[plane, 0:512, :] = value[:, 0:LANES]
+    refs.pre[plane, 512:1024, :] = value[:, LANES : 2 * LANES]
+
+
+def line_rows(z, c):
+    return pl.ds(pl.multiple_of((z * 2 + c) * 64, 64), 64)
+
+
+def put_feed_grads(refs, p, f):
+    z, h = f // 2, f % 2
+    up = dot(refs.fin_t[...], refs.dpre[:, C : 2 * C])
+
+    @pl.when(h == p.c)
+    def _():
+        put_halves(refs, 0, up)
+
+    @pl.when(h != p.c)
+    def _():
+        for g in range(4):
+            refs.psend[UP][z, g] = up[g * 128 : (g + 1) * 128].astype(BF16)
+
+    put_halves(refs, 1 + h, dot(refs.cot_t[...], refs.dpre[:, 0:C]))
+    half = pl.ds(pl.multiple_of(h * 64, 64), 64)
+    for zz in range(4):
+        part = halves_of(refs, 1 + h, line_rows(zz, 1 - p.c))
+        refs.psend[DOWN][z, zz, half, :] = part.astype(BF16)
+
+
+def merge_up(refs, p, z):
+    rs_pair(refs, p, UP, z).wait()
+    for g in range(4):
+        rs_merge(refs, p, UP, g, z, halves_of(refs, 0, pl.ds(g * 128, 128)))
+
+
+def merge_down(refs, p, g):
+    rs_pair(refs, p, DOWN, g).wait()
+    for z in range(4):
+        own = jnp.concatenate(
+            [halves_of(refs, 1 + h, line_rows(z, p.c)) for h in range(2)], axis=0
+        )
+        rs_merge_at(refs, p, DOWN, g, z, own)
+
+
+def rs_merge_at(refs, p, a, g, z, own):
+    e = z % 2
+    y, x = g // 2, g % 2
+    role = (1 - e) * ((x + p.x) % 2) + e * ((y + p.y) % 2)
+    place = spot(a, g, z)
+    v = (own + refs.precv[a][place].astype(F32)).astype(BF16)
+
+    @pl.when(role == 1)
+    def _():
+        refs.psend[a][place] = v
+
+    @pl.when(role == 0)
+    def _():
+        refs.precv[a][place] = v
+
+
+def put_out_grads(refs, p):
+    def one(g):
+        put_halves(refs, g, dot(refs.fin_t[...], refs.slow[g]))
+        for z in range(4):
+            part = halves_of(refs, g, line_rows(z, 1 - p.c))
+            refs.psend[OUT][z, g] = part.astype(BF16)
+
+    loop(4, one)
+
+
+def merge_out(refs, p):
+    rs_pair(refs, p, OUT, 0).wait()
+
+    def one(z):
+        for g in range(4):
+            rs_merge(refs, p, OUT, g, z, halves_of(refs, g, line_rows(z, p.c)))
+
+    loop(4, one)
+
+
+def mix_part(refs, g, c):
+    cols = []
+    for j in range(3):
+        q = 3 * c + j
+        rows = pl.ds(pl.multiple_of((q % 2) * 512 + g * 128, 128), 128)
+        cols.append(refs.pre[q // 2, rows, :])
+    return jnp.concatenate(cols, axis=1)
+
+
+def put_mix_grads(refs, p, z):
+    for j in range(3):
+        put_halves(refs, j, dot(refs.min_t[...], refs.dpre[:, j * C : (j + 1) * C]))
+    for g in range(4):
+        refs.psend[MIX][z, g] = mix_part(refs, g, 1 - p.c).astype(BF16)
+
+
+def merge_mix(refs, p, z):
+    rs_pair(refs, p, MIX, z).wait()
+    for g in range(4):
+        rs_merge(refs, p, MIX, g, z, mix_part(refs, g, p.c))
+
+
+def all_z(body):
+    loop(4, body)
+
+
+def second(refs, p, a, z):
+    rs_second(refs, p, a, z)
+    rs_second_copy(refs, p, a, z).start()
+
+
+def third(refs, p, a, z):
+    rs_third(refs, p, a, z)
+    rs_third_send(refs, p, a, z)
+
+
+def feed_tick(refs, p, f):
+    @pl.when((f % 2 == 0) & (f >= 2))
+    def _():
+        merge_up(refs, p, f // 2 - 1)
+        merge_down(refs, p, f // 2 - 1)
+        rs_first_send(refs, p, UP, f // 2 - 1)
+
+    @pl.when((f % 2 == 0) & (f >= 4))
+    def _():
+        second(refs, p, UP, f // 2 - 2)
+
+    @pl.when((f % 2 == 0) & (f >= 6))
+    def _():
+        third(refs, p, UP, f // 2 - 3)
+
+
+def fused_kernel(*args):
+    refs = FusedRefs(args)
+    refs.fin_grad = refs.fin_g
+    T, D = refs.tok_p.shape
+    p = Place()
+    load = pltpu.make_async_copy(refs.cot_in, refs.io, refs.io_s)
+    load.start()
+    gather_start(refs, p)
+    load.wait()
+    cot_in(refs, T)
+    load = pltpu.make_async_copy(refs.tok_in, refs.io, refs.io_s)
+    load.start()
+    gather_vectors(refs, p)
+    load.wait()
+    norm_in(refs, T)
+    mixer_slots(refs, p, T)
+    mix_out(refs, T)
+    clear(refs.oacc, T)
+    refs.dfe[...] = jnp.zeros_like(refs.dfe)
+
+    def feed_step(f):
+        feed(refs, f, T)
+        feed_tick(refs, p, f)
+        put_feed_grads(refs, p, f)
+
+        @pl.when(f % 2 == 1)
+        def _():
+            rs_pair(refs, p, UP, f // 2).start()
+            rs_pair(refs, p, DOWN, f // 2).start()
+
+    loop(8, feed_step)
+    feed_back(refs, T)
+    store = pltpu.make_async_copy(refs.io, refs.block_out, refs.io_s)
+    store.start()
+    merge_up(refs, p, 3)
+    merge_down(refs, p, 3)
+    rs_first_send(refs, p, UP, 3)
+    all_z(lambda z: rs_first_send(refs, p, DOWN, z))
+    second(refs, p, UP, 2)
+    third(refs, p, UP, 1)
+    put_out_grads(refs, p)
+    rs_pair(refs, p, OUT, 0).start()
+    clear(refs.oacc, T)
+    store.wait()
+
+    def chunk(n):
+        return (p.z + 1 + n) % 4
+
+    def mixer_step(n):
+        z = chunk(n)
+        mixer_back(refs, z, T)
+
+        @pl.when(n == 0)
+        def _():
+            merge_out(refs, p)
+            all_z(lambda z: rs_first_send(refs, p, OUT, z))
+            all_z(lambda z: second(refs, p, DOWN, z))
+            second(refs, p, UP, 3)
+            third(refs, p, UP, 2)
+
+        @pl.when(n >= 1)
+        def _():
+            merge_mix(refs, p, chunk(n - 1))
+            rs_first_send(refs, p, MIX, chunk(n - 1))
+
+        @pl.when(n == 1)
+        def _():
+            all_z(lambda z: second(refs, p, OUT, z))
+            all_z(lambda z: third(refs, p, DOWN, z))
+            third(refs, p, UP, 3)
+
+        @pl.when(n >= 2)
+        def _():
+            second(refs, p, MIX, chunk(n - 2))
+
+        @pl.when(n == 2)
+        def _():
+            all_z(lambda z: third(refs, p, OUT, z))
+
+        @pl.when(n == 3)
+        def _():
+            third(refs, p, MIX, chunk(0))
+
+        put_mix_grads(refs, p, z)
+        rs_pair(refs, p, MIX, z).start()
+
+    loop(4, mixer_step)
+    norm_back(refs, T)
+    store = pltpu.make_async_copy(refs.io, refs.tgrad_out, refs.io_s)
+    store.start()
+    merge_mix(refs, p, chunk(3))
+    rs_first_send(refs, p, MIX, chunk(3))
+    vector_exchange(refs, p)
+    second(refs, p, MIX, chunk(2))
+    third(refs, p, MIX, chunk(1))
+    for a in (UP, DOWN, OUT):
+        rs_last(refs, p, a)
+    second(refs, p, MIX, chunk(3))
+    third(refs, p, MIX, chunk(2))
+    third(refs, p, MIX, chunk(3))
+    rs_last(refs, p, MIX)
+    rs_drain(refs, p)
+    adafactor(refs, p)
+    store.wait()
+
+
+def fused(*args):
+    T, D = args[0].shape
+    Z, F = 4, 8
+    sds = jax.ShapeDtypeStruct
+    vm = pl.BlockSpec(memory_space=pltpu.VMEM)
+    anyspec = pl.BlockSpec(memory_space=pl.ANY)
+    V = pltpu.VMEM
+    S = pltpu.SemaphoreType.DMA
+    outs = (
+        sds((T, D), BF16), sds((T, D), BF16),
+        sds((128, 384), F32), sds((64, 256), F32), sds((128, 256), F32), sds((64, 512), F32),
+        sds((128, 384), F32), sds((64, 256), F32), sds((128, 256), F32), sds((64, 512), F32),
+        sds((8, LANES), F32), sds((16, LANES), F32), sds((8, LANES), F32),
+    )
+    row = V((1, LANES), F32)
+    box = V((32, 1, LANES), F32)
+    scratch = [
+        V((Z, D, 3 * C), BF16), V((Z, D, C), BF16), V((F, D, C), BF16), V((F, D, C), BF16),
+        V((1, D), F32), V((1, D), F32), V((Z, 1, C), F32), V((Z, 1, C), F32),
+        box, row, V((1, D), F32), V((1, D), F32), V((Z, 1, C), F32), V((Z, 1, C), F32),
+        V((T, D), BF16), V((T, D), BF16), V((D, T), BF16), V((D, T), BF16),
+        V((T, D), BF16), V((D, T), BF16),
+        V((D // LANES, T, LANES), F32), V((T, D), F32),
+        V((8, T, LANES), F32), V((4, T, LANES), F32),
+        V((T, 3 * C), BF16), V((Z, T, C), BF16), V((Z, T + SUB, C), F32),
+        V((Z, T, C), F32), V((Z, T, C), F32), V((Z, T, C), F32), V((Z, T, C), F32),
+        S((7,)), S((3,)), S((3,)), S((4,)), S((4,)), S((4,)),
+        S((4,)), S((4,)), S(()), S(()), S((3, 3)), S((3, 4)),
+        S((3, 4)), S((3, 4)), S((3, 4, 2)), S((3, 4, 2)), S((3, 4)), S((3, 4)),
+        box, box, V((16, LANES), F32), V((8, 16, LANES), F32),
+        V((8, LANES), F32), V((4, 8, LANES), F32), row, box, row, box,
+        S((4, 4)), S((4, 4)), S((4, 4, 2)), S((4, 4, 2)), S((4, 4)), S((4, 4)),
+        S((4, 4)), S((4, 4)), S(()), S(()),
+        S((7,)), S((7,)), S((3,)), S((3,)), S(()), S(()), S(()), S(()), S(()),
+    ]
+    scratch += (
+        [V((4, 4) + s, BF16) for s in SHAPES] * 2
+        + [V((4, 2) + s, BF16) for s in SHAPES]
+        + [V((4,) + s, BF16) for s in SHAPES] * 2
+        + [V(s, F32) for s in SHAPES]
+    )
+    return pl.pallas_call(
+        fused_kernel,
+        out_shape=outs,
+        in_specs=[anyspec, anyspec] + [vm] * (len(args) - 2),
+        out_specs=(anyspec, anyspec) + (vm,) * (len(outs) - 2),
+        scratch_shapes=scratch,
+        compiler_params=pltpu.CompilerParams(
+            vmem_limit_bytes=67043328, collective_id=0, has_side_effects=True
+        ),
+        name="fused",
+    )(*args)
 
 
 def gathered_layer(tok, cot, mix, ow, uw, dw, mg, fb, ib, fg):
@@ -1412,42 +1599,31 @@
     groups = lax.axis_size("grp")
     inners = lax.axis_size("inner")
     seqs, length, width = tokens.shape
-    paired = (groups, inners) == (4, 8) and (length, width) == (1024, 512)
     hidden = forget_weight.shape[1] * inners
     ff = up_weight.shape[1] * inners
+    paired = (groups, inners) == (4, 8) and (length, width, hidden, ff) == (1024, 512, 1024, 2048)
     Z, F = hidden // C, ff // C
     if paired:
-        results = layer_ag(
+        block_output, tokens_grad, *packed = fused(
             tokens.reshape(length, width), cotangent.reshape(length, width),
             forget_weight, input_gate_weight, candidate_weight,
-            output_weight, up_weight, down_weight,
+            output_weight.T, up_weight, down_weight.T,
             mixer_gain, forget_bias, input_bias, feed_norm_gain,
+            mixer_second, forget_rows, forget_columns, input_rows, input_columns,
+            candidate_rows, candidate_columns, forget_second, input_second,
+            output_rows, output_columns, feed_second,
+            up_rows, up_columns, down_rows, down_columns,
         )
-    else:
-        results = gathered_layer(
-            tokens.reshape(length, width), cotangent.reshape(length, width),
-            (forget_weight, input_gate_weight, candidate_weight),
-            output_weight, up_weight, down_weight,
-            mixer_gain, forget_bias, input_bias, feed_norm_gain,
-        )
-    if paired:
-        packed = exchange(
-            results[2:],
-            (
-                forget_weight, input_gate_weight, candidate_weight,
-                output_weight, up_weight, down_weight,
-                mixer_gain, forget_bias, input_bias, feed_norm_gain,
-            ),
-            (
-                mixer_second, forget_rows, forget_columns, input_rows, input_columns,
-                candidate_rows, candidate_columns, forget_second, input_second,
-                output_rows, output_columns, feed_second,
-                up_rows, up_columns, down_rows, down_columns,
-            ),
-        )
-        return (
-            results[0].reshape(tokens.shape), results[1].reshape(tokens.shape), *finish(packed)
-        )
+        done = list(finish(packed))
+        for k in (6, 9, 16, 19):
+            done[k] = done[k].T
+        return (block_output.reshape(tokens.shape), tokens_grad.reshape(tokens.shape), *done)
+    results = gathered_layer(
+        tokens.reshape(length, width), cotangent.reshape(length, width),
+        (forget_weight, input_gate_weight, candidate_weight),
+        output_weight, up_weight, down_weight,
+        mixer_gain, forget_bias, input_bias, feed_norm_gain,
+    )
     block_output, tokens_grad, gmix, got, gup, gdt, fgg, mgg, fbg, ibg = results
     block_output = block_output.reshape(tokens.shape)
     tokens_grad = tokens_grad.reshape(tokens.shape)

time: 231 us -> 173 us (0.75)
  Pallas kernels: 217 us -> 169 us
  local copies, waits for them, and re-layouts: 13 us -> 2.57 us
    pallas_call x2 -> x1, Pallas kernels: 214 us -> 167 us  [fused(): pl.pallas_call(fused_kernel, out_shape=outs, in_specs=[anyspec, anyspec]...]
    unnamed x10 -> x6, local copies, waits for them, and re-layouts: 13 us -> 2.57 us
where the time goes in v4:
time: 173 us
  Pallas kernels  169 us (98%)
  local copies, waits for them, and re-layouts  2.57 us (1%)
    pallas_call x1, Pallas kernels, fused(): pl.pallas_call(fused_kernel, out_shape=outs, in_specs=[anyspec, anyspec]...  167 us

profile of v4, /device:TPU:0, one launch (start us, length us, event | category | flops | bytes accessed | tf_op | source)
XLA Modules:
  0.0 172.5 jit_solution(6889088124574368482)
XLA Ops:
  0.7 166.7 %fused.1 = (bf16[1024,512]{1,0:T(8,128)(2,1)}, bf16[1024,512]{1,0:T(8,128)(2,1)}, f32[128,384]{1,0:T(8,128)}, f32[64,256]{1,0:T(8,128)}, f32[128,256]{1,0:T(8,12...) custom-call(bf16[1024,512]{1,0:T(8,128)(2,1)} %bitcast.12, ...), custom_call_target="tpu_custom_call" | custom-call | tf_op jit(solution)/shard_map/fused/pallas_call | solution.py:1533
  167.4 0.0 copy-start.1
  167.4 2.5 %finish.1 = (f32[16]{0:T(128)}, f32[128,128]{1,0:T(8,128)}, f32[128,128]{1,0:T(8,128)}, f32[128,128]{1,0:T(8,128)}, f32[32]{0:T(128)}, /*index=5*/f32[32]{0:T(12...) custom-call(f32[128,384]{1,0:T(8,128)} %get-tuple-element.91.grad_mi, ...), custom_call_target="tpu_custom_call" | custom-call | tf_op jit(solution)/shard_map/finish/pallas_call | solution.py:1200
  169.9 0.0 copy-done.1
  169.9 0.0 copy-start
  169.9 1.0 copy.69
  170.9 0.6 copy-done
  171.5 1.0 copy.70
Async XLA Ops:
  167.4 2.5 %copy-start.1 = (bf16[1024,512]{1,0:T(8,128)(2,1)S(1)}, bf16[1024,512]{1,0:T(8,128)(2,1)}, u32[]{:S(2)}) copy-start(bf16[1024,512]{1,0:T(8,128)(2,1)} %get-tuple-element.89) | copy-start | bytes 3145732
  169.9 1.6 copy-start

commit v5 on v4

--- a/solution.py
+++ b/solution.py
@@ -137,7 +137,7 @@
     loop(T // LANES, place)
 
 
-def mixer_forward(refs, z, T):
+def mixer_forward(refs, z, T, hook=None):
     pre, ac, st = refs.pre, refs.buf, refs.st
     halves = C // LANES
     width = 3 * LANES
@@ -196,7 +196,11 @@
 
     one = jnp.ones((SUB, LANES), F32)
     zero = jnp.zeros((SUB, LANES), F32)
+    if hook is not None:
+        hook(1)
     ends = lax.fori_loop(0, T // 64, gates, tuple((one, zero) for _ in range(halves)))
+    if hook is not None:
+        hook(2)
     for h in range(halves):
         a, b = ends[h]
         rows = [jnp.zeros((1, LANES), F32)]
@@ -537,12 +541,18 @@
     return jnp.concatenate(rows + [jnp.zeros((1, LANES - used), F32)], axis=1)
 
 
+FIRST = (3, 0)
+LATER = (1, 2)
+
+
 def block_of(refs, a, g, i):
     if a == 0:
         return refs.wot.at[g, at(i, 64), :]
     if a == 1:
         return refs.wup.at[i, at(g, 128), :]
-    return refs.wdt.at[pl.ds(2 * g, 2), at(i, 64), :]
+    if a == 2:
+        return refs.wdt.at[pl.ds(2 * g, 2), at(i, 64), :]
+    return refs.wmix.at[i // 2, at(g, 128), at(i % 2, 384)]
 
 
 def blocks_of(refs, a, i):
@@ -550,11 +560,162 @@
         return refs.wot.at[:, at(i, 64), :]
     if a == 1:
         return refs.wup.at[i]
-    return refs.wdt.at[:, at(i, 64), :]
-
-
-def mix_column(refs, z, c):
-    return refs.wmix.at[z, :, at(c, 384)]
+    if a == 2:
+        return refs.wdt.at[:, at(i, 64), :]
+    return refs.wmix.at[i // 2, :, at(i % 2, 384)]
+
+
+def line_send(refs, p, a):
+    blk = block_of(refs, a, p.g, p.i)
+    for s in range(1, 4):
+        peer = (p.g, slot_chunk(p, s) * 2 + p.c)
+        rcopy(blk, blk, refs.gz_s.at[a, s - 1], refs.gz_r.at[a, p.z], peer).start()
+
+
+def near_of(p, a, z):
+    return p.near(z + (a in LATER))
+
+
+def far_of(p, a, z):
+    return p.far(z + (a in LATER))
+
+
+def line_wait(refs, p, a, z):
+    @pl.when(z != p.z)
+    def _():
+        blk = block_of(refs, a, p.g, z * 2 + p.c)
+        rcopy(blk, blk, refs.gp_s.at[a, z, 0], refs.gz_r.at[a, z], p.partner).wait_recv()
+
+
+def near_send(refs, p, a, z):
+    blk = block_of(refs, a, p.g, z * 2 + p.c)
+    near, far = (near_of(p, a, z), p.i), (far_of(p, a, z), p.i)
+    rcopy(blk, blk, refs.gn_s.at[a, z], refs.gn_r.at[a, z], near).start()
+    rcopy(blk, blk, refs.gf_s.at[a, z, 0], refs.gf_r.at[a, z, 0], far).start()
+
+
+def far_send(refs, p, a, z):
+    near = block_of(refs, a, near_of(p, a, z), z * 2 + p.c)
+    far = (far_of(p, a, z), p.i)
+    rcopy(near, near, refs.gn_s.at[a, z], refs.gn_r.at[a, z], p.partner).wait_recv()
+    rcopy(near, near, refs.gf_s.at[a, z, 1], refs.gf_r.at[a, z, 1], far).start()
+
+
+def far_wait(refs, p, a, z, k):
+    blk = block_of(refs, a, p.g, z * 2 + p.c)
+    rcopy(blk, blk, refs.gf_s.at[a, z, k], refs.gf_r.at[a, z, k], p.partner).wait_recv()
+
+
+def pair_copy(refs, p, a, z, c):
+    full = blocks_of(refs, a, z * 2 + c)
+    return rcopy(full, full, refs.gp_s.at[a, z, 0], refs.gp_r.at[a, z, 0], p.partner)
+
+
+def first_step(refs, p, kind, s):
+    for a in FIRST:
+        z = slot_chunk(p, s)
+        if kind == "n":
+            line_wait(refs, p, a, z)
+            near_send(refs, p, a, z)
+        elif kind == "f":
+            far_send(refs, p, a, z)
+        elif kind == "p":
+            far_wait(refs, p, a, z, 0)
+            far_wait(refs, p, a, z, 1)
+            pair_copy(refs, p, a, z, p.c).start()
+        else:
+            pair_copy(refs, p, a, z, 1 - p.c).wait_recv()
+
+
+def up_step(refs, p, kind, m):
+    if kind == "n":
+
+        @pl.when(p.z != m)
+        def _():
+            line_wait(refs, p, 1, m)
+            near_send(refs, p, 1, m)
+    elif kind == "f":
+        far_send(refs, p, 1, m)
+    elif kind == "p":
+        far_wait(refs, p, 1, m, 0)
+        far_wait(refs, p, 1, m, 1)
+        pair_copy(refs, p, 1, m, p.c).start()
+    else:
+        pair_copy(refs, p, 1, m, 1 - p.c).wait_recv()
+
+
+def up_own(refs, p, phase):
+    inner = (p.z + 1) // 2 % 2
+
+    @pl.when(inner == phase)
+    def _():
+        near_send(refs, p, 1, p.z)
+
+
+def down_pair(refs, p, z, phase, k, c):
+    g = (1 + k) if phase else 3 * k
+    blk = block_of(refs, 2, g, z * 2 + c)
+    return rcopy(blk, blk, refs.gp_s.at[2, z, phase * 2 + k], refs.gp_r.at[2, z, phase * 2 + k], p.partner)
+
+
+def down_step(refs, p, kind, phase, s):
+    z = slot_chunk(p, s)
+    active = (p.x + p.y) % 2 == phase
+    idle = (p.x + p.y) % 2 != phase
+    if kind == "n":
+
+        @pl.when(active)
+        def _():
+            line_wait(refs, p, 2, z)
+            near_send(refs, p, 2, z)
+    elif kind == "f":
+
+        @pl.when(idle)
+        def _():
+            far_send(refs, p, 2, z)
+    elif kind == "p":
+
+        @pl.when(active)
+        def _():
+            far_wait(refs, p, 2, z, 1)
+
+        @pl.when(idle)
+        def _():
+            far_wait(refs, p, 2, z, 0)
+
+        for k in range(2):
+            down_pair(refs, p, z, phase, k, p.c).start()
+    else:
+        for k in range(2):
+            down_pair(refs, p, z, phase, k, 1 - p.c).wait_recv()
+
+
+def gather_drain(refs, p):
+    for a in range(4):
+        blk = block_of(refs, a, p.g, p.i)
+        for k in range(3):
+            rcopy(blk, blk, refs.gz_s.at[a, k], refs.gz_r.at[a, p.z], p.partner).wait_send()
+        for z in range(4):
+            blk = block_of(refs, a, p.g, z * 2 + p.c)
+            rcopy(blk, blk, refs.gn_s.at[a, z], refs.gn_r.at[a, z], p.partner).wait_send()
+            for k in range(2):
+                rcopy(blk, blk, refs.gf_s.at[a, z, k], refs.gf_r.at[a, z, k], p.partner).wait_send()
+            if a == 2:
+                for k in range(4):
+                    down_pair(refs, p, z, k // 2, k % 2, p.c).wait_send()
+            else:
+                pair_copy(refs, p, a, z, p.c).wait_send()
+
+
+def gather_hook(refs, p, actions):
+    for action in actions.split():
+        kind, number = action[1], int(action[-1])
+        if action[0] == "M":
+            first_step(refs, p, kind, number)
+        elif action[0] == "U":
+            up_step(refs, p, kind, number)
+        else:
+            down_step(refs, p, kind, int(action[2]), number)
 
 
 def gather_start(refs, p):
@@ -579,25 +740,31 @@
     row = pack_vectors(refs.mg, refs.fbv, refs.ibv, refs.fg)
     refs.vstage[...] = row
     refs.vecs[p.me] = row
+    for c in local:
+        c.wait()
     entry_barrier(p)
-    for c in local[:3]:
-        c.wait()
-    own = refs.wmix.at[p.z, at(p.g, 128), at(p.c, 384)]
-    for k in range(1, 4):
-        peer = p.flip(k % 2, k // 2)
-        rcopy(own, own, refs.mxg_s.at[k - 1], refs.mxg_r.at[k - 1], (peer, p.i)).start()
 
     def vector(k):
         rcopy(refs.vstage, refs.vecs.at[p.me], refs.vec_s, refs.vec_r, p.other(k + 1)).start()
 
+    for a in FIRST:
+        near_send(refs, p, a, p.z)
+    up_own(refs, p, 0)
+    down_step(refs, p, "n", 0, 0)
     loop(31, vector)
-    for c in local[3:]:
-        c.wait()
-    for a in range(3):
-        blk = block_of(refs, a, p.g, p.i)
-        for k in range(1, 4):
-            peer = (p.g, ((p.z + k) % 4) * 2 + p.c)
-            rcopy(blk, blk, refs.ffz_s.at[a, k - 1], refs.ffz_r.at[a, p.z], peer).start()
+    for a in FIRST:
+        line_send(refs, p, a)
+    inner = (p.z + 1) // 2 % 2
+
+    @pl.when(inner == 0)
+    def _():
+        line_send(refs, p, 1)
+
+    line_send(refs, p, 2)
+
+    @pl.when(inner == 1)
+    def _():
+        line_send(refs, p, 1)
 
 
 def gather_vectors(refs, p):
@@ -613,145 +780,6 @@
         refs.ib[z] = ib[:, z * C : (z + 1) * C]
 
 
-def mix_exchange(refs, p, s):
-    def send_partner(z):
-        col = mix_column(refs, z, p.c)
-        rcopy(col, col, refs.mxp_s.at[z], refs.mxp_r.at[z], p.partner).start()
-
-    def wait_partner(z):
-        col = mix_column(refs, z, 1 - p.c)
-        rcopy(col, col, refs.mxp_s.at[z], refs.mxp_r.at[z], p.partner).wait_recv()
-
-    def send_up(z):
-        col = mix_column(refs, z, p.c)
-        rcopy(col, col, refs.mxu_s.at[z], refs.mxz_r.at[z], (p.g, p.i + 2)).start()
-
-    def send_down(z):
-        col = mix_column(refs, z, p.c)
-        rcopy(col, col, refs.mxd_s.at[z], refs.mxz_r.at[z], (p.g, p.i - 2)).start()
-
-    def wait_line(z):
-        col = mix_column(refs, z, p.c)
-        rcopy(col, col, refs.mxp_s.at[z], refs.mxz_r.at[z], p.partner).wait_recv()
-
-    @pl.when(s == 0)
-    def _():
-        for k in range(1, 4):
-            peer = p.flip(k % 2, k // 2)
-            blk = refs.wmix.at[p.z, at(peer, 128), at(p.c, 384)]
-            rcopy(blk, blk, refs.mxg_s.at[k - 1], refs.mxg_r.at[k - 1], (peer, p.i)).wait()
-
-        @pl.when(p.z < 3)
-        def _():
-            send_up(p.z)
-
-        @pl.when(p.z > 0)
-        def _():
-            send_down(p.z)
-
-        send_partner(p.z)
-        wait_partner(p.z)
-
-    below, above = p.z - s, p.z + s
-
-    @pl.when((s > 0) & (below >= 0))
-    def _():
-        wait_line(below)
-
-        @pl.when(p.z < 3)
-        def _():
-            send_up(below)
-
-        send_partner(below)
-
-    @pl.when((s > 0) & (above < 4))
-    def _():
-        wait_line(above)
-
-        @pl.when(p.z > 0)
-        def _():
-            send_down(above)
-
-        send_partner(above)
-
-    @pl.when((s > 0) & (below >= 0))
-    def _():
-        wait_partner(below)
-
-    @pl.when((s > 0) & (above < 4))
-    def _():
-        wait_partner(above)
-
-
-def mix_drain(refs, p):
-    for z in range(4):
-        col = mix_column(refs, z, p.c)
-        rcopy(col, col, refs.mxp_s.at[z], refs.mxp_r.at[z], p.partner).wait_send()
-
-        @pl.when((z <= p.z) & (p.z < 3))
-        def _():
-            rcopy(col, col, refs.mxu_s.at[z], refs.mxz_r.at[z], p.partner).wait_send()
-
-        @pl.when((z >= p.z) & (p.z > 0))
-        def _():
-            rcopy(col, col, refs.mxd_s.at[z], refs.mxz_r.at[z], p.partner).wait_send()
-
-
-def feed_second(refs, p):
-    for a in range(3):
-        for z in range(4):
-            blk = block_of(refs, a, p.g, z * 2 + p.c)
-
-            @pl.when(p.z != z)
-            def _():
-                rcopy(blk, blk, refs.ffp_s.at[a, z], refs.ffz_r.at[a, z], p.partner).wait_recv()
-
-            rcopy(blk, blk, refs.ff2_s.at[a, z], refs.ff2_r.at[a, z], (p.near(z), p.i)).start()
-
-
-def feed_third(refs, p):
-    for a in range(3):
-        for z in range(4):
-            mine = block_of(refs, a, p.g, z * 2 + p.c)
-            near = block_of(refs, a, p.near(z), z * 2 + p.c)
-            far = (p.far(z), p.i)
-            rcopy(near, near, refs.ff2_s.at[a, z], refs.ff2_r.at[a, z], (p.near(z), p.i)).wait_recv()
-            rcopy(mine, mine, refs.ff3_s.at[a, z, 0], refs.ff3_r.at[a, z, 0], far).start()
-            rcopy(near, near, refs.ff3_s.at[a, z, 1], refs.ff3_r.at[a, z, 1], far).start()
-
-
-def feed_fourth(refs, p):
-    for a in range(3):
-        for z in range(4):
-            blk = block_of(refs, a, p.g, z * 2 + p.c)
-            far = (p.far(z), p.i)
-            for k in range(2):
-                rcopy(blk, blk, refs.ff3_s.at[a, z, k], refs.ff3_r.at[a, z, k], far).wait_recv()
-            full = blocks_of(refs, a, z * 2 + p.c)
-            rcopy(full, full, refs.ffp_s.at[a, z], refs.ffp_r.at[a, z], p.partner).start()
-
-
-def feed_last(refs, p):
-    for a in range(3):
-        for z in range(4):
-            full = blocks_of(refs, a, z * 2 + 1 - p.c)
-            rcopy(full, full, refs.ffp_s.at[a, z], refs.ffp_r.at[a, z], p.partner).wait_recv()
-
-
-def feed_drain(refs, p):
-    for a in range(3):
-        for k in range(1, 4):
-            blk = block_of(refs, a, p.g, p.i)
-            rcopy(blk, blk, refs.ffz_s.at[a, k - 1], refs.ffz_r.at[a, p.z], p.partner).wait_send()
-        for z in range(4):
-            blk = block_of(refs, a, p.g, z * 2 + p.c)
-            rcopy(blk, blk, refs.ff2_s.at[a, z], refs.ff2_r.at[a, z], p.partner).wait_send()
-            for k in range(2):
-                rcopy(blk, blk, refs.ff3_s.at[a, z, k], refs.ff3_r.at[a, z, k], p.partner).wait_send()
-            full = blocks_of(refs, a, z * 2 + p.c)
-            rcopy(full, full, refs.ffp_s.at[a, z], refs.ffp_r.at[a, z], p.partner).wait_send()
-
-
 def slot_chunk(p, s):
     low = jnp.minimum(p.z, 3 - p.z)
     shift = jnp.where(s == 0, 1, jnp.where(s == 1, -1, 0))
@@ -759,27 +787,27 @@
     return jnp.where(p.z < 2, m, 3 - m)
 
 
+SLOT_HOOKS = (
+    ("", "Mf2 Dn01", "Mp1 Mf3 Un0 Un3"),
+    ("Md1", "Mp2 Df00 Df01", "Dn02 Dn03 Uf0 Uf3"),
+    ("Md2", "Mp3", "Df02 Df03 Dp00 Dp01"),
+    ("Md3", "Un1 Un2 Dn10 Dn11 Dn12 Dn13", "Dp02 Dp03 Up0 Up3"),
+)
+
+
 def mixer_slots(refs, p, T):
+    def hook(s, j):
+        for k in range(4):
+
+            @pl.when(s == k)
+            def _():
+                gather_hook(refs, p, SLOT_HOOKS[k][j])
+
     def slot(s):
-        mix_exchange(refs, p, s)
-        mixer_forward(refs, slot_chunk(p, s), T)
-
-        @pl.when(s == 0)
-        def _():
-            feed_second(refs, p)
-
-        @pl.when(s == 1)
-        def _():
-            feed_third(refs, p)
-
-        @pl.when(s == 2)
-        def _():
-            feed_fourth(refs, p)
+        hook(s, 0)
+        mixer_forward(refs, slot_chunk(p, s), T, lambda j: hook(s, j))
 
     loop(4, slot)
-    mix_drain(refs, p)
-    feed_last(refs, p)
-    feed_drain(refs, p)
 
 
 SHAPES = ((128, 256), (128, 256), (128, 384), (64, 256))
@@ -1224,17 +1252,16 @@
             self.resid, self.dfe,
             self.pre, self.buf, self.dpre, self.slow, self.st,
             self.keep, self.k_f, self.k_i, self.k_c,
-            self.loc_s, self.mxg_s, self.mxg_r, self.mxu_s, self.mxd_s, self.mxz_r,
-            self.mxp_s, self.mxp_r, self.vec_s, self.vec_r, self.ffz_s, self.ffz_r,
-            self.ff2_s, self.ff2_r, self.ff3_s, self.ff3_r, self.ffp_s, self.ffp_r,
+            self.loc_s, self.vec_s, self.vec_r, self.gz_s, self.gz_r,
+            self.gn_s, self.gn_r, self.gf_s, self.gf_r, self.gp_s, self.gp_r,
             self.vout, self.vin, self.rowst, self.rowin, self.colst, self.colin,
             self.scal, self.scin, self.clip, self.clin,
             self.rp_s, self.rp_r, self.r1_s, self.r1_r, self.r2_s, self.r2_r,
             self.r3_s, self.r3_r, self.vex_s, self.vex_r,
             self.row_s, self.row_r, self.col_s, self.col_r, self.sc_s, self.sc_r,
             self.cl_s, self.cl_r, self.io_s,
-        ) = args[:119]
-        rest = list(args[119:])
+        ) = args[:112]
+        rest = list(args[112:])
         self.psend, self.precv, self.r1, self.r2, self.r3, self.fin_g = (
             rest[4 * k : 4 * k + 4] for k in range(6)
         )
@@ -1367,20 +1394,25 @@
     rs_third_send(refs, p, a, z)
 
 
+def feed_order(k):
+    return jnp.where(k == 1, 3, jnp.where(k >= 2, k - 1, 0))
+
+
 def feed_tick(refs, p, f):
     @pl.when((f % 2 == 0) & (f >= 2))
     def _():
-        merge_up(refs, p, f // 2 - 1)
-        merge_down(refs, p, f // 2 - 1)
-        rs_first_send(refs, p, UP, f // 2 - 1)
+        last = feed_order(f // 2 - 1)
+        merge_up(refs, p, last)
+        merge_down(refs, p, last)
+        rs_first_send(refs, p, UP, last)
 
     @pl.when((f % 2 == 0) & (f >= 4))
     def _():
-        second(refs, p, UP, f // 2 - 2)
+        second(refs, p, UP, feed_order(f // 2 - 2))
 
     @pl.when((f % 2 == 0) & (f >= 6))
     def _():
-        third(refs, p, UP, f // 2 - 3)
+        third(refs, p, UP, feed_order(f // 2 - 3))
 
 
 def fused_kernel(*args):
@@ -1398,31 +1430,48 @@
     gather_vectors(refs, p)
     load.wait()
     norm_in(refs, T)
+    gather_hook(refs, p, "Mf0 Mn1 Mn2 Mf1 Mp0 Mn3 Md0")
     mixer_slots(refs, p, T)
+    up_own(refs, p, 1)
     mix_out(refs, T)
+    gather_hook(refs, p, "Ud0 Ud3 Dd00 Dd01 Dd02 Dd03")
     clear(refs.oacc, T)
     refs.dfe[...] = jnp.zeros_like(refs.dfe)
 
     def feed_step(f):
-        feed(refs, f, T)
+        @pl.when(f == 4)
+        def _():
+            gather_hook(refs, p, "Ud1 Ud2 Dd10 Dd11 Dd12 Dd13")
+
+        feed(refs, feed_order(f // 2) * 2 + f % 2, T)
+
+        @pl.when(f == 0)
+        def _():
+            gather_hook(refs, p, "Uf1 Uf2 Df10 Df11 Df12 Df13")
+
+        @pl.when(f == 1)
+        def _():
+            gather_hook(refs, p, "Up1 Up2 Dp10 Dp11 Dp12 Dp13")
+
         feed_tick(refs, p, f)
-        put_feed_grads(refs, p, f)
+        put_feed_grads(refs, p, feed_order(f // 2) * 2 + f % 2)
 
         @pl.when(f % 2 == 1)
         def _():
-            rs_pair(refs, p, UP, f // 2).start()
-            rs_pair(refs, p, DOWN, f // 2).start()
+            rs_pair(refs, p, UP, feed_order(f // 2)).start()
+            rs_pair(refs, p, DOWN, feed_order(f // 2)).start()
 
     loop(8, feed_step)
     feed_back(refs, T)
     store = pltpu.make_async_copy(refs.io, refs.block_out, refs.io_s)
     store.start()
-    merge_up(refs, p, 3)
-    merge_down(refs, p, 3)
-    rs_first_send(refs, p, UP, 3)
+    gather_drain(refs, p)
+    merge_up(refs, p, 2)
+    merge_down(refs, p, 2)
+    rs_first_send(refs, p, UP, 2)
     all_z(lambda z: rs_first_send(refs, p, DOWN, z))
-    second(refs, p, UP, 2)
-    third(refs, p, UP, 1)
+    second(refs, p, UP, 1)
+    third(refs, p, UP, 3)
     put_out_grads(refs, p)
     rs_pair(refs, p, OUT, 0).start()
     clear(refs.oacc, T)
@@ -1440,8 +1489,8 @@
             merge_out(refs, p)
             all_z(lambda z: rs_first_send(refs, p, OUT, z))
             all_z(lambda z: second(refs, p, DOWN, z))
-            second(refs, p, UP, 3)
-            third(refs, p, UP, 2)
+            second(refs, p, UP, 2)
+            third(refs, p, UP, 1)
 
         @pl.when(n >= 1)
         def _():
@@ -1452,7 +1501,7 @@
         def _():
             all_z(lambda z: second(refs, p, OUT, z))
             all_z(lambda z: third(refs, p, DOWN, z))
-            third(refs, p, UP, 3)
+            third(refs, p, UP, 2)
 
         @pl.when(n >= 2)
         def _():
@@ -1515,9 +1564,8 @@
         V((8, T, LANES), F32), V((4, T, LANES), F32),
         V((T, 3 * C), BF16), V((Z, T, C), BF16), V((Z, T + SUB, C), F32),
         V((Z, T, C), F32), V((Z, T, C), F32), V((Z, T, C), F32), V((Z, T, C), F32),
-        S((7,)), S((3,)), S((3,)), S((4,)), S((4,)), S((4,)),
-        S((4,)), S((4,)), S(()), S(()), S((3, 3)), S((3, 4)),
-        S((3, 4)), S((3, 4)), S((3, 4, 2)), S((3, 4, 2)), S((3, 4)), S((3, 4)),
+        S((7,)), S(()), S(()), S((4, 3)), S((4, 4)),
+        S((4, 4)), S((4, 4)), S((4, 4, 2)), S((4, 4, 2)), S((4, 4, 4)), S((4, 4, 4)),
         box, box, V((16, LANES), F32), V((8, 16, LANES), F32),
         V((8, LANES), F32), V((4, 8, LANES), F32), row, box, row, box,
         S((4, 4)), S((4, 4)), S((4, 4, 2)), S((4, 4, 2)), S((4, 4)), S((4, 4)),

time: 173 us -> 162 us (0.936)
  Pallas kernels: 169 us -> 158 us
    pallas_call x1, Pallas kernels: 167 us -> 156 us  [fused(): pl.pallas_call(fused_kernel, out_shape=outs, in_specs=[anyspec, anyspec]...]
where the time goes in v5:
time: 162 us
  Pallas kernels  158 us (98%)
  local copies, waits for them, and re-layouts  2.57 us (2%)
    pallas_call x1, Pallas kernels, fused(): pl.pallas_call(fused_kernel, out_shape=outs, in_specs=[anyspec, anyspec]...  156 us

profile of v5, /device:TPU:0, one launch (start us, length us, event | category | flops | bytes accessed | tf_op | source)
XLA Modules:
  0.0 161.7 jit_solution(16335005808857828538)
XLA Ops:
  0.7 155.9 %fused.1 = (bf16[1024,512]{1,0:T(8,128)(2,1)}, bf16[1024,512]{1,0:T(8,128)(2,1)}, f32[128,384]{1,0:T(8,128)}, f32[64,256]{1,0:T(8,128)}, f32[128,256]{1,0:T(8,12...) custom-call(bf16[1024,512]{1,0:T(8,128)(2,1)} %bitcast.12, ...), custom_call_target="tpu_custom_call" | custom-call | tf_op jit(solution)/shard_map/fused/pallas_call | solution.py:1581
  156.6 0.0 copy-start.1
  156.6 2.5 %finish.1 = (f32[16]{0:T(128)}, f32[128,128]{1,0:T(8,128)}, f32[128,128]{1,0:T(8,128)}, f32[128,128]{1,0:T(8,128)}, f32[32]{0:T(128)}, /*index=5*/f32[32]{0:T(12...) custom-call(f32[128,384]{1,0:T(8,128)} %get-tuple-element.91.grad_mi, ...), custom_call_target="tpu_custom_call" | custom-call | tf_op jit(solution)/shard_map/finish/pallas_call | solution.py:1228
  159.1 0.0 copy-done.1
  159.1 0.0 copy-start
  159.1 1.0 copy.69
  160.1 0.6 copy-done
  160.7 1.0 copy.70
Async XLA Ops:
  156.6 2.5 %copy-start.1 = (bf16[1024,512]{1,0:T(8,128)(2,1)S(1)}, bf16[1024,512]{1,0:T(8,128)(2,1)}, u32[]{:S(2)}) copy-start(bf16[1024,512]{1,0:T(8,128)(2,1)} %get-tuple-element.89) | copy-start | bytes 3145732
  159.1 1.6 copy-start

commit v6 on v5

--- a/solution.py
+++ b/solution.py
@@ -40,19 +40,14 @@
 
 
 def gelu_parts(x):
-    ax = jnp.abs(x)
-    e = jnp.exp(-0.5 * (x * x))
-    t = 1.0 / (1.0 + (0.4 * math.sqrt(0.5)) * ax)
-    poly = jnp.full_like(t, ERFC[-1])
+    e = jnp.exp2((x * x) * (-0.5 / math.log(2.0)))
+    t = 1.0 / (1.0 + (0.4 * math.sqrt(0.5)) * jnp.abs(x))
+    poly = jnp.full_like(t, 0.5 * ERFC[-1])
     for c in ERFC[-2::-1]:
-        poly = poly * t + c
-    half = 0.5 * (poly * t * e)
+        poly = poly * t + 0.5 * c
+    half = poly * (t * e)
     cdf = jnp.where(x >= 0, 1.0 - half, half)
     return x * cdf, cdf + (x * e) * (1.0 / math.sqrt(2.0 * math.pi))
-
-
-def strided(ref, j, n):
-    return ref[pl.ds(j, SUB, stride=n), :]
 
 
 def gather_rows(tmp, j0, n, D):
@@ -69,6 +64,9 @@
             tmp[q, pl.ds(j0 + jj, SUB, stride=n), :] = out[
                 jj * SUB : (jj + 1) * SUB, q * LANES : (q + 1) * LANES
             ]
+
+
+LOG2E = 1.0 / math.log(2.0)
 
 
 def load_planes(ref, rows, start=0, count=None):
@@ -161,25 +159,27 @@
             pf = pre[3 * h, pl.ds(r0, 64), :] + fb[:, lanes]
             pi = pre[3 * h + 1, pl.ds(r0, 64), :] + ib[:, lanes]
             pc = pre[3 * h + 2, pl.ds(r0, 64), :]
+            pf, pi = pf * LOG2E, pi * LOG2E
             m = jnp.minimum(jnp.minimum(pf, pi), 0.0)
-            e0 = jnp.exp(m)
-            ef = jnp.exp(m - pf)
-            ei = jnp.exp(m - pi)
+            e0 = jnp.exp2(m)
+            ef = jnp.exp2(m - pf)
+            ei = jnp.exp2(m - pi)
             nk = e0 + ei
             na = e0 + ef
-            inv = 1.0 / (nk + na)
+            both = nk + na
+            floor = jnp.maximum(na, 1e-37)
+            rec = 1.0 / (both * floor)
+            inv = rec * floor
             keep = nk * inv
             admit = na * inv
-            not_f = 1.0 / (1.0 + jnp.exp(pf))
-            not_i = 1.0 / (1.0 + jnp.exp(pi))
             ec = jnp.exp(jnp.minimum(pc, 0.0))
             sg = ec / (1.0 + ec)
             positive = pc >= 0
             value = jnp.where(positive, pc + 0.5, sg)
             slope = jnp.where(positive, 1.0, sg * (1.0 - sg))
             refs.keep[z, pl.ds(r0, 64), lanes] = keep
-            refs.k_f[z, pl.ds(r0, 64), lanes] = keep * not_f
-            refs.k_i[z, pl.ds(r0, 64), lanes] = keep * not_i
+            refs.k_f[z, pl.ds(r0, 64), lanes] = keep * (ef * (rec * both))
+            refs.k_i[z, pl.ds(r0, 64), lanes] = ei * inv
             refs.k_c[z, pl.ds(r0, 64), lanes] = admit * slope
             inflow = admit * value
             alist, blist = [], []
@@ -241,20 +241,36 @@
 
 def feed(refs, f, T):
     wup, wdt = refs.wup, refs.wdt
-
-    def body(i):
-        rows = at(i, 256)
+    size = 256
+    tiles = T // size
+
+    def project(i):
+        rows = slice(i * size, (i + 1) * size)
         store_planes(refs.buf, rows, dot(refs.fin[rows, :], wup[f]))
         store_planes(refs.buf, rows, dot(refs.cot_p[rows, :], wdt[f]), 2)
-        for k in range(4):
-            sub = pl.ds(pl.multiple_of(i * 256 + k * 64, 64), 64)
-            act, slope = gelu_parts(load_planes(refs.buf, sub, 0, 2))
-            refs.dpre[sub, 0:C] = act.astype(BF16)
-            refs.dpre[sub, C : 2 * C] = (load_planes(refs.buf, sub, 2, 2) * slope).astype(BF16)
+
+    def activate(i):
+        for k in range(size // 32):
+            rows = slice(i * size + k * 32, i * size + (k + 1) * 32)
+            for q in range(C // LANES):
+                act, slope = gelu_parts(refs.buf[q, rows, :])
+                lanes = slice(q * LANES, (q + 1) * LANES)
+                refs.dpre[rows, lanes] = act.astype(BF16)
+                lanes = slice(C + q * LANES, C + (q + 1) * LANES)
+                refs.dpre[rows, lanes] = (refs.buf[2 + q, rows, :] * slope).astype(BF16)
+
+    def add(i):
+        rows = slice(i * size, (i + 1) * size)
         add_planes(refs.oacc, rows, dot_t(refs.dpre[rows, 0:C], wdt[f]))
         refs.dfe[rows, :] += dot_t(refs.dpre[rows, C : 2 * C], wup[f])
 
-    loop(T // 256, body)
+    for i in range(tiles + 2):
+        if i < tiles:
+            project(i)
+        if 1 <= i < tiles + 1:
+            activate(i - 1)
+        if i >= 2:
+            add(i - 2)
 
 
 def feed_back(refs, T):
@@ -1290,6 +1306,7 @@
 def put_feed_grads(refs, p, f):
     z, h = f // 2, f % 2
     up = dot(refs.fin_t[...], refs.dpre[:, C : 2 * C])
+    put_halves(refs, 1 + h, dot(refs.cot_t[...], refs.dpre[:, 0:C]))
 
     @pl.when(h == p.c)
     def _():
@@ -1300,7 +1317,6 @@
         for g in range(4):
             refs.psend[UP][z, g] = up[g * 128 : (g + 1) * 128].astype(BF16)
 
-    put_halves(refs, 1 + h, dot(refs.cot_t[...], refs.dpre[:, 0:C]))
     half = pl.ds(pl.multiple_of(h * 64, 64), 64)
     for zz in range(4):
         part = halves_of(refs, 1 + h, line_rows(zz, 1 - p.c))

time: 162 us -> 151 us (0.932)
  Pallas kernels: 158 us -> 147 us
    pallas_call x1, Pallas kernels: 156 us -> 145 us  [fused(): pl.pallas_call(fused_kernel, out_shape=outs, in_specs=[anyspec, anyspec]...]
where the time goes in v6:
time: 151 us
  Pallas kernels  147 us (97%)
  local copies, waits for them, and re-layouts  2.57 us (2%)
    pallas_call x1, Pallas kernels, fused(): pl.pallas_call(fused_kernel, out_shape=outs, in_specs=[anyspec, anyspec]...  145 us

profile of v6, /device:TPU:0, one launch (start us, length us, event | category | flops | bytes accessed | tf_op | source)
XLA Modules:
  0.0 150.6 jit_solution(10293473507871851089)
XLA Ops:
  0.7 144.7 %fused.1 = (bf16[1024,512]{1,0:T(8,128)(2,1)}, bf16[1024,512]{1,0:T(8,128)(2,1)}, f32[128,384]{1,0:T(8,128)}, f32[64,256]{1,0:T(8,128)}, f32[128,256]{1,0:T(8,12...) custom-call(bf16[1024,512]{1,0:T(8,128)(2,1)} %bitcast.12, ...), custom_call_target="tpu_custom_call" | custom-call | tf_op jit(solution)/shard_map/fused/pallas_call | solution.py:1597
  145.4 0.0 copy-start.1
  145.5 2.5 %finish.1 = (f32[16]{0:T(128)}, f32[128,128]{1,0:T(8,128)}, f32[128,128]{1,0:T(8,128)}, f32[128,128]{1,0:T(8,128)}, f32[32]{0:T(128)}, /*index=5*/f32[32]{0:T(12...) custom-call(f32[128,384]{1,0:T(8,128)} %get-tuple-element.91.grad_mi, ...), custom_call_target="tpu_custom_call" | custom-call | tf_op jit(solution)/shard_map/finish/pallas_call | solution.py:1244
  148.0 0.0 copy-done.1
  148.0 0.0 copy-start
  148.0 1.0 copy.69
  149.0 0.6 copy-done
  149.6 1.0 copy.70
Async XLA Ops:
  145.4 2.5 %copy-start.1 = (bf16[1024,512]{1,0:T(8,128)(2,1)S(1)}, bf16[1024,512]{1,0:T(8,128)(2,1)}, u32[]{:S(2)}) copy-start(bf16[1024,512]{1,0:T(8,128)(2,1)} %get-tuple-element.89) | copy-start | bytes 3145732
  148.0 1.6 %copy-start = (bf16[1024,512]{1,0:T(8,128)(2,1)S(1)}, bf16[1024,512]{1,0:T(8,128)(2,1)}, u32[]{:S(2)}) copy-start(bf16[1024,512]{1,0:T(8,128)(2,1)} %get-tuple-element.90) | copy-start | bytes 3145732

commit v7 on v6

--- a/solution.py
+++ b/solution.py
@@ -305,7 +305,7 @@
     loop(T // LANES, emit)
 
 
-def mixer_back(refs, z, T):
+def mixer_back(refs, z, T, hook=None):
     buf, st = refs.buf, refs.st
     halves = C // LANES
     width = 3 * LANES
@@ -339,6 +339,8 @@
     for s in range(SUB - 1, 0, -1):
         rows.insert(0, e[s : s + 1] + dk[s : s + 1] * rows[0])
     tail = jnp.concatenate(rows, axis=0)
+    if hook is not None:
+        hook()
 
     def grads(i, sums):
         r0 = pl.multiple_of(i * 64, 64)
@@ -374,6 +376,8 @@
         refs.fbg[z, :, lanes] = jnp.sum(sums[h][0], axis=0, keepdims=True)
         refs.ibg[z, :, lanes] = jnp.sum(sums[h][1], axis=0, keepdims=True)
 
+
+def mixer_input_back(refs, z, T):
     def back(i):
         rows = at(i, 256)
         add_planes(refs.oacc, rows, dot_t(refs.dpre[rows, :], refs.wmix[z]))
@@ -451,6 +455,7 @@
     def mixer_step(z):
         gst[0, :, 0:C] = dot(refs.fin_t[...], refs.slow[z])
         mixer_back(refs, z, T)
+        mixer_input_back(refs, z, T)
         gst[1, :, :] = dot(refs.min_t[...], refs.dpre[...])
         one = pltpu.make_async_copy(gst.at[0, :, 0:C], refs.got.at[z], sem.at[0])
         two = pltpu.make_async_copy(gst.at[1], refs.gmix.at[z], sem.at[1])
@@ -517,12 +522,15 @@
         y = (self.y + fy) % 2
         return y * 2 + x
 
+    def turn(self, z):
+        return (z + self.c) % 2
+
     def near(self, z):
-        e = z % 2
+        e = self.turn(z)
         return self.flip(1 - e, e)
 
     def far(self, z):
-        e = z % 2
+        e = self.turn(z)
         return self.flip(e, 1 - e)
 
     def other(self, k):
@@ -627,8 +635,8 @@
     return rcopy(full, full, refs.gp_s.at[a, z, 0], refs.gp_r.at[a, z, 0], p.partner)
 
 
-def first_step(refs, p, kind, s):
-    for a in FIRST:
+def first_step(refs, p, arrays, kind, s):
+    for a in arrays:
         z = slot_chunk(p, s)
         if kind == "n":
             line_wait(refs, p, a, z)
@@ -727,7 +735,9 @@
     for action in actions.split():
         kind, number = action[1], int(action[-1])
         if action[0] == "M":
-            first_step(refs, p, kind, number)
+            first_step(refs, p, (3,), kind, number)
+        elif action[0] == "W":
+            first_step(refs, p, (0,), kind, number)
         elif action[0] == "U":
             up_step(refs, p, kind, number)
         else:
@@ -804,10 +814,10 @@
 
 
 SLOT_HOOKS = (
-    ("", "Mf2 Dn01", "Mp1 Mf3 Un0 Un3"),
-    ("Md1", "Mp2 Df00 Df01", "Dn02 Dn03 Uf0 Uf3"),
-    ("Md2", "Mp3", "Df02 Df03 Dp00 Dp01"),
-    ("Md3", "Un1 Un2 Dn10 Dn11 Dn12 Dn13", "Dp02 Dp03 Up0 Up3"),
+    ("", "Mn3", "Mp1 Mf2"),
+    ("Md1", "Mf3 Wf0 Wn1 Wn2", "Mp2 Wn3 Wf1 Dn01"),
+    ("Md2", "Mp3 Wf2 Wp0 Un0 Un3", "Wf3 Df00 Dn02 Dn03 Df01"),
+    ("Md3", "Wp1 Wp2 Wp3 Uf0 Uf3 Df02 Df03", "Dp00 Dp01 Dp02 Dp03 Up0 Up3"),
 )
 
 
@@ -847,7 +857,7 @@
 
 
 def rs_role(p, g, z):
-    e = z % 2
+    e = p.turn(z)
     y, x = g // 2, g % 2
     return (1 - e) * ((x + p.x) % 2) + e * ((y + p.y) % 2)
 
@@ -875,7 +885,7 @@
 
 
 def rs_group(p, z, k, sent):
-    e = z % 2
+    e = p.turn(z)
     x = (1 - e) * ((p.x + sent) % 2) + e * k
     y = (1 - e) * k + e * ((p.y + sent) % 2)
     return y * 2 + x
@@ -895,7 +905,7 @@
 
 
 def rs_second(refs, p, a, z):
-    e = z % 2
+    e = p.turn(z)
     mine = (1 - e) * p.y + e * p.x
     for k in range(2):
         rs_first_copy(refs, p, a, z, k).wait_recv()
@@ -913,7 +923,7 @@
 
 
 def rs_second_copy(refs, p, a, z):
-    e = z % 2
+    e = p.turn(z)
     other = 1 - ((1 - e) * p.y + e * p.x)
     place = spot(a, rs_group(p, z, other, 0), z)
     return rcopy(
@@ -1202,11 +1212,20 @@
 
 def finish_kernel(
     grad_mix, grad_out, grad_up, grad_down, new_mix, new_out, new_up, new_down,
-    vectors, rows, columns,
+    vectors, rows, columns, block_in, token_in,
     g_mg, g_f, g_i, g_c, g_fb, g_ib, g_o, g_fg, g_u, g_d,
     n_mg, n_f, n_i, n_c, n_fb, n_ib, n_o, n_fg, n_u, n_d,
     s_m, r_f, c_f, r_i, c_i, r_c, c_c, s_f, s_i, r_o, c_o, s_g, r_u, c_u, r_d, c_d, norms,
+    block_out, token_out, stage, sem,
 ):
+    copies = []
+    for k, (src, dst) in enumerate(((block_in, block_out), (token_in, token_out))):
+        fetch = pltpu.make_async_copy(src, stage.at[k], sem.at[0, k])
+        fetch.start()
+        copies.append((fetch, pltpu.make_async_copy(stage.at[k], dst, sem.at[1, k])))
+    for fetch, put in copies:
+        fetch.wait()
+        put.start()
     for src, outs in ((grad_mix, (g_f, g_i, g_c)), (new_mix, (n_f, n_i, n_c))):
         for k, o in enumerate(outs):
             o[...] = src[:, k * 128 : (k + 1) * 128]
@@ -1230,24 +1249,29 @@
             else:
                 for k in range(a, b):
                     o[(k - a) * LANES : (k - a + 1) * LANES] = src[k, :]
-
-
-def finish(packed):
+    for fetch, put in copies:
+        put.wait()
+
+
+def finish(packed, block, tgrad):
     sds = jax.ShapeDtypeStruct
     f = lambda *s: sds(s, F32)
-    block = [f(16), f(128, 128), f(128, 128), f(128, 128), f(32), f(32), f(64, 256), f(16),
+    small = [f(16), f(128, 128), f(128, 128), f(128, 128), f(32), f(32), f(64, 256), f(16),
              f(128, 256), f(64, 512)]
     states = [f(16), f(128), f(128), f(128), f(128), f(128), f(128), f(32), f(32), f(256), f(64),
               f(16), f(128), f(256), f(512), f(64)]
-    outs = tuple(block + block + states + [f(10)])
+    big = sds(block.shape, BF16)
+    outs = tuple(small + small + states + [f(10), big, big])
     vm = pl.BlockSpec(memory_space=pltpu.VMEM)
+    anyspec = pl.BlockSpec(memory_space=pl.ANY)
     return pl.pallas_call(
         finish_kernel,
         out_shape=outs,
-        in_specs=[vm] * len(packed),
-        out_specs=(vm,) * len(outs),
+        in_specs=[vm] * len(packed) + [anyspec] * 2,
+        out_specs=(vm,) * (len(outs) - 2) + (anyspec,) * 2,
+        scratch_shapes=[pltpu.VMEM((2,) + block.shape, BF16), pltpu.SemaphoreType.DMA((2, 2))],
         name="finish",
-    )(*packed)
+    )(*packed, block, tgrad)
 
 
 class FusedRefs:
@@ -1339,7 +1363,7 @@
 
 
 def rs_merge_at(refs, p, a, g, z, own):
-    e = z % 2
+    e = p.turn(z)
     y, x = g // 2, g % 2
     role = (1 - e) * ((x + p.x) % 2) + e * ((y + p.y) % 2)
     place = spot(a, g, z)
@@ -1441,14 +1465,16 @@
     gather_start(refs, p)
     load.wait()
     cot_in(refs, T)
+    gather_hook(refs, p, "Mf0 Mn1")
     load = pltpu.make_async_copy(refs.tok_in, refs.io, refs.io_s)
     load.start()
     gather_vectors(refs, p)
     load.wait()
     norm_in(refs, T)
-    gather_hook(refs, p, "Mf0 Mn1 Mn2 Mf1 Mp0 Mn3 Md0")
+    gather_hook(refs, p, "Mp0 Mf1 Mn2 Md0")
     mixer_slots(refs, p, T)
     up_own(refs, p, 1)
+    gather_hook(refs, p, "Wd0 Wd1 Wd2 Wd3 Un1 Un2 Dn10 Dn11 Dn12 Dn13")
     mix_out(refs, T)
     gather_hook(refs, p, "Ud0 Ud3 Dd00 Dd01 Dd02 Dd03")
     clear(refs.oacc, T)
@@ -1496,22 +1522,31 @@
     def chunk(n):
         return (p.z + 1 + n) % 4
 
-    def mixer_step(n):
-        z = chunk(n)
-        mixer_back(refs, z, T)
-
+    def early(n):
         @pl.when(n == 0)
         def _():
             merge_out(refs, p)
             all_z(lambda z: rs_first_send(refs, p, OUT, z))
             all_z(lambda z: second(refs, p, DOWN, z))
             second(refs, p, UP, 2)
-            third(refs, p, UP, 1)
 
         @pl.when(n >= 1)
         def _():
             merge_mix(refs, p, chunk(n - 1))
             rs_first_send(refs, p, MIX, chunk(n - 1))
+
+        @pl.when(n >= 2)
+        def _():
+            second(refs, p, MIX, chunk(n - 2))
+
+        @pl.when(n == 3)
+        def _():
+            third(refs, p, MIX, chunk(0))
+
+    def late(n):
+        @pl.when(n == 0)
+        def _():
+            third(refs, p, UP, 1)
 
         @pl.when(n == 1)
         def _():
@@ -1519,34 +1554,31 @@
             all_z(lambda z: third(refs, p, DOWN, z))
             third(refs, p, UP, 2)
 
-        @pl.when(n >= 2)
-        def _():
-            second(refs, p, MIX, chunk(n - 2))
-
         @pl.when(n == 2)
         def _():
             all_z(lambda z: third(refs, p, OUT, z))
 
-        @pl.when(n == 3)
-        def _():
-            third(refs, p, MIX, chunk(0))
-
+    def mixer_step(n):
+        z = chunk(n)
+        mixer_back(refs, z, T, lambda: early(n))
         put_mix_grads(refs, p, z)
         rs_pair(refs, p, MIX, z).start()
+        mixer_input_back(refs, z, T)
+        late(n)
 
     loop(4, mixer_step)
+    merge_mix(refs, p, chunk(3))
+    rs_first_send(refs, p, MIX, chunk(3))
+    second(refs, p, MIX, chunk(2))
+    third(refs, p, MIX, chunk(1))
     norm_back(refs, T)
     store = pltpu.make_async_copy(refs.io, refs.tgrad_out, refs.io_s)
     store.start()
-    merge_mix(refs, p, chunk(3))
-    rs_first_send(refs, p, MIX, chunk(3))
     vector_exchange(refs, p)
-    second(refs, p, MIX, chunk(2))
-    third(refs, p, MIX, chunk(1))
     for a in (UP, DOWN, OUT):
         rs_last(refs, p, a)
+    third(refs, p, MIX, chunk(2))
     second(refs, p, MIX, chunk(3))
-    third(refs, p, MIX, chunk(2))
     third(refs, p, MIX, chunk(3))
     rs_last(refs, p, MIX)
     rs_drain(refs, p)
@@ -1678,7 +1710,7 @@
             output_rows, output_columns, feed_second,
             up_rows, up_columns, down_rows, down_columns,
         )
-        done = list(finish(packed))
+        *done, block_output, tokens_grad = finish(packed, block_output, tokens_grad)
         for k in (6, 9, 16, 19):
             done[k] = done[k].T
         return (block_output.reshape(tokens.shape), tokens_grad.reshape(tokens.shape), *done)

time: 151 us -> 145 us (0.960)
  local copies, waits for them, and re-layouts: 2.57 us -> 0 us
  Pallas kernels: 147 us -> 145 us
    pallas_call x1, Pallas kernels: 145 us -> 139 us  [fused(): pl.pallas_call(fused_kernel, out_shape=outs, in_specs=[anyspec, anyspec]...]
    unnamed x6 -> x0, local copies, waits for them, and re-layouts: 2.57 us -> none
    pallas_call x1, Pallas kernels: 2.51 us -> 5.02 us  [finish(): pl.pallas_call(finish_kernel, out_shape=outs, in_specs=[vm] * len(packed)...]
where the time goes in v7:
time: 145 us
  Pallas kernels  145 us (100%)
    pallas_call x1, Pallas kernels, fused(): pl.pallas_call(fused_kernel, out_shape=outs, in_specs=[anyspec, anyspec]...  139 us
    pallas_call x1, Pallas kernels, finish(): pl.pallas_call(finish_kernel, out_shape=outs, in_specs=[vm] * len(packed)...  5.02 us

profile of v7, /device:TPU:0, one launch (start us, length us, event | category | flops | bytes accessed | tf_op | source)
XLA Modules:
  0.0 145.2 jit_solution(1941814032047244463)
XLA Ops:
  0.7 139.5 %fused.1 = (bf16[1024,512]{1,0:T(8,128)(2,1)}, bf16[1024,512]{1,0:T(8,128)(2,1)}, f32[128,384]{1,0:T(8,128)}, f32[64,256]{1,0:T(8,128)}, f32[128,256]{1,0:T(8,12...) custom-call(bf16[1024,512]{1,0:T(8,128)(2,1)} %bitcast.10, ...), custom_call_target="tpu_custom_call" | custom-call | tf_op jit(solution)/shard_map/fused/pallas_call | solution.py:1629
  140.2 5.0 %finish.1 = (f32[16]{0:T(128)}, f32[128,128]{1,0:T(8,128)}, f32[128,128]{1,0:T(8,128)}, f32[128,128]{1,0:T(8,128)}, f32[32]{0:T(128)}, /*index=5*/f32[32]{0:T(12...) custom-call(f32[128,384]{1,0:T(8,128)} %get-tuple-element.91.grad_mi, ...), custom_call_target="tpu_custom_call" | custom-call | tf_op jit(solution)/shard_map/finish/pallas_call | solution.py:1267

commit v8 on v7

--- a/solution.py
+++ b/solution.py
@@ -50,20 +50,28 @@
     return x * cdf, cdf + (x * e) * (1.0 / math.sqrt(2.0 * math.pi))
 
 
-def gather_rows(tmp, j0, n, D):
-    columns = [
-        jnp.concatenate([tmp[q, pl.ds(j0 + jj, SUB, stride=n), :] for jj in range(16)], axis=0)
-        for q in range(D // LANES)
-    ]
-    return jnp.concatenate(columns, axis=1)
-
-
-def scatter_rows(tmp, j0, n, out):
-    for q in range(out.shape[1] // LANES):
-        for jj in range(16):
-            tmp[q, pl.ds(j0 + jj, SUB, stride=n), :] = out[
-                jj * SUB : (jj + 1) * SUB, q * LANES : (q + 1) * LANES
-            ]
+def reorder(inverse):
+    row = lax.broadcasted_iota(jnp.int32, (LANES, LANES), 0)
+    col = lax.broadcasted_iota(jnp.int32, (LANES, LANES), 1)
+    step = LANES // SUB
+    source = (row % step) * SUB + row // step if inverse else (row % SUB) * step + row // SUB
+    return jnp.where(col == source, 1.0, 0.0).astype(BF16)
+
+
+def tile_rows(i, s, T):
+    step = LANES // SUB
+    return pl.ds(pl.multiple_of(i * step + s * (T // SUB), step), step)
+
+
+def gather_rows(ref, i, order, T):
+    return dot(order, jnp.concatenate([ref[tile_rows(i, s, T), :] for s in range(SUB)], axis=0))
+
+
+def scatter_rows(ref, i, order, out, T):
+    step = LANES // SUB
+    flat = dot(order, out.astype(BF16)).astype(BF16)
+    for s in range(SUB):
+        ref[tile_rows(i, s, T), :] = flat[s * step : (s + 1) * step]
 
 
 LOG2E = 1.0 / math.log(2.0)
@@ -90,21 +98,11 @@
 
 
 def norm_in(refs, T):
-    n = T // SUB
-    tmp, g1 = refs.buf, refs.g1
-    D = g1.shape[1]
-
-    def widen(i):
-        rows = at(i, LANES)
-        wide = refs.tok[rows, :].astype(F32)
-        for q in range(D // LANES):
-            tmp[q, rows, :] = wide[:, q * LANES : (q + 1) * LANES]
-
-    loop(T // LANES, widen)
+    order = reorder(False)
 
     def place(i):
-        x = gather_rows(tmp, i * 16, n, D)
-        y = x * lax.rsqrt(jnp.mean(x * x, axis=-1, keepdims=True) + EPS) * g1[...]
+        x = gather_rows(refs.tok, i, order, T)
+        y = x * lax.rsqrt(jnp.mean(x * x, axis=-1, keepdims=True) + EPS) * refs.g1[...]
         rows = at(i, LANES)
         refs.tok_p[rows, :] = x.astype(BF16)
         refs.min[rows, :] = y.astype(BF16)
@@ -114,20 +112,10 @@
 
 
 def cot_in(refs, T):
-    n = T // SUB
-    tmp = refs.buf
-    D = refs.g1.shape[1]
-
-    def widen(i):
-        rows = at(i, LANES)
-        wide = refs.cot[rows, :].astype(F32)
-        for q in range(D // LANES):
-            tmp[q, rows, :] = wide[:, q * LANES : (q + 1) * LANES]
-
-    loop(T // LANES, widen)
+    order = reorder(False)
 
     def place(i):
-        x = gather_rows(tmp, i * 16, n, D)
+        x = gather_rows(refs.cot, i, order, T)
         rows = at(i, LANES)
         refs.cot_p[rows, :] = x.astype(BF16)
         refs.cot_t[:, rows] = x.T.astype(BF16)
@@ -274,8 +262,7 @@
 
 
 def feed_back(refs, T):
-    n = T // SUB
-    tmp = refs.buf
+    order = reorder(True)
     D = refs.g1.shape[1]
 
     def body(i, total):
@@ -283,7 +270,7 @@
         x = load_planes(refs.resid, rows)
         df = refs.dfe[rows, :]
         out = x + load_planes(refs.oacc, rows, 0, D // LANES)
-        scatter_rows(tmp, i * 16, n, out)
+        scatter_rows(refs.block, i, order, out, T)
         r = lax.rsqrt(jnp.mean(x * x, axis=-1, keepdims=True) + EPS)
         nrm = x * r
         dn = df * refs.g2[...]
@@ -296,13 +283,6 @@
 
     total = lax.fori_loop(0, T // LANES, body, jnp.zeros((SUB, D), F32))
     refs.fgg[...] = jnp.sum(total, axis=0, keepdims=True)
-
-    def emit(i):
-        rows = at(i, LANES)
-        for q in range(D // LANES):
-            refs.block[rows, q * LANES : (q + 1) * LANES] = tmp[q, rows, :].astype(BF16)
-
-    loop(T // LANES, emit)
 
 
 def mixer_back(refs, z, T, hook=None):
@@ -386,8 +366,7 @@
 
 
 def norm_back(refs, T):
-    n = T // SUB
-    tmp = refs.buf
+    order = reorder(True)
     D = refs.g1.shape[1]
 
     def body(i, total):
@@ -399,18 +378,11 @@
         dn = d_in * refs.g1[...]
         mean = jnp.mean(dn * nrm, axis=-1, keepdims=True)
         out = refs.dfe[rows, :] + r * (dn - nrm * mean)
-        scatter_rows(tmp, i * 16, n, out)
+        scatter_rows(refs.tgrad, i, order, out, T)
         return total + (d_in * nrm).reshape(16, SUB, D).sum(axis=0)
 
     total = lax.fori_loop(0, T // LANES, body, jnp.zeros((SUB, D), F32))
     refs.mgg[...] = jnp.sum(total, axis=0, keepdims=True)
-
-    def emit(i):
-        rows = at(i, LANES)
-        for q in range(D // LANES):
-            refs.tgrad[rows, q * LANES : (q + 1) * LANES] = tmp[q, rows, :].astype(BF16)
-
-    loop(T // LANES, emit)
 
 
 class Refs:
@@ -1090,38 +1062,57 @@
     loop(31, one)
 
 
-def gradient_blocks(refs):
-    mix = refs.fin_g[MIX][...]
+def gradient_blocks(refs, start):
     down = refs.fin_g[DOWN][...]
-    return [
-        mix[:, 0:128], mix[:, 128:256], mix[:, 256:384], refs.fin_g[OUT][...], refs.fin_g[UP][...],
+    rest = [
+        refs.fin_g[OUT][...], refs.fin_g[UP][...],
         jnp.concatenate([down[0:64], down[64:128]], axis=1),
     ]
-
-
-def adafactor(refs, p):
-    grads = gradient_blocks(refs)
-    flipped = (False, False, False, True, False, True)
+    if start:
+        return rest
+    mix = refs.fin_g[MIX][...]
+    return [mix[:, 0:128], mix[:, 128:256], mix[:, 256:384]] + rest
+
+
+FLIPPED = (False, False, False, True, False, True)
+
+
+def part_stats(grads, flips):
     row_parts, column_parts, totals = [], [], []
-    for grad, flip in zip(grads, flipped):
+    for grad, flip in zip(grads, flips):
         sq = grad * grad
         down, across = own_row(sq), lane_sum(sq)
         row_parts += cut(down) if flip else [across]
         column_parts += [wide(across)] if flip else cut(down)
         totals.append(jnp.sum(down, axis=1, keepdims=True))
-    refs.rowst[...] = jnp.concatenate(row_parts + [jnp.zeros((6, LANES), F32)], axis=0)
-    refs.colst[...] = jnp.concatenate(column_parts + [jnp.zeros((1, LANES), F32)], axis=0)
-    weights = parameter_blocks(refs)
+    return row_parts, column_parts, totals
+
+
+def adafactor_early(refs, p):
+    rows, columns, totals = part_stats(gradient_blocks(refs, 3), FLIPPED[3:])
+    refs.rowst[...] = jnp.concatenate([jnp.zeros((3, LANES), F32)] + rows + [jnp.zeros((6, LANES), F32)], axis=0)
+    refs.colst[...] = jnp.concatenate(
+        [jnp.zeros((3, LANES), F32)] + columns + [jnp.zeros((1, LANES), F32)], axis=0
+    )
     params = pack_vectors(refs.mg, refs.fbv, refs.ibv, refs.fg)
     squares = [None] * 10
-    for slot, w in zip(MATRIX_SLOTS, weights):
+    for slot, w in zip(MATRIX_SLOTS, parameter_blocks(refs)):
         squares[slot] = total(w * w)
     for slot, start, count in VECTORS:
         squares[slot] = segment(params * params, start, count)
-    rows_old, columns_old = old_rows(refs), old_columns(refs)
+    rows_old = old_rows(refs)
     first = jnp.where(p.i == 0, 1.0, 0.0)
     row_sums = [first * total(jnp.concatenate(rows_old[a:b], axis=0)) for a, b in ROW_PLACES]
-    refs.scal[...] = scalars(totals + squares + row_sums)
+    refs.scal[...] = scalars([0.0] * 3 + totals + squares + row_sums)
+
+
+def adafactor(refs, p):
+    grads = gradient_blocks(refs, 0)
+    flipped = FLIPPED
+    rows, columns, totals = part_stats(grads[0:3], FLIPPED[0:3])
+    refs.rowst[0:3, :] = jnp.concatenate(rows, axis=0)
+    refs.colst[0:3, :] = jnp.concatenate(columns, axis=0)
+    refs.scal[...] += scalars(totals)
     refs.rowin[p.i] = refs.rowst[...]
     refs.colin[p.g] = refs.colst[...]
     refs.scin[p.me] = refs.scal[...]
@@ -1136,6 +1127,9 @@
             refs.colst, refs.colin.at[p.g], refs.col_s.at[k - 1], refs.col_r.at[k - 1], peer
         ).start()
     broadcast_row(refs.scal, refs.scin, refs.sc_s, refs.sc_r, p)
+    weights = parameter_blocks(refs)
+    params = pack_vectors(refs.mg, refs.fbv, refs.ibv, refs.fg)
+    rows_old, columns_old = old_rows(refs), old_columns(refs)
     vec_rows = refs.vin.at[pl.ds(0, 31)]
     rcopy(vec_rows, vec_rows, refs.vex_s, refs.vex_r, p.partner).wait()
     vector_grad = jnp.sum(refs.vin[...].reshape(32, LANES), axis=0, keepdims=True)
@@ -1378,6 +1372,18 @@
         refs.precv[a][place] = v
 
 
+def down_first_send(refs, p, g):
+    def one(z):
+        e = p.turn(z)
+        y, x = g // 2, g % 2
+
+        @pl.when(rs_role(p, g, z) == 1)
+        def _():
+            rs_first_copy(refs, p, DOWN, z, (1 - e) * y + e * x).start()
+
+    loop(4, one)
+
+
 def put_out_grads(refs, p):
     def one(g):
         put_halves(refs, g, dot(refs.fin_t[...], refs.slow[g]))
@@ -1445,6 +1451,7 @@
         merge_up(refs, p, last)
         merge_down(refs, p, last)
         rs_first_send(refs, p, UP, last)
+        down_first_send(refs, p, last)
 
     @pl.when((f % 2 == 0) & (f >= 4))
     def _():
@@ -1511,7 +1518,7 @@
     merge_up(refs, p, 2)
     merge_down(refs, p, 2)
     rs_first_send(refs, p, UP, 2)
-    all_z(lambda z: rs_first_send(refs, p, DOWN, z))
+    down_first_send(refs, p, 2)
     second(refs, p, UP, 1)
     third(refs, p, UP, 3)
     put_out_grads(refs, p)
@@ -1527,8 +1534,6 @@
         def _():
             merge_out(refs, p)
             all_z(lambda z: rs_first_send(refs, p, OUT, z))
-            all_z(lambda z: second(refs, p, DOWN, z))
-            second(refs, p, UP, 2)
 
         @pl.when(n >= 1)
         def _():
@@ -1539,6 +1544,10 @@
         def _():
             second(refs, p, MIX, chunk(n - 2))
 
+        @pl.when(n == 2)
+        def _():
+            all_z(lambda z: third(refs, p, DOWN, z))
+
         @pl.when(n == 3)
         def _():
             third(refs, p, MIX, chunk(0))
@@ -1546,12 +1555,13 @@
     def late(n):
         @pl.when(n == 0)
         def _():
+            second(refs, p, UP, 2)
+            all_z(lambda z: second(refs, p, DOWN, z))
             third(refs, p, UP, 1)
 
         @pl.when(n == 1)
         def _():
             all_z(lambda z: second(refs, p, OUT, z))
-            all_z(lambda z: third(refs, p, DOWN, z))
             third(refs, p, UP, 2)
 
         @pl.when(n == 2)
@@ -1577,6 +1587,7 @@
     vector_exchange(refs, p)
     for a in (UP, DOWN, OUT):
         rs_last(refs, p, a)
+    adafactor_early(refs, p)
     third(refs, p, MIX, chunk(2))
     second(refs, p, MIX, chunk(3))
     third(refs, p, MIX, chunk(3))

time: 145 us -> 138 us (0.952)
  Pallas kernels: 145 us -> 138 us
    pallas_call x1, Pallas kernels: 139 us -> 133 us  [fused(): pl.pallas_call(fused_kernel, out_shape=outs, in_specs=[anyspec, anyspec]...]
where the time goes in v8:
time: 138 us
  Pallas kernels  138 us (100%)
    pallas_call x1, Pallas kernels, fused(): pl.pallas_call(fused_kernel, out_shape=outs, in_specs=[anyspec, anyspec]...  133 us
    pallas_call x1, Pallas kernels, finish(): pl.pallas_call(finish_kernel, out_shape=outs, in_specs=[vm] * len(packed)...  5.02 us

profile of v8, /device:TPU:0, one launch (start us, length us, event | category | flops | bytes accessed | tf_op | source)
XLA Modules:
  0.0 138.3 jit_solution(5603026711410826425)
XLA Ops:
  0.7 132.5 %fused.1 = (bf16[1024,512]{1,0:T(8,128)(2,1)}, bf16[1024,512]{1,0:T(8,128)(2,1)}, f32[128,384]{1,0:T(8,128)}, f32[64,256]{1,0:T(8,128)}, f32[128,256]{1,0:T(8,12...) custom-call(bf16[1024,512]{1,0:T(8,128)(2,1)} %bitcast.10, ...), custom_call_target="tpu_custom_call" | custom-call | tf_op jit(solution)/shard_map/fused/pallas_call | solution.py:1640
  133.2 5.0 %finish.1 = (f32[16]{0:T(128)}, f32[128,128]{1,0:T(8,128)}, f32[128,128]{1,0:T(8,128)}, f32[128,128]{1,0:T(8,128)}, f32[32]{0:T(128)}, /*index=5*/f32[32]{0:T(12...) custom-call(f32[128,384]{1,0:T(8,128)} %get-tuple-element.91.grad_mi, ...), custom_call_target="tpu_custom_call" | custom-call | tf_op jit(solution)/shard_map/finish/pallas_call | solution.py:1261

commit v9 on v8

--- a/solution.py
+++ b/solution.py
@@ -232,20 +232,20 @@
     size = 256
     tiles = T // size
 
+    up, back = {}, {}
+
     def project(i):
         rows = slice(i * size, (i + 1) * size)
-        store_planes(refs.buf, rows, dot(refs.fin[rows, :], wup[f]))
-        store_planes(refs.buf, rows, dot(refs.cot_p[rows, :], wdt[f]), 2)
+        up[i] = dot(refs.fin[rows, :], wup[f])
+        back[i] = dot(refs.cot_p[rows, :], wdt[f])
 
     def activate(i):
         for k in range(size // 32):
+            part = slice(k * 32, (k + 1) * 32)
             rows = slice(i * size + k * 32, i * size + (k + 1) * 32)
-            for q in range(C // LANES):
-                act, slope = gelu_parts(refs.buf[q, rows, :])
-                lanes = slice(q * LANES, (q + 1) * LANES)
-                refs.dpre[rows, lanes] = act.astype(BF16)
-                lanes = slice(C + q * LANES, C + (q + 1) * LANES)
-                refs.dpre[rows, lanes] = (refs.buf[2 + q, rows, :] * slope).astype(BF16)
+            act, slope = gelu_parts(up[i][part])
+            refs.dpre[rows, 0:C] = act.astype(BF16)
+            refs.dpre[rows, C : 2 * C] = (back[i][part] * slope).astype(BF16)
 
     def add(i):
         rows = slice(i * size, (i + 1) * size)
@@ -510,14 +510,17 @@
         return (t // 8, t % 8)
 
 
-def entry_barrier(place):
+def entry_signal(place):
     barrier = pltpu.get_barrier_semaphore()
 
     def greet(k):
         pl.semaphore_signal(barrier, inc=1, device_id=place.other(k + 1), device_id_type=MESH)
 
     loop(31, greet)
-    pl.semaphore_wait(barrier, 31)
+
+
+def entry_wait():
+    pl.semaphore_wait(pltpu.get_barrier_semaphore(), 31)
 
 
 def spread(values, start, count, total):
@@ -682,8 +685,7 @@
         for k in range(2):
             down_pair(refs, p, z, phase, k, p.c).start()
     else:
-        for k in range(2):
-            down_pair(refs, p, z, phase, k, 1 - p.c).wait_recv()
+        down_pair(refs, p, z, phase, 0 if kind == "d" else 1, 1 - p.c).wait_recv()
 
 
 def gather_drain(refs, p):
@@ -740,7 +742,7 @@
     refs.vecs[p.me] = row
     for c in local:
         c.wait()
-    entry_barrier(p)
+    entry_wait()
 
     def vector(k):
         rcopy(refs.vstage, refs.vecs.at[p.me], refs.vec_s, refs.vec_r, p.other(k + 1)).start()
@@ -749,7 +751,8 @@
         near_send(refs, p, a, p.z)
     up_own(refs, p, 0)
     down_step(refs, p, "n", 0, 0)
-    loop(31, vector)
+    for k in range(31):
+        vector(k)
     for a in FIRST:
         line_send(refs, p, a)
     inner = (p.z + 1) // 2 % 2
@@ -1037,7 +1040,8 @@
     def one(k):
         rcopy(src, box.at[p.me], send, recv, p.other(k + 1)).start()
 
-    loop(31, one)
+    for k in range(31):
+        one(k)
 
 
 def settle_row(box, send, recv, p):
@@ -1059,7 +1063,8 @@
         t = (p.me + k + 1) % 32
         rcopy(refs.vout.at[t], refs.vin.at[p.me], refs.vex_s, refs.vex_r, p.other(k + 1)).start()
 
-    loop(31, one)
+    for k in range(31):
+        one(k)
 
 
 def gradient_blocks(refs, start):
@@ -1467,6 +1472,7 @@
     refs.fin_grad = refs.fin_g
     T, D = refs.tok_p.shape
     p = Place()
+    entry_signal(p)
     load = pltpu.make_async_copy(refs.cot_in, refs.io, refs.io_s)
     load.start()
     gather_start(refs, p)
@@ -1483,14 +1489,22 @@
     up_own(refs, p, 1)
     gather_hook(refs, p, "Wd0 Wd1 Wd2 Wd3 Un1 Un2 Dn10 Dn11 Dn12 Dn13")
     mix_out(refs, T)
-    gather_hook(refs, p, "Ud0 Ud3 Dd00 Dd01 Dd02 Dd03")
+    gather_hook(refs, p, "Ud0 Dd00 Dd01 Dd02 Dd03")
     clear(refs.oacc, T)
     refs.dfe[...] = jnp.zeros_like(refs.dfe)
 
     def feed_step(f):
+        @pl.when(f == 2)
+        def _():
+            gather_hook(refs, p, "Ud3 De00 De01 De02 De03")
+
         @pl.when(f == 4)
         def _():
-            gather_hook(refs, p, "Ud1 Ud2 Dd10 Dd11 Dd12 Dd13")
+            gather_hook(refs, p, "Ud1 Dd10 Dd11 Dd12 Dd13")
+
+        @pl.when(f == 6)
+        def _():
+            gather_hook(refs, p, "Ud2 De10 De11 De12 De13")
 
         feed(refs, feed_order(f // 2) * 2 + f % 2, T)
 

time: 138 us -> 137 us (level)
  Pallas kernels: 138 us -> 136 us
    pallas_call x1, Pallas kernels: 133 us -> 131 us  [fused(): pl.pallas_call(fused_kernel, out_shape=outs, in_specs=[anyspec, anyspec]...]
where the time goes in v9:
time: 137 us; the launch traced here: 136 us
  Pallas kernels  136 us (99%)
    pallas_call x1, Pallas kernels, fused(): pl.pallas_call(fused_kernel, out_shape=outs, in_specs=[anyspec, anyspec]...  131 us
    pallas_call x1, Pallas kernels, finish(): pl.pallas_call(finish_kernel, out_shape=outs, in_specs=[vm] * len(packed)...  5.02 us

profile of v9, /device:TPU:0, one launch (start us, length us, event | category | flops | bytes accessed | tf_op | source)
XLA Modules:
  0.0 136.4 jit_solution(9770270079612684684)
XLA Ops:
  0.7 130.7 %fused.1 = (bf16[1024,512]{1,0:T(8,128)(2,1)}, bf16[1024,512]{1,0:T(8,128)(2,1)}, f32[128,384]{1,0:T(8,128)}, f32[64,256]{1,0:T(8,128)}, f32[128,256]{1,0:T(8,12...) custom-call(bf16[1024,512]{1,0:T(8,128)(2,1)} %bitcast.10, ...), custom_call_target="tpu_custom_call" | custom-call | tf_op jit(solution)/shard_map/fused/pallas_call | solution.py:1654
  131.4 5.0 %finish.1 = (f32[16]{0:T(128)}, f32[128,128]{1,0:T(8,128)}, f32[128,128]{1,0:T(8,128)}, f32[128,128]{1,0:T(8,128)}, f32[32]{0:T(128)}, /*index=5*/f32[32]{0:T(12...) custom-call(f32[128,384]{1,0:T(8,128)} %get-tuple-element.91.grad_mi, ...), custom_call_target="tpu_custom_call" | custom-call | tf_op jit(solution)/shard_map/finish/pallas_call | solution.py:1266

commit v10 on v9

--- a/solution.py
+++ b/solution.py
@@ -516,7 +516,8 @@
     def greet(k):
         pl.semaphore_signal(barrier, inc=1, device_id=place.other(k + 1), device_id_type=MESH)
 
-    loop(31, greet)
+    for k in range(31):
+        greet(k)
 
 
 def entry_wait():
@@ -1598,12 +1599,12 @@
     norm_back(refs, T)
     store = pltpu.make_async_copy(refs.io, refs.tgrad_out, refs.io_s)
     store.start()
+    second(refs, p, MIX, chunk(3))
+    third(refs, p, MIX, chunk(2))
     vector_exchange(refs, p)
     for a in (UP, DOWN, OUT):
         rs_last(refs, p, a)
     adafactor_early(refs, p)
-    third(refs, p, MIX, chunk(2))
-    second(refs, p, MIX, chunk(3))
     third(refs, p, MIX, chunk(3))
     rs_last(refs, p, MIX)
     rs_drain(refs, p)

time: 137 us -> 136 us (level)
  no operation moved by 1% of the time
where the time goes in v10:
time: 136 us; the launch traced here: 135 us
  Pallas kernels  135 us (99%)
    pallas_call x1, Pallas kernels, fused(): pl.pallas_call(fused_kernel, out_shape=outs, in_specs=[anyspec, anyspec]...  130 us
    pallas_call x1, Pallas kernels, finish(): pl.pallas_call(finish_kernel, out_shape=outs, in_specs=[vm] * len(packed)...  5.02 us

profile of v10, /device:TPU:0, one launch (start us, length us, event | category | flops | bytes accessed | tf_op | source)
XLA Modules:
  0.0 135.4 jit_solution(15002736138944556665)
XLA Ops:
  0.7 129.7 %fused.1 = (bf16[1024,512]{1,0:T(8,128)(2,1)}, bf16[1024,512]{1,0:T(8,128)(2,1)}, f32[128,384]{1,0:T(8,128)}, f32[64,256]{1,0:T(8,128)}, f32[128,256]{1,0:T(8,12...) custom-call(bf16[1024,512]{1,0:T(8,128)(2,1)} %bitcast.10, ...), custom_call_target="tpu_custom_call" | custom-call | tf_op jit(solution)/shard_map/fused/pallas_call | solution.py:1655
  130.4 5.0 %finish.1 = (f32[16]{0:T(128)}, f32[128,128]{1,0:T(8,128)}, f32[128,128]{1,0:T(8,128)}, f32[128,128]{1,0:T(8,128)}, f32[32]{0:T(128)}, /*index=5*/f32[32]{0:T(12...) custom-call(f32[128,384]{1,0:T(8,128)} %get-tuple-element.91.grad_mi, ...), custom_call_target="tpu_custom_call" | custom-call | tf_op jit(solution)/shard_map/finish/pallas_call | solution.py:1267
